TPU v7x, 32 devices: a whole 2x2x4 slice. The times are simulated.
32 devices in a mesh: section: 2 (over x), expert: 16 (over z, y, core).
Axes of the slice: x: 2, y: 2, z: 4, core: 2. Of those that a mesh axis runs over, the one named last changes fastest.
Arguments:
- hidden_in: bfloat16 [2, 128, 3584], P(None, 'expert'), may hold values from -6 to 6
- layer_gain: float32 [2, 3584], P('section'), may hold values from 0.25 to 1.75
- router: bfloat16 [2, 3584, 4], P('section'), may hold values from -0.09375 to 0.09375
- w_gate: bfloat16 [2, 3584, 8192], P('section', None, 'expert'), may hold values from -0.09375 to 0.09375
- w_up: bfloat16 [2, 3584, 8192], P('section', None, 'expert'), may hold values from -0.09375 to 0.09375
- w_down: bfloat16 [2, 8192, 3584], P('section', 'expert'), may hold values from -0.125 to 0.125
- final_gain: float32 [3584], replicated, may hold values from 0.25 to 1.75
- head: bfloat16 [8192, 3584], P(('section', 'expert')), may hold values from -18.775102 to 18.775102
- routing: int32 [2, 2, 128, 2], P('section', None, 'expert'), may hold values from 0 to 3, all different within a row; in each aligned block of 8 rows (0 to 7, 8 to 15, ..., all dimensions but the last counted through in order) at most 4 rows name the same one
- targets: int32 [2, 128], replicated, may hold values from 0 to 8191
- seq_ids: int32 [2, 128], replicated, may hold values from 0 to 3, never falling along the last dimension, each value on 1 to 64 neighbouring positions
Outputs:
- token_logprob: float32 [2, 128], P(None, 'expert')
- seq_mean: float32 [2, 4], replicated
Inputs may be any that keep to these rules, and one draw needn't show every extreme that they name: `routing`: in each aligned block of 8 tokens (the tokens of one device) a token's 2 experts differ and no expert is named by more than 4 tokens; some expert is named by exactly 4. `seq_ids`: ids never fall along a micro-batch's tokens; each of the 4 ids occurs on 1 to 64 tokens, one on exactly 64.
All inputs are finite; a program needn't handle non-finite values.
Results may differ from a plain program's by a relative error of at most 0.014.
Values may be sent and summed in bfloat16 or wider, within the bound.
No kernel may reach another device: no remote copies, remote signals or barrier semaphores. Data moves between devices by JAX's collectives and lax.ppermute only.
A program may use at most 64 MiB of HBM per device.

v0:
```python
import jax
import jax.numpy as jnp
from jax import lax
from jax.sharding import PartitionSpec as P

SEQS = 4


def shifted(shard, axis, by):
    size = lax.axis_size(axis)
    pairs = [(i, i + by) for i in range(size) if 0 <= i + by < size]
    return lax.ppermute(shard, axis, pairs)


def broadcast(block, axis, holder):
    block = jnp.where(lax.axis_index(axis) == holder, block, jnp.zeros_like(block))
    return lax.psum(block, axis)


def rms_scale(states, gain):
    values = states.astype(jnp.float32)
    factor = lax.rsqrt(jnp.mean(values * values, -1, keepdims=True) + 1e-06)
    return values * factor * gain


def body(
    hidden_in, layer_gain, router, w_gate, w_up, w_down, final_gain, head, routing, targets, seq_ids
):
    micro_count, tok_count, model_width = hidden_in.shape
    expert_count = router.shape[2]
    top_count = routing.shape[3]
    sections = lax.axis_size("section")
    members = lax.axis_size("expert")
    section_pos = lax.axis_index("section")
    member_pos = lax.axis_index("expert")
    split_count = members // expert_count
    capacity = min(tok_count, 9 * tok_count * top_count // (8 * expert_count))
    tick_count = micro_count + sections - 1

    def expert_rows(incoming):
        sources, slot_count, width_in = incoming.shape
        flat_rows = incoming.reshape(sources * slot_count, width_in)
        gate_val = jnp.dot(flat_rows, w_gate[0], preferred_element_type=jnp.float32)
        up_val = jnp.dot(flat_rows, w_up[0], preferred_element_type=jnp.float32)
        inner = (jax.nn.silu(gate_val) * up_val).astype(jnp.bfloat16)
        partial_value = jnp.dot(inner, w_down[0], preferred_element_type=jnp.float32).astype(
            jnp.bfloat16
        )
        return lax.all_to_all(
            partial_value.reshape(sources, slot_count, width_in),
            "expert",
            split_axis=0,
            concat_axis=0,
            tiled=True,
        )

    def expert_layer(states, micro_pos):
        route_ids = lax.dynamic_index_in_dim(routing[0], micro_pos, 0, keepdims=False)
        normed = rms_scale(states, layer_gain[0]).astype(jnp.bfloat16)
        logits = jnp.dot(normed, router[0], preferred_element_type=jnp.float32)
        chosen = route_ids[:, :, None] == jnp.arange(expert_count, dtype=jnp.int32)[None, None, :]
        affinity = jax.nn.sigmoid(jnp.sum(jnp.where(chosen, logits[:, None, :], 0.0), -1))
        weight = affinity / jnp.sum(affinity, -1, keepdims=True)
        flags = chosen.reshape(tok_count * top_count, expert_count).astype(jnp.int32)
        ranks = jnp.cumsum(flags, 0) - flags
        slot_ids = jnp.sum(ranks * flags, -1).reshape(tok_count, top_count)
        destination = route_ids * capacity + slot_ids
        places = jnp.arange(expert_count * capacity, dtype=jnp.int32)
        table = jnp.any(places[:, None, None] == destination[None], -1).astype(jnp.bfloat16)
        packed = jnp.dot(table, normed, preferred_element_type=jnp.float32).astype(jnp.bfloat16)
        outgoing = jnp.broadcast_to(
            packed.reshape(expert_count, 1, capacity, model_width),
            (expert_count, split_count, capacity, model_width),
        )
        outgoing = outgoing.reshape(members, capacity, model_width)
        returned = expert_rows(
            lax.all_to_all(outgoing, "expert", split_axis=0, concat_axis=0, tiled=True)
        )
        summed = jnp.sum(
            returned.reshape(expert_count, split_count, capacity, model_width).astype(jnp.float32),
            1,
        )
        summed = summed.reshape(expert_count * capacity, model_width)
        picked = summed[destination]
        mixed = jnp.sum(weight[:, :, None] * picked, 1)
        return (states.astype(jnp.float32) + 2.5 * mixed).astype(jnp.bfloat16)

    def advance(step, carry):
        arrived, record = carry
        entering = lax.dynamic_index_in_dim(
            hidden_in, jnp.minimum(step, micro_count - 1), 0, keepdims=False
        )
        states = jnp.where(section_pos == 0, entering, arrived)
        micro_pos = jnp.clip(step - section_pos, 0, micro_count - 1)
        result = expert_layer(states, micro_pos)
        finished = step - (sections - 1)
        record_pos = jnp.clip(finished, 0, micro_count - 1)
        keeping = (finished >= 0) & (section_pos == sections - 1)
        previous = lax.dynamic_index_in_dim(record, record_pos, 0, keepdims=False)
        record = lax.dynamic_update_index_in_dim(
            record, jnp.where(keeping, result, previous), record_pos, 0
        )
        arrived = shifted(result, "section", 1)
        return (arrived, record)

    start_rows = jnp.zeros((tok_count, model_width), jnp.bfloat16)
    start_record = jnp.zeros((micro_count, tok_count, model_width), jnp.bfloat16)
    arrived, record = lax.fori_loop(0, tick_count, advance, (start_rows, start_record))
    shared = broadcast(record, "section", sections - 1)
    normed = rms_scale(lax.all_gather(shared, "expert", axis=1, tiled=True), final_gain).astype(
        jnp.bfloat16
    )
    logits = jnp.einsum("mrd,vd->mrv", normed, head, preferred_element_type=jnp.float32)
    voc_count = head.shape[0]
    vocab_start = (section_pos * members + member_pos) * voc_count
    vocab_ids = vocab_start + jnp.arange(voc_count, dtype=jnp.int32)
    target_hit = targets[:, :, None] == vocab_ids[None, None, :]
    target_part = jnp.sum(jnp.where(target_hit, logits, 0.0), -1)
    local_max = jnp.max(logits, -1)
    peak = lax.pmax(local_max, ("section", "expert"))
    local_sum = jnp.sum(jnp.exp(logits - peak[..., None]), -1)
    total, target_logit = lax.psum((local_sum, target_part), ("section", "expert"))
    logprob = target_logit - (peak + jnp.log(total))
    token_part = lax.dynamic_slice_in_dim(logprob, member_pos * tok_count, tok_count, 1)
    member = seq_ids[:, :, None] == jnp.arange(SEQS, dtype=jnp.int32)[None, None, :]
    sums = jnp.sum(jnp.where(member, logprob[..., None], 0.0), 1)
    counts = jnp.sum(member.astype(jnp.float32), 1)
    return (token_part, sums / counts)


def solution(mesh):
    return jax.shard_map(
        body,
        mesh=mesh,
        in_specs=(
            P(None, "expert", None),
            P("section", None),
            P("section", None, None),
            P("section", None, "expert"),
            P("section", None, "expert"),
            P("section", "expert", None),
            P(),
            P(("section", "expert"), None),
            P("section", None, "expert", None),
            P(),
            P(),
        ),
        out_specs=(P(None, "expert"), P()),
        check_vma=False,
    )
```

profile of v0, /device:TPU:0, one launch (start us, length us, event | category | flops | bytes accessed | tf_op | source)
XLA Modules:
  0.0 332.3 jit_solution(14966221587501759313)
XLA Ops:
  7.3 167.9 %while.17 = (s32[]{:T(128)}, bf16[8,3584]{1,0:T(8,128)(2,1)S(1)}, bf16[2,8,3584]{2,1,0:T(8,128)(2,1)S(1)}, pred[]{:T(512)}, bf16[2,8,3584]{2,1,0:T(8,128)(2,1)},...) while((s32[]{:T(128)}, bf16[8,3584]{1,0:T(8,128)(2,1)S(1)}, ...), condition=%wide.region_9.10_spmd, body=%wide.region_0.9_spmd.sunk | while | flops 707251328 | bytes 21631636 | solution.py:108
  7.3 0.8 constant_dynamic-slice_fusion.6
  8.7 0.7 multiply_add_fusion.2
  9.5 1.0 fusion.70
  10.5 0.8 reduce.2
  11.5 0.9 broadcast_in_dim.134
  12.4 7.4 %all-to-all-start = ((bf16[16,4,3584]{2,1,0:T(4,128)(2,1)}), bf16[16,4,3584]{2,1,0:T(4,128)(2,1)S(1)}, u32[]{:S(2)}, u32[]{:S(2)}) async-start(bf16[16,4,3584]{2,1,0:T(4,128)(2,1)} %bitcast.77), calls=%async_computation | async-start | bytes 917504 | tf_op jit(solution)/shard_map/while/body/eval_jaxpr/all_to_all | solution.py:77
  21.5 0.9 fusion.72
  22.5 10.5 %all-to-all-done = bf16[16,4,3584]{2,1,0:T(4,128)(2,1)S(1)} async-done(((bf16[16,4,3584]{2,1,0:T(4,128)(2,1)}), bf16[16,4,3584]{2,1,0:T(4,128)(2,1)S(1)}, u32[]{:S(2)}, u32[]{:S(2)}) %all-to-all-start) | async-done | bytes 458784 | tf_op jit(solution)/shard_map/while/body/eval_jaxpr/all_to_all | solution.py:77
  33.2 2.8 fusion.71
  35.9 4.6 %convolution_convert_fusion.5 = bf16[64,3584]{1,0:T(8,128)(2,1)S(1)} fusion(bf16[1,512,3584]{2,1,0:T(8,128)(2,1)} %get-tuple-element.450, bf16[64,3584]{1,0:T(8,128)(2,1)S(1)} %reshape.218, bf16[1,3584,512]{2,1,0:T(8,128)(2,1)} %get-tuple-element.449, f32[64,512]{1,0:T(8,128)S(1)} %fusion.71), kind=kOutput, calls=%fused_computation.1.clone.1 | convolution fusion | flops 470188032 | bytes 8388608 | tf_op jit(solution)/shard_map/while/body/eval_jaxpr/dot_general | solution.py:46
  40.6 0.9 reshape.219
  41.4 3.8 %all-to-all-start.1 = ((bf16[16,4,3584]{2,1,0:T(4,128)(2,1)}), bf16[16,4,3584]{2,1,0:T(4,128)(2,1)S(1)}, u32[]{:S(2)}, u32[]{:S(2)}) async-start(bf16[16,4,3584]{2,1,0:T(4,128)(2,1)} %reshape.219), calls=%async_computation.1 | async-start | bytes 917504 | tf_op jit(solution)/shard_map/while/body/eval_jaxpr/all_to_all | solution.py:49
  45.4 13.1 %all-to-all-done.1 = bf16[16,4,3584]{2,1,0:T(4,128)(2,1)S(1)} async-done(((bf16[16,4,3584]{2,1,0:T(4,128)(2,1)}), bf16[16,4,3584]{2,1,0:T(4,128)(2,1)S(1)}, u32[]{:S(2)}, u32[]{:S(2)}) %all-to-all-start.1) | async-done | bytes 458784 | tf_op jit(solution)/shard_map/while/body/eval_jaxpr/all_to_all | solution.py:49
  59.9 3.4 %collective-permute-start = (bf16[8,3584]{1,0:T(8,128)(2,1)S(1)}, bf16[8,3584]{1,0:T(8,128)(2,1)S(1)}, u32[]{:S(2)}, u32[]{:S(2)}) collective-permute-start(bf16[8,3584]{1,0:T(8,128)(2,1)S(1)} %get-tuple-element.401), channel_id=1, source_target_pairs={{0,16},{1,17},{2,18},{3,19},{4,20},{5,21},{6,22},{7,23},{8,24},{9,... | collective-permute-start | bytes 172040 | tf_op jit(solution)/shard_map/while/body/eval_jaxpr/ppermute | solution.py:12
  63.4 1.8 collective-permute-done
  67.2 1.0 fusion.70
  68.2 0.8 reduce.2
  69.3 0.9 broadcast_in_dim.134
  70.1 3.8 %all-to-all-start = ((bf16[16,4,3584]{2,1,0:T(4,128)(2,1)}), bf16[16,4,3584]{2,1,0:T(4,128)(2,1)S(1)}, u32[]{:S(2)}, u32[]{:S(2)}) async-start(bf16[16,4,3584]{2,1,0:T(4,128)(2,1)} %bitcast.77), calls=%async_computation | async-start | bytes 917504 | tf_op jit(solution)/shard_map/while/body/eval_jaxpr/all_to_all | solution.py:77
  75.6 0.9 fusion.72
  76.6 10.5 %all-to-all-done = bf16[16,4,3584]{2,1,0:T(4,128)(2,1)S(1)} async-done(((bf16[16,4,3584]{2,1,0:T(4,128)(2,1)}), bf16[16,4,3584]{2,1,0:T(4,128)(2,1)S(1)}, u32[]{:S(2)}, u32[]{:S(2)}) %all-to-all-start) | async-done | bytes 458784 | tf_op jit(solution)/shard_map/while/body/eval_jaxpr/all_to_all | solution.py:77
  87.3 2.8 fusion.71
  90.1 4.6 %convolution_convert_fusion.5 = bf16[64,3584]{1,0:T(8,128)(2,1)S(1)} fusion(bf16[1,512,3584]{2,1,0:T(8,128)(2,1)} %get-tuple-element.450, bf16[64,3584]{1,0:T(8,128)(2,1)S(1)} %reshape.218, bf16[1,3584,512]{2,1,0:T(8,128)(2,1)} %get-tuple-element.449, f32[64,512]{1,0:T(8,128)S(1)} %fusion.71), kind=kOutput, calls=%fused_computation.1.clone.1 | convolution fusion | flops 470188032 | bytes 8388608 | tf_op jit(solution)/shard_map/while/body/eval_jaxpr/dot_general | solution.py:46
  94.7 0.9 reshape.219
  95.6 3.8 %all-to-all-start.1 = ((bf16[16,4,3584]{2,1,0:T(4,128)(2,1)}), bf16[16,4,3584]{2,1,0:T(4,128)(2,1)S(1)}, u32[]{:S(2)}, u32[]{:S(2)}) async-start(bf16[16,4,3584]{2,1,0:T(4,128)(2,1)} %reshape.219), calls=%async_computation.1 | async-start | bytes 917504 | tf_op jit(solution)/shard_map/while/body/eval_jaxpr/all_to_all | solution.py:49
  99.5 13.1 %all-to-all-done.1 = bf16[16,4,3584]{2,1,0:T(4,128)(2,1)S(1)} async-done(((bf16[16,4,3584]{2,1,0:T(4,128)(2,1)}), bf16[16,4,3584]{2,1,0:T(4,128)(2,1)S(1)}, u32[]{:S(2)}, u32[]{:S(2)}) %all-to-all-start.1) | async-done | bytes 458784 | tf_op jit(solution)/shard_map/while/body/eval_jaxpr/all_to_all | solution.py:49
  114.1 4.3 %collective-permute-start = (bf16[8,3584]{1,0:T(8,128)(2,1)S(1)}, bf16[8,3584]{1,0:T(8,128)(2,1)S(1)}, u32[]{:S(2)}, u32[]{:S(2)}) collective-permute-start(bf16[8,3584]{1,0:T(8,128)(2,1)S(1)} %get-tuple-element.401), channel_id=1, source_target_pairs={{0,16},{1,17},{2,18},{3,19},{4,20},{5,21},{6,22},{7,23},{8,24},{9,... | collective-permute-start | bytes 172040 | tf_op jit(solution)/shard_map/while/body/eval_jaxpr/ppermute | solution.py:12
  118.4 1.8 collective-permute-done
  122.3 1.0 fusion.70
  123.2 0.8 reduce.2
  124.3 0.9 broadcast_in_dim.134
  125.2 3.8 %all-to-all-start = ((bf16[16,4,3584]{2,1,0:T(4,128)(2,1)}), bf16[16,4,3584]{2,1,0:T(4,128)(2,1)S(1)}, u32[]{:S(2)}, u32[]{:S(2)}) async-start(bf16[16,4,3584]{2,1,0:T(4,128)(2,1)} %bitcast.77), calls=%async_computation | async-start | bytes 917504 | tf_op jit(solution)/shard_map/while/body/eval_jaxpr/all_to_all | solution.py:77
  130.7 0.9 fusion.72
  131.7 10.5 %all-to-all-done = bf16[16,4,3584]{2,1,0:T(4,128)(2,1)S(1)} async-done(((bf16[16,4,3584]{2,1,0:T(4,128)(2,1)}), bf16[16,4,3584]{2,1,0:T(4,128)(2,1)S(1)}, u32[]{:S(2)}, u32[]{:S(2)}) %all-to-all-start) | async-done | bytes 458784 | tf_op jit(solution)/shard_map/while/body/eval_jaxpr/all_to_all | solution.py:77
  142.3 2.8 fusion.71
  145.1 4.6 %convolution_convert_fusion.5 = bf16[64,3584]{1,0:T(8,128)(2,1)S(1)} fusion(bf16[1,512,3584]{2,1,0:T(8,128)(2,1)} %get-tuple-element.450, bf16[64,3584]{1,0:T(8,128)(2,1)S(1)} %reshape.218, bf16[1,3584,512]{2,1,0:T(8,128)(2,1)} %get-tuple-element.449, f32[64,512]{1,0:T(8,128)S(1)} %fusion.71), kind=kOutput, calls=%fused_computation.1.clone.1 | convolution fusion | flops 470188032 | bytes 8388608 | tf_op jit(solution)/shard_map/while/body/eval_jaxpr/dot_general | solution.py:46
  149.7 0.9 reshape.219
  150.6 3.8 %all-to-all-start.1 = ((bf16[16,4,3584]{2,1,0:T(4,128)(2,1)}), bf16[16,4,3584]{2,1,0:T(4,128)(2,1)S(1)}, u32[]{:S(2)}, u32[]{:S(2)}) async-start(bf16[16,4,3584]{2,1,0:T(4,128)(2,1)} %reshape.219), calls=%async_computation.1 | async-start | bytes 917504 | tf_op jit(solution)/shard_map/while/body/eval_jaxpr/all_to_all | solution.py:49
  154.5 13.1 %all-to-all-done.1 = bf16[16,4,3584]{2,1,0:T(4,128)(2,1)S(1)} async-done(((bf16[16,4,3584]{2,1,0:T(4,128)(2,1)}), bf16[16,4,3584]{2,1,0:T(4,128)(2,1)S(1)}, u32[]{:S(2)}, u32[]{:S(2)}) %all-to-all-start.1) | async-done | bytes 458784 | tf_op jit(solution)/shard_map/while/body/eval_jaxpr/all_to_all | solution.py:49
  169.1 4.3 %collective-permute-start = (bf16[8,3584]{1,0:T(8,128)(2,1)S(1)}, bf16[8,3584]{1,0:T(8,128)(2,1)S(1)}, u32[]{:S(2)}, u32[]{:S(2)}) collective-permute-start(bf16[8,3584]{1,0:T(8,128)(2,1)S(1)} %get-tuple-element.401), channel_id=1, source_target_pairs={{0,16},{1,17},{2,18},{3,19},{4,20},{5,21},{6,22},{7,23},{8,24},{9,... | collective-permute-start | bytes 172040 | tf_op jit(solution)/shard_map/while/body/eval_jaxpr/ppermute | solution.py:12
  173.4 1.8 collective-permute-done
  175.9 21.4 %all-reduce.3.cloned.1.call-done = bf16[2,8,3584]{2,1,0:T(8,128)(2,1)} async-done(((bf16[2,8,3584]{2,1,0:T(8,128)(2,1)}), bf16[2,8,3584]{2,1,0:T(8,128)(2,1)}) %all-reduce.3.cloned.1.call-update) | async-done | bytes 114704 | tf_op jit(solution)/shard_map/psum | solution.py:17
  197.5 42.9 %all-gather.2.cloned.1.call-done = bf16[2,128,3584]{2,1,0:T(8,128)(2,1)} async-done(((bf16[2,8,3584]{2,1,0:T(8,128)(2,1)}), bf16[2,128,3584]{2,1,0:T(8,128)(2,1)}) %all-gather.2.cloned.1.call-update) | async-done | bytes 1835024 | tf_op jit(solution)/shard_map/all_gather | solution.py:110
  240.4 1.9 fusion.30
  242.4 2.3 fusion.39
  244.6 38.4 %pmax.7 = f32[2,128]{1,0:T(2,128)S(1)} all-reduce(f32[2,128]{1,0:T(2,128)S(1)} %get-tuple-element.314), channel_id=1, replica_groups=mesh['section'=2,'expert'=16] {'section','expert'}, use_global_device_ids=true, to_apply=%region_15.16 | all-reduce | flops 256 | bytes 2048 | tf_op jit(solution)/shard_map/pmax | solution.py:120
  283.3 40.9 %all-reduce = (f32[2,128]{1,0:T(2,128)S(1)}, f32[2,128]{1,0:T(2,128)S(1)}) all-reduce(f32[2,128]{1,0:T(2,128)S(1)} %get-tuple-element.279, f32[2,128]{1,0:T(2,128)S(1)} %get-tuple-element.278), channel_id=1, replica_groups=mesh['section'=2,'expert'=16] {'section','expert'}, use_global_device_ids=true, to_apply=%region_13.14 | all-reduce | flops 512 | bytes 4096 | tf_op jit(solution)/shard_map/psum | solution.py:122
  (116 shorter events, 18.3 us)
Async XLA Ops:
  7.2 235.2 %copy-start = (bf16[256,3584]{1,0:T(8,128)(2,1)S(1)}, bf16[256,3584]{1,0:T(8,128)(2,1)}, u32[]{:S(2)}) copy-start(bf16[256,3584]{1,0:T(8,128)(2,1)} %param.20) | copy-start | bytes 5505028
  7.2 190.2 %all-reduce.3.cloned.1.call-start = ((), (), s32[]{:S(2)}) async-start(), calls=%async_computation.2 | async-start | bytes 229376 | tf_op jit(solution)/shard_map/psum | solution.py:17
  7.3 235.1 %copy-start.3 = (f32[3584]{0:T(1024)S(1)}, f32[3584]{0:T(1024)}, u32[]{:S(2)}) copy-start(f32[3584]{0:T(1024)} %param.19) | copy-start | bytes 43012
  12.4 20.6 %all-to-all-start = ((bf16[16,4,3584]{2,1,0:T(4,128)(2,1)}), bf16[16,4,3584]{2,1,0:T(4,128)(2,1)S(1)}, u32[]{:S(2)}, u32[]{:S(2)}) async-start(bf16[16,4,3584]{2,1,0:T(4,128)(2,1)} %bitcast.77), calls=%async_computation | async-start | bytes 917504 | tf_op jit(solution)/shard_map/while/body/eval_jaxpr/all_to_all | solution.py:77
  41.4 17.0 %all-to-all-start.1 = ((bf16[16,4,3584]{2,1,0:T(4,128)(2,1)}), bf16[16,4,3584]{2,1,0:T(4,128)(2,1)S(1)}, u32[]{:S(2)}, u32[]{:S(2)}) async-start(bf16[16,4,3584]{2,1,0:T(4,128)(2,1)} %reshape.219), calls=%async_computation.1 | async-start | bytes 917504 | tf_op jit(solution)/shard_map/while/body/eval_jaxpr/all_to_all | solution.py:49
  59.9 5.2 %collective-permute-start = (bf16[8,3584]{1,0:T(8,128)(2,1)S(1)}, bf16[8,3584]{1,0:T(8,128)(2,1)S(1)}, u32[]{:S(2)}, u32[]{:S(2)}) collective-permute-start(bf16[8,3584]{1,0:T(8,128)(2,1)S(1)} %get-tuple-element.401), channel_id=1, source_target_pairs={{0,16},{1,17},{2,18},{3,19},{4,20},{5,21},{6,22},{7,23},{8,24},{9,... | collective-permute-start | bytes 172040 | tf_op jit(solution)/shard_map/while/body/eval_jaxpr/ppermute | solution.py:12
  70.1 17.0 %all-to-all-start = ((bf16[16,4,3584]{2,1,0:T(4,128)(2,1)}), bf16[16,4,3584]{2,1,0:T(4,128)(2,1)S(1)}, u32[]{:S(2)}, u32[]{:S(2)}) async-start(bf16[16,4,3584]{2,1,0:T(4,128)(2,1)} %bitcast.77), calls=%async_computation | async-start | bytes 917504 | tf_op jit(solution)/shard_map/while/body/eval_jaxpr/all_to_all | solution.py:77
  95.6 17.0 %all-to-all-start.1 = ((bf16[16,4,3584]{2,1,0:T(4,128)(2,1)}), bf16[16,4,3584]{2,1,0:T(4,128)(2,1)S(1)}, u32[]{:S(2)}, u32[]{:S(2)}) async-start(bf16[16,4,3584]{2,1,0:T(4,128)(2,1)} %reshape.219), calls=%async_computation.1 | async-start | bytes 917504 | tf_op jit(solution)/shard_map/while/body/eval_jaxpr/all_to_all | solution.py:49
  114.1 6.1 %collective-permute-start = (bf16[8,3584]{1,0:T(8,128)(2,1)S(1)}, bf16[8,3584]{1,0:T(8,128)(2,1)S(1)}, u32[]{:S(2)}, u32[]{:S(2)}) collective-permute-start(bf16[8,3584]{1,0:T(8,128)(2,1)S(1)} %get-tuple-element.401), channel_id=1, source_target_pairs={{0,16},{1,17},{2,18},{3,19},{4,20},{5,21},{6,22},{7,23},{8,24},{9,... | collective-permute-start | bytes 172040 | tf_op jit(solution)/shard_map/while/body/eval_jaxpr/ppermute | solution.py:12
  125.2 17.0 %all-to-all-start = ((bf16[16,4,3584]{2,1,0:T(4,128)(2,1)}), bf16[16,4,3584]{2,1,0:T(4,128)(2,1)S(1)}, u32[]{:S(2)}, u32[]{:S(2)}) async-start(bf16[16,4,3584]{2,1,0:T(4,128)(2,1)} %bitcast.77), calls=%async_computation | async-start | bytes 917504 | tf_op jit(solution)/shard_map/while/body/eval_jaxpr/all_to_all | solution.py:77
  150.6 17.0 %all-to-all-start.1 = ((bf16[16,4,3584]{2,1,0:T(4,128)(2,1)}), bf16[16,4,3584]{2,1,0:T(4,128)(2,1)S(1)}, u32[]{:S(2)}, u32[]{:S(2)}) async-start(bf16[16,4,3584]{2,1,0:T(4,128)(2,1)} %reshape.219), calls=%async_computation.1 | async-start | bytes 917504 | tf_op jit(solution)/shard_map/while/body/eval_jaxpr/all_to_all | solution.py:49
  169.1 6.1 %collective-permute-start = (bf16[8,3584]{1,0:T(8,128)(2,1)S(1)}, bf16[8,3584]{1,0:T(8,128)(2,1)S(1)}, u32[]{:S(2)}, u32[]{:S(2)}) collective-permute-start(bf16[8,3584]{1,0:T(8,128)(2,1)S(1)} %get-tuple-element.401), channel_id=1, source_target_pairs={{0,16},{1,17},{2,18},{3,19},{4,20},{5,21},{6,22},{7,23},{8,24},{9,... | collective-permute-start | bytes 172040 | tf_op jit(solution)/shard_map/while/body/eval_jaxpr/ppermute | solution.py:12
  175.9 64.5 %all-gather.2.cloned.1.call-start = ((), (), s32[]{:S(2)}) async-start(), calls=%async_computation.3 | async-start | bytes 1949696 | tf_op jit(solution)/shard_map/all_gather | solution.py:110
  197.4 85.6 %copy-start.1 = (s32[2,128]{1,0:T(2,128)S(1)}, s32[2,128]{1,0:T(2,128)}, u32[]{:S(2)}) copy-start(s32[2,128]{1,0:T(2,128)} %param.22) | copy-start | bytes 3076
  197.4 126.7 %copy-start.2 = (s32[2,128]{1,0:T(2,128)S(1)}, s32[2,128]{1,0:T(2,128)}, u32[]{:S(2)}) copy-start(s32[2,128]{1,0:T(2,128)} %param.23) | copy-start | bytes 3076
Sparse Core Ops, SparseCore 0:
  176.0 21.3 all-reduce.2
  199.7 40.6 all-gather.1
where the time goes:
time: 334 us; the launch traced here: 332 us
  waiting for transfers between devices  141 us (42%)
  blocking collectives  79.3 us (24%)
  starting transfers between devices  38.5 us (12%)
  matrix products  28 us (8%)
  other arithmetic  16 us (5%)
  local copies, waits for them, and re-layouts  15.4 us (5%)
  between operations  14.1 us (4%)
    all_gather x1, waiting for transfers between devices, body(): lax.all_gather(shared, 'expert', axis=1, tiled=True)  42.9 us
    psum x1, blocking collectives, body(): lax.psum((local_sum, target_part), ('section', 'expert'))  40.9 us
    all_to_all x3, waiting for transfers between devices, expert_rows(): lax.all_to_all(partial_value.reshape(sources, slot_count, width_in), 'exp...  39.2 us
    pmax x1, blocking collectives, body(): peak = lax.pmax(local_max, ('section', 'expert'))  38.4 us
    all_to_all x3, waiting for transfers between devices, expert_layer(): lax.all_to_all(outgoing, 'expert', split_axis=0, concat_axis=0, tiled=True)  31.6 us
    psum x1, waiting for transfers between devices, broadcast(): return lax.psum(block, axis)  21.4 us
    all_to_all x3, starting transfers between devices, expert_layer(): lax.all_to_all(outgoing, 'expert', split_axis=0, concat_axis=0, tiled=True)  15 us
    dot_general x3, matrix products, expert_rows(): jnp.dot(inner, w_down[0], preferred_element_type=jnp.float32)  13.8 us
  transfers between devices with their start and end apart: 11, of which 11 were waited for; matrix products, arithmetic and copies ran while one was open for 3% of the time, Pallas kernels for 0%

commit v1 on v0

v1 whole, which is shorter than its diff:
```python
import jax
import jax.numpy as jnp
from jax import lax
from jax.sharding import PartitionSpec as P


SEQS = 4
PAIR = 2


def rms_scale(states, gain):
    values = states.astype(jnp.float32)
    factor = lax.rsqrt(jnp.mean(values * values, -1, keepdims=True) + 1e-06)
    return values * factor * gain


def body(
    hidden_in, layer_gain, router, w_gate, w_up, w_down, final_gain, head, routing, targets, seq_ids
):
    micro, toks, width = hidden_in.shape
    experts = router.shape[2]
    tops = routing.shape[3]
    sections = lax.axis_size("section")
    members = lax.axis_size("expert")
    section_pos = lax.axis_index("section")
    member_pos = lax.axis_index("expert")
    splits = members // experts
    halves = splits // PAIR
    groups = members // PAIR
    cap = min(toks, 9 * toks * tops // (8 * experts))
    parity = member_pos % PAIR
    same_core = [[g * PAIR + c for g in range(groups)] for c in range(PAIR)]
    partner = [(i, i ^ 1) for i in range(members)]

    def exchange(rows):
        return lax.all_to_all(
            rows, "expert", split_axis=0, concat_axis=0, axis_index_groups=same_core, tiled=True
        )

    def swap_core(rows):
        return lax.ppermute(rows, "expert", partner)

    head_blocks = [head]
    for shift in range(1, micro):
        ring = [(s, s - s % micro + (s + shift) % micro) for s in range(sections)]
        head_blocks.append(lax.ppermute(head, "section", ring))
    batch_pos = section_pos % micro

    route = routing[0].reshape(micro, toks * tops)
    same = route[:, :, None] == route[:, None, :]
    order = jnp.arange(toks * tops)
    slot = jnp.sum(jnp.where(same & (order[None, None, :] < order[None, :, None]), 1, 0), -1)
    batch_ids = jnp.arange(micro, dtype=jnp.int32)[:, None]
    place = ((route * micro + batch_ids) * cap + slot).reshape(micro * toks, tops)
    row = jnp.arange(experts * halves * micro * cap, dtype=jnp.int32)
    per_expert = micro * cap
    row_place = row // (halves * per_expert) * per_expert + row % per_expert
    hit = place[:, :, None] == row_place[None, None, :]
    pack = jnp.any(hit, 1).astype(jnp.bfloat16).T
    chosen = routing[0].reshape(micro * toks, tops)[:, :, None] == jnp.arange(experts, dtype=jnp.int32)

    def ffn(rows):
        gate_val = jnp.dot(rows, w_gate[0], preferred_element_type=jnp.float32)
        up_val = jnp.dot(rows, w_up[0], preferred_element_type=jnp.float32)
        inner = (jax.nn.silu(gate_val) * up_val).astype(jnp.bfloat16)
        return jnp.dot(inner, w_down[0], preferred_element_type=jnp.float32).astype(jnp.bfloat16)

    def layer(states):
        normed = rms_scale(states, layer_gain[0]).astype(jnp.bfloat16)
        packed = jnp.dot(pack, normed, preferred_element_type=jnp.float32).astype(jnp.bfloat16)
        mine = exchange(packed)
        other = swap_core(mine)
        logits = jnp.dot(normed, router[0], preferred_element_type=jnp.float32)
        affinity = jax.nn.sigmoid(jnp.sum(jnp.where(chosen, logits[:, None, :], 0.0), -1))
        weight = affinity / jnp.sum(affinity, -1, keepdims=True)
        mix = jnp.sum(jnp.where(hit, 2.5 * weight[:, :, None], 0.0), 1)
        mix_hi = lax.reduce_precision(mix, 8, 7)
        mix_lo = (mix - mix_hi).astype(jnp.bfloat16)
        mix_hi = mix_hi.astype(jnp.bfloat16)
        parts = ffn(jnp.concatenate([mine, other], 0))
        half = parts.shape[0] // 2
        total = parts[:half].astype(jnp.float32) + swap_core(parts[half:]).astype(jnp.float32)
        back = exchange(total.astype(jnp.bfloat16))
        mixed = jnp.dot(mix_hi, back, preferred_element_type=jnp.float32)
        mixed = mixed + jnp.dot(mix_lo, back, preferred_element_type=jnp.float32)
        return (states.astype(jnp.float32) + mixed).astype(jnp.bfloat16)

    states = hidden_in.reshape(micro * toks, width)
    for tick in range(sections):
        states = layer(states)
        if tick < sections - 1:
            states = lax.ppermute(states, "section", [(tick, tick + 1)])

    states = states.reshape(micro, toks, width)
    last = sections - 1
    mine = states[last % micro]
    for s in range(sections - 1):
        moved = lax.ppermute(states[s % micro], "section", [(last, s)])
        mine = jnp.where(section_pos == s, moved, mine)
    final = rms_scale(mine, final_gain).astype(jnp.bfloat16)
    near = exchange(jnp.broadcast_to(final[None], (groups, toks, width)).reshape(groups * toks, width))
    rows = jnp.concatenate([near, swap_core(near)], 0)

    vocab = head.shape[0]
    my_targets = lax.dynamic_index_in_dim(targets, batch_pos, 0, keepdims=False)
    my_targets = my_targets.reshape(groups, PAIR, toks).transpose(1, 0, 2)
    my_targets = jnp.where(parity == 0, my_targets, my_targets[::-1]).reshape(-1)
    logits = [
        jnp.dot(rows, block.T, preferred_element_type=jnp.float32) for block in head_blocks
    ]
    peak = logits[0].max(-1)
    for block in logits[1:]:
        peak = jnp.maximum(peak, block.max(-1))
    summed = jnp.zeros_like(peak)
    target = jnp.zeros_like(peak)
    for shift, block in enumerate(logits):
        owner = section_pos - batch_pos + (batch_pos - shift) % micro
        start = (owner * members + member_pos) * vocab
        ids = start + jnp.arange(vocab, dtype=jnp.int32)
        summed = summed + jnp.sum(jnp.exp(block - peak[:, None]), -1)
        target = target + jnp.sum(jnp.where(my_targets[:, None] == ids[None, :], block, 0.0), -1)
    stats = jnp.stack([peak, summed, target]).reshape(3, PAIR, groups * toks)
    stats = jnp.where(parity == 0, stats, stats[:, ::-1]).reshape(1, 3 * PAIR * groups * toks)
    world = sections * members
    stats = lax.all_to_all(
        jnp.broadcast_to(stats, (world, stats.shape[1])),
        ("section", "expert"),
        split_axis=0,
        concat_axis=0,
        tiled=True,
    )
    stats = stats.reshape(sections // micro, micro, members, 3, PAIR, groups, toks)
    peaks, sums, hits = stats[:, :, :, 0], stats[:, :, :, 1], stats[:, :, :, 2]
    top = jnp.max(peaks, (0, 2), keepdims=True)
    total = jnp.sum(sums * jnp.exp(peaks - top), (0, 2))
    logprob = jnp.sum(hits, (0, 2)) - (top[0, :, 0] + jnp.log(total))
    logprob = logprob.transpose(0, 2, 1, 3).reshape(micro, members * toks)
    token_part = lax.dynamic_slice_in_dim(logprob, member_pos * toks, toks, 1)
    member = seq_ids[:, :, None] == jnp.arange(SEQS, dtype=jnp.int32)[None, None, :]
    sums = jnp.sum(jnp.where(member, logprob[..., None], 0.0), 1)
    counts = jnp.sum(member.astype(jnp.float32), 1)
    return (token_part, sums / counts)


def solution(mesh):
    return jax.shard_map(
        body,
        mesh=mesh,
        in_specs=(
            P(None, "expert", None),
            P("section", None),
            P("section", None, None),
            P("section", None, "expert"),
            P("section", None, "expert"),
            P("section", "expert", None),
            P(),
            P(("section", "expert"), None),
            P("section", None, "expert", None),
            P(),
            P(),
        ),
        out_specs=(P(None, "expert"), P()),
        check_vma=False,
    )
```

time: 334 us -> 170 us (0.51)
  waiting for transfers between devices: 141 us -> 66.7 us
  blocking collectives: 79.3 us -> 51.7 us
  starting transfers between devices: 38.5 us -> 18.8 us
  between operations: 14.1 us -> 0.97 us
  local copies, waits for them, and re-layouts: 15.4 us -> 4.63 us
  other arithmetic: 16 us -> 6.17 us
  matrix products: 28 us -> 20 us
    all_to_all x0 -> x3, blocking collectives: none -> 51.7 us  [exchange(): lax.all_to_all(rows, 'expert', split_axis=0, concat_axis=0, axis_index_gr...]
    all_gather x1 -> x0, waiting for transfers between devices: 42.9 us -> none  [body(): lax.all_gather(shared, 'expert', axis=1, tiled=True)]
    psum x1 -> x0, blocking collectives: 40.9 us -> none  [body(): lax.psum((local_sum, target_part), ('section', 'expert'))]
    pmax x1 -> x0, blocking collectives: 38.4 us -> none  [body(): peak = lax.pmax(local_max, ('section', 'expert'))]
    all_to_all x6 -> x3, waiting for transfers between devices: 70.8 us -> 33.7 us  [the longest x2 26.4 us: exchange(): lax.all_to_all(rows, 'expert', split_axis=0, concat_axis=0, axis_index_gr...]
    ppermute x3 -> x8, waiting for transfers between devices: 5.41 us -> 33 us  [the longest x1 19.4 us: body(): head_blocks.append(lax.ppermute(head, 'section', ring))]
    psum x1 -> x0, waiting for transfers between devices: 21.4 us -> none  [broadcast(): return lax.psum(block, axis)]
    all_to_all x6 -> x3, starting transfers between devices: 26.4 us -> 11 us  [the longest x2 7.14 us: exchange(): lax.all_to_all(rows, 'expert', split_axis=0, concat_axis=0, axis_index_gr...]
  transfers between devices with their start and end apart: 11 -> 11, of which waited for: 11 -> 11; matrix products, arithmetic and copies ran while one was open for 3% -> 1% of each run, Pallas kernels for 0% -> 0%
where the time goes in v1:
time: 170 us; the launch traced here: 169 us
  waiting for transfers between devices  66.7 us (39%)
  blocking collectives  51.7 us (30%)
  matrix products  20 us (12%)
  starting transfers between devices  18.8 us (11%)
  other arithmetic  6.17 us (4%)
  local copies, waits for them, and re-layouts  4.63 us (3%)
    all_to_all x3, blocking collectives, exchange(): lax.all_to_all(rows, 'expert', split_axis=0, concat_axis=0, axis_index_gr...  51.7 us
    all_to_all x2, waiting for transfers between devices, exchange(): lax.all_to_all(rows, 'expert', split_axis=0, concat_axis=0, axis_index_gr...  26.4 us
    ppermute x1, waiting for transfers between devices, body(): head_blocks.append(lax.ppermute(head, 'section', ring))  19.4 us
    dot_general x2, matrix products, ffn(): jnp.dot(inner, w_down[0], preferred_element_type=jnp.float32)  8.9 us
    ppermute x5, waiting for transfers between devices, swap_core(): return lax.ppermute(rows, 'expert', partner)  8.5 us
    all_to_all x1, waiting for transfers between devices, body(): lax.all_to_all(jnp.broadcast_to(stats, (world, stats.shape[1])), ('sectio...  7.33 us
    all_to_all x2, starting transfers between devices, exchange(): lax.all_to_all(rows, 'expert', split_axis=0, concat_axis=0, axis_index_gr...  7.14 us
    dot_general x2, matrix products, ffn(): up_val = jnp.dot(rows, w_up[0], preferred_element_type=jnp.float32)  5.34 us
  transfers between devices with their start and end apart: 11, of which 11 were waited for; matrix products, arithmetic and copies ran while one was open for 1% of the time, Pallas kernels for 0%

profile of v1, /device:TPU:0, one launch (start us, length us, event | category | flops | bytes accessed | tf_op | source)
XLA Modules:
  0.0 169.0 jit_solution(5127702445238640479)
XLA Ops:
  0.6 0.7 copy.42
  1.3 0.8 copy.43
  2.3 0.2 select_reduce_fusion.2
  2.7 1.0 fusion.32
  3.9 0.8 reduce.5
  4.7 1.2 fusion
  5.9 20.3 %all_to_all.63 = bf16[8,8,3584]{2,1,0:T(8,128)(2,1)S(1)} all-to-all(bf16[8,8,3584]{2,1,0:T(8,128)(2,1)S(1)} %fusion), channel_id=1, replica_groups={{0,2,4,6,8,10,12,14},{1,3,5,7,9,11,13,15},{16,18,20,22,24,26,28,30},{17..., dimensions={0} | all-to-all | bytes 917504 | tf_op jit(solution)/shard_map/all_to_all | solution.py:36
  26.2 1.8 %collective-permute-done = bf16[64,3584]{1,0:T(8,128)(2,1)S(1)} collective-permute-done((bf16[64,3584]{1,0:T(8,128)(2,1)S(1)}, bf16[64,3584]{1,0:T(8,128)(2,1)S(1)}, u32[]{:S(2)}, u32[]{:S(2)}) %collective-permute-start) | collective-permute-done | bytes 458784 | tf_op jit(solution)/shard_map/ppermute | solution.py:41
  28.0 2.7 %fusion.10 = f32[128,512]{1,0:T(8,128)S(1)} fusion(bf16[1,3584,512]{2,1,0:T(8,128)(2,1)} %param.15, bf16[64,3584]{1,0:T(8,128)(2,1)S(1)} %collective-permute-done, bf16[64,3584]{1,0:T(8,128)(2,1)S(1)} %bitcast.90), kind=kOutput, calls=%fused_computation.16 | convolution fusion | flops 471597056 | bytes 4849664 | tf_op jit(solution)/shard_map/dot_general | solution.py:64
  30.7 4.4 %convolution_convert_fusion.1 = bf16[128,3584]{1,0:T(8,128)(2,1)S(1)} fusion(bf16[1,512,3584]{2,1,0:T(8,128)(2,1)} %param.16, f32[128,512]{1,0:T(8,128)S(1)} %fusion.10, bf16[1,3584,512]{2,1,0:T(8,128)(2,1)} %param.14, bf16[64,3584]{1,0:T(8,128)(2,1)S(1)} %collective-permute-done, bf16[64,3584]{1,0:T(8,128)(2,1)S(1)} %bitcast.91), kind=kOutput, calls=%fused_computation.1 | convolution fusion | flops 942211072 | bytes 9437184 | tf_op jit(solution)/shard_map/dot_general | solution.py:66
  35.2 0.2 collective-permute-start.1
  35.4 1.7 collective-permute-done.1
  37.1 0.9 fusion.18
  38.0 3.5 %all-to-all-start.1 = ((bf16[8,8,3584]{2,1,0:T(8,128)(2,1)}), bf16[8,8,3584]{2,1,0:T(8,128)(2,1)S(1)}, u32[]{:S(2)}, u32[]{:S(2)}) async-start(bf16[8,8,3584]{2,1,0:T(8,128)(2,1)} %fusion.18), calls=%async_computation.1 | async-start | bytes 917504 | tf_op jit(solution)/shard_map/all_to_all | solution.py:36
  41.5 0.2 fusion.52
  41.9 13.2 %all-to-all-done.1 = bf16[8,8,3584]{2,1,0:T(8,128)(2,1)S(1)} async-done(((bf16[8,8,3584]{2,1,0:T(8,128)(2,1)}), bf16[8,8,3584]{2,1,0:T(8,128)(2,1)S(1)}, u32[]{:S(2)}, u32[]{:S(2)}) %all-to-all-start.1) | async-done | bytes 458784 | tf_op jit(solution)/shard_map/all_to_all | solution.py:36
  55.2 0.2 fusion.4
  55.4 3.4 %collective-permute-start.2 = (bf16[16,3584]{1,0:T(8,128)(2,1)S(1)}, bf16[16,3584]{1,0:T(8,128)(2,1)S(1)}, u32[]{:S(2)}, u32[]{:S(2)}) collective-permute-start(bf16[16,3584]{1,0:T(8,128)(2,1)S(1)} %fusion.4), channel_id=1, source_target_pairs={{0,16},{1,17},{2,18},{3,19},{4,20},{5,21},{6,22},{7,23},{8,24},{9,... | collective-permute-start | bytes 344072 | tf_op jit(solution)/shard_map/ppermute | solution.py:92
  58.8 2.3 %collective-permute-done.2 = bf16[16,3584]{1,0:T(8,128)(2,1)S(1)} collective-permute-done((bf16[16,3584]{1,0:T(8,128)(2,1)S(1)}, bf16[16,3584]{1,0:T(8,128)(2,1)S(1)}, u32[]{:S(2)}, u32[]{:S(2)}) %collective-permute-start.2) | collective-permute-done | bytes 114720 | tf_op jit(solution)/shard_map/ppermute | solution.py:92
  61.3 0.3 fusion.1
  61.7 16.2 %all_to_all.64 = bf16[8,8,3584]{2,1,0:T(8,128)(2,1)S(1)} all-to-all(bf16[8,8,3584]{2,1,0:T(8,128)(2,1)S(1)} %fusion.1), channel_id=1, replica_groups={{0,2,4,6,8,10,12,14},{1,3,5,7,9,11,13,15},{16,18,20,22,24,26,28,30},{17..., dimensions={0} | all-to-all | bytes 917504 | tf_op jit(solution)/shard_map/all_to_all | solution.py:36
  77.9 1.8 %collective-permute-done.3 = bf16[64,3584]{1,0:T(8,128)(2,1)S(1)} collective-permute-done((bf16[64,3584]{1,0:T(8,128)(2,1)S(1)}, bf16[64,3584]{1,0:T(8,128)(2,1)S(1)}, u32[]{:S(2)}, u32[]{:S(2)}) %collective-permute-start.3) | collective-permute-done | bytes 458784 | tf_op jit(solution)/shard_map/ppermute | solution.py:41
  79.7 2.7 %fusion.8 = f32[128,512]{1,0:T(8,128)S(1)} fusion(bf16[1,3584,512]{2,1,0:T(8,128)(2,1)} %param.15, bf16[64,3584]{1,0:T(8,128)(2,1)S(1)} %collective-permute-done.3, bf16[64,3584]{1,0:T(8,128)(2,1)S(1)} %bitcast.93), kind=kOutput, calls=%fused_computation.14 | convolution fusion | flops 471597056 | bytes 4849664 | tf_op jit(solution)/shard_map/dot_general | solution.py:64
  82.4 4.5 %convolution_convert_fusion = bf16[128,3584]{1,0:T(8,128)(2,1)S(1)} fusion(bf16[1,512,3584]{2,1,0:T(8,128)(2,1)} %param.16, f32[128,512]{1,0:T(8,128)S(1)} %fusion.8, bf16[1,3584,512]{2,1,0:T(8,128)(2,1)} %param.14, bf16[64,3584]{1,0:T(8,128)(2,1)S(1)} %collective-permute-done.3, bf16[64,3584]{1,0:T(8,128)(2,1)S(1)} %bitcast.94), kind=kOutput, calls=%fused_computation | convolution fusion | flops 942211072 | bytes 9437184 | tf_op jit(solution)/shard_map/dot_general | solution.py:66
  86.9 0.2 collective-permute-start.4
  87.1 1.7 collective-permute-done.4
  88.8 0.9 fusion.19
  89.6 3.6 %all-to-all-start.3 = ((bf16[8,8,3584]{2,1,0:T(8,128)(2,1)}), bf16[8,8,3584]{2,1,0:T(8,128)(2,1)S(1)}, u32[]{:S(2)}, u32[]{:S(2)}) async-start(bf16[8,8,3584]{2,1,0:T(8,128)(2,1)} %fusion.19), calls=%async_computation.3 | async-start | bytes 917504 | tf_op jit(solution)/shard_map/all_to_all | solution.py:36
  93.3 0.2 fusion.59
  93.6 13.2 %all-to-all-done.3 = bf16[8,8,3584]{2,1,0:T(8,128)(2,1)S(1)} async-done(((bf16[8,8,3584]{2,1,0:T(8,128)(2,1)}), bf16[8,8,3584]{2,1,0:T(8,128)(2,1)S(1)}, u32[]{:S(2)}, u32[]{:S(2)}) %all-to-all-start.3) | async-done | bytes 458784 | tf_op jit(solution)/shard_map/all_to_all | solution.py:36
  107.0 0.2 fusion.5
  107.2 1.3 collective-permute-start.5
  108.5 2.7 %collective-permute-start.7 = (bf16[256,3584]{1,0:T(8,128)(2,1)S(1)}, bf16[256,3584]{1,0:T(8,128)(2,1)}, u32[]{:S(2)}, u32[]{:S(2)}) collective-permute-start(bf16[256,3584]{1,0:T(8,128)(2,1)S(1)} %copy-done.4), channel_id=1, source_target_pairs={{0,16},{16,0},{1,17},{17,1},{2,18},{18,2},{3,19},{19,3},{4,20},{20... | collective-permute-start | bytes 5505032 | tf_op jit(solution)/shard_map/ppermute | solution.py:46
  111.2 2.7 %collective-permute-done.5 = bf16[8,3584]{1,0:T(8,128)(2,1)S(1)} collective-permute-done((bf16[8,3584]{1,0:T(8,128)(2,1)S(1)}, bf16[8,3584]{1,0:T(8,128)(2,1)S(1)}, u32[]{:S(2)}, u32[]{:S(2)}) %collective-permute-start.5) | collective-permute-done | bytes 57376 | tf_op jit(solution)/shard_map/ppermute | solution.py:98
  114.2 15.2 %all_to_all.65 = bf16[8,8,3584]{2,1,0:T(8,128)(2,1)S(1)} all-to-all(bf16[8,8,3584]{2,1,0:T(8,128)(2,1)S(1)} %broadcast_in_dim.104), channel_id=1, replica_groups={{0,2,4,6,8,10,12,14},{1,3,5,7,9,11,13,15},{16,18,20,22,24,26,28,30},{17..., dimensions={0} | all-to-all | bytes 917504 | tf_op jit(solution)/shard_map/all_to_all | solution.py:36
  129.7 1.5 collective-permute-done.6
  131.2 0.8 fusion.82
  132.0 19.4 %collective-permute-done.7 = bf16[256,3584]{1,0:T(8,128)(2,1)} collective-permute-done((bf16[256,3584]{1,0:T(8,128)(2,1)S(1)}, bf16[256,3584]{1,0:T(8,128)(2,1)}, u32[]{:S(2)}, u32[]{:S(2)}) %collective-permute-start.7) | collective-permute-done | bytes 1835040 | tf_op jit(solution)/shard_map/ppermute | solution.py:46
  151.4 2.3 %fusion.83 = (f32[128]{0:T(128)S(1)}, f32[128,256]{1,0:T(8,128)S(1)}) fusion(bf16[256,3584]{1,0:T(8,128)(2,1)} %collective-permute-done.7, bf16[64,3584]{1,0:T(8,128)(2,1)S(1)} %collective-permute-done.6, bf16[64,3584]{1,0:T(8,128)(2,1)S(1)} %bitcast.97), kind=kOutput, calls=%fused_computation.137 | convolution fusion | flops 236748672 | bytes 2884096 | tf_op jit(solution)/shard_map/dot_general | solution.py:109
  153.8 0.2 select_reduce_fusion.1
  154.3 0.7 broadcast_in_dim.107
  155.0 3.9 %all-to-all-start.5 = ((f32[32,1,384]{2,1,0:T(1,128)}), f32[32,1,384]{2,1,0:T(1,128)S(1)}, u32[]{:S(2)}, u32[]{:S(2)}) async-start(f32[32,1,384]{2,1,0:T(1,128)} %broadcast_in_dim.107), calls=%async_computation.5 | async-start | bytes 98304 | tf_op jit(solution)/shard_map/all_to_all | solution.py:125
  158.9 7.3 %all-to-all-done.5 = f32[32,1,384]{2,1,0:T(1,128)S(1)} async-done(((f32[32,1,384]{2,1,0:T(1,128)}), f32[32,1,384]{2,1,0:T(1,128)S(1)}, u32[]{:S(2)}, u32[]{:S(2)}) %all-to-all-start.5) | async-done | bytes 49184 | tf_op jit(solution)/shard_map/all_to_all | solution.py:125
  166.4 0.2 reshape.318
  166.6 0.3 slice_reduce_fusion.1
  167.0 0.4 fusion.44
  167.8 0.6 constant_dynamic-slice_fusion
  168.4 0.6 div.70
  (70 shorter events, 2.9 us)
Async XLA Ops:
  0.6 40.9 %copy-start = (bf16[1,3584,4]{1,2,0:T(4,128)(2,1)S(1)}, bf16[1,3584,4]{1,2,0:T(4,128)(2,1)}, u32[]{:S(2)}) copy-start(bf16[1,3584,4]{1,2,0:T(4,128)(2,1)} %param.13) | copy-start | bytes 86020
  26.2 1.8 %collective-permute-start = (bf16[64,3584]{1,0:T(8,128)(2,1)S(1)}, bf16[64,3584]{1,0:T(8,128)(2,1)S(1)}, u32[]{:S(2)}, u32[]{:S(2)}) collective-permute-start(bf16[64,3584]{1,0:T(8,128)(2,1)S(1)} %bitcast.89), channel_id=1, source_target_pairs={{0,1},{1,0},{2,3},{3,2},{4,5},{5,4},{6,7},{7,6},{8,9},{9,8},{10,11... | collective-permute-start | bytes 1376264 | tf_op jit(solution)/shard_map/ppermute | solution.py:41
  35.2 6.4 %copy-start.1 = (bf16[2,8,3584]{2,1,0:T(8,128)(2,1)S(1)}, bf16[2,8,3584]{2,1,0:T(8,128)(2,1)}, u32[]{:S(2)}) copy-start(bf16[2,8,3584]{2,1,0:T(8,128)(2,1)} %param.11) | copy-start | bytes 344068
  35.2 1.9 %collective-permute-start.1 = (bf16[64,3584]{1,0:T(8,128)(2,1)S(1)}, bf16[64,3584]{1,0:T(8,128)(2,1)S(1)}, u32[]{:S(2)}, u32[]{:S(2)}) collective-permute-start(bf16[64,3584]{1,0:T(8,128)(2,1)S(1)} %slice.39), channel_id=1, source_target_pairs={{0,1},{1,0},{2,3},{3,2},{4,5},{5,4},{6,7},{7,6},{8,9},{9,8},{10,11... | collective-permute-start | bytes 1376264 | tf_op jit(solution)/shard_map/ppermute | solution.py:41
  38.0 17.1 %all-to-all-start.1 = ((bf16[8,8,3584]{2,1,0:T(8,128)(2,1)}), bf16[8,8,3584]{2,1,0:T(8,128)(2,1)S(1)}, u32[]{:S(2)}, u32[]{:S(2)}) async-start(bf16[8,8,3584]{2,1,0:T(8,128)(2,1)} %fusion.18), calls=%async_computation.1 | async-start | bytes 917504 | tf_op jit(solution)/shard_map/all_to_all | solution.py:36
  55.4 5.8 %collective-permute-start.2 = (bf16[16,3584]{1,0:T(8,128)(2,1)S(1)}, bf16[16,3584]{1,0:T(8,128)(2,1)S(1)}, u32[]{:S(2)}, u32[]{:S(2)}) collective-permute-start(bf16[16,3584]{1,0:T(8,128)(2,1)S(1)} %fusion.4), channel_id=1, source_target_pairs={{0,16},{1,17},{2,18},{3,19},{4,20},{5,21},{6,22},{7,23},{8,24},{9,... | collective-permute-start | bytes 344072 | tf_op jit(solution)/shard_map/ppermute | solution.py:92
  77.9 1.8 %collective-permute-start.3 = (bf16[64,3584]{1,0:T(8,128)(2,1)S(1)}, bf16[64,3584]{1,0:T(8,128)(2,1)S(1)}, u32[]{:S(2)}, u32[]{:S(2)}) collective-permute-start(bf16[64,3584]{1,0:T(8,128)(2,1)S(1)} %bitcast.92), channel_id=1, source_target_pairs={{0,1},{1,0},{2,3},{3,2},{4,5},{5,4},{6,7},{7,6},{8,9},{9,8},{10,11... | collective-permute-start | bytes 1376264 | tf_op jit(solution)/shard_map/ppermute | solution.py:41
  86.9 21.7 %copy-start.4 = (bf16[256,3584]{1,0:T(8,128)(2,1)S(1)}, bf16[256,3584]{1,0:T(8,128)(2,1)}, u32[]{:S(2)}) copy-start(bf16[256,3584]{1,0:T(8,128)(2,1)} %param.18) | copy-start | bytes 5505028
  86.9 1.9 %collective-permute-start.4 = (bf16[64,3584]{1,0:T(8,128)(2,1)S(1)}, bf16[64,3584]{1,0:T(8,128)(2,1)S(1)}, u32[]{:S(2)}, u32[]{:S(2)}) collective-permute-start(bf16[64,3584]{1,0:T(8,128)(2,1)S(1)} %slice.41), channel_id=1, source_target_pairs={{0,1},{1,0},{2,3},{3,2},{4,5},{5,4},{6,7},{7,6},{8,9},{9,8},{10,11... | collective-permute-start | bytes 1376264 | tf_op jit(solution)/shard_map/ppermute | solution.py:41
  89.6 24.4 %copy-start.2 = (f32[3584]{0:T(1024)S(1)}, f32[3584]{0:T(1024)}, u32[]{:S(2)}) copy-start(f32[3584]{0:T(1024)} %param.17) | copy-start | bytes 43012
  89.6 17.2 %all-to-all-start.3 = ((bf16[8,8,3584]{2,1,0:T(8,128)(2,1)}), bf16[8,8,3584]{2,1,0:T(8,128)(2,1)S(1)}, u32[]{:S(2)}, u32[]{:S(2)}) async-start(bf16[8,8,3584]{2,1,0:T(8,128)(2,1)} %fusion.19), calls=%async_computation.3 | async-start | bytes 917504 | tf_op jit(solution)/shard_map/all_to_all | solution.py:36
  93.5 35.9 %copy-start.5 = (s32[2,128]{1,0:T(2,128)S(1)}, s32[2,128]{1,0:T(2,128)}, u32[]{:S(2)}) copy-start(s32[2,128]{1,0:T(2,128)} %param.20) | copy-start | bytes 3076
  107.2 6.7 %collective-permute-start.5 = (bf16[8,3584]{1,0:T(8,128)(2,1)S(1)}, bf16[8,3584]{1,0:T(8,128)(2,1)S(1)}, u32[]{:S(2)}, u32[]{:S(2)}) collective-permute-start(bf16[8,3584]{1,0:T(8,128)(2,1)S(1)} %slice.42), channel_id=1, source_target_pairs={{16,0},{17,1},{18,2},{19,3},{20,4},{21,5},{22,6},{23,7},{24,8},{25... | collective-permute-start | bytes 172040 | tf_op jit(solution)/shard_map/ppermute | solution.py:98
  108.5 42.9 %collective-permute-start.7 = (bf16[256,3584]{1,0:T(8,128)(2,1)S(1)}, bf16[256,3584]{1,0:T(8,128)(2,1)}, u32[]{:S(2)}, u32[]{:S(2)}) collective-permute-start(bf16[256,3584]{1,0:T(8,128)(2,1)S(1)} %copy-done.4), channel_id=1, source_target_pairs={{0,16},{16,0},{1,17},{17,1},{2,18},{18,2},{3,19},{19,3},{4,20},{20... | collective-permute-start | bytes 5505032 | tf_op jit(solution)/shard_map/ppermute | solution.py:46
  129.4 1.8 %collective-permute-start.6 = (bf16[64,3584]{1,0:T(8,128)(2,1)S(1)}, bf16[64,3584]{1,0:T(8,128)(2,1)S(1)}, u32[]{:S(2)}, u32[]{:S(2)}) collective-permute-start(bf16[64,3584]{1,0:T(8,128)(2,1)S(1)} %bitcast.95), channel_id=1, source_target_pairs={{0,1},{1,0},{2,3},{3,2},{4,5},{5,4},{6,7},{7,6},{8,9},{9,8},{10,11... | collective-permute-start | bytes 1376264 | tf_op jit(solution)/shard_map/ppermute | solution.py:41
  153.7 14.0 %copy-start.3 = (s32[2,128]{1,0:T(2,128)S(1)}, s32[2,128]{1,0:T(2,128)}, u32[]{:S(2)}) copy-start(s32[2,128]{1,0:T(2,128)} %param.21) | copy-start | bytes 3076
  155.0 11.2 %all-to-all-start.5 = ((f32[32,1,384]{2,1,0:T(1,128)}), f32[32,1,384]{2,1,0:T(1,128)S(1)}, u32[]{:S(2)}, u32[]{:S(2)}) async-start(f32[32,1,384]{2,1,0:T(1,128)} %broadcast_in_dim.107), calls=%async_computation.5 | async-start | bytes 98304 | tf_op jit(solution)/shard_map/all_to_all | solution.py:125

commit v2 on v1

v2 whole, which is shorter than its diff:
```python
import jax
import jax.numpy as jnp
from jax import lax
from jax.experimental import pallas as pl
from jax.experimental.pallas import tpu as pltpu
from jax.sharding import PartitionSpec as P


SEQS = 4
PAIR = 2
HALVES = 2
LANES = 128
MIB = 1024 * 1024
VMEM = pl.BlockSpec(memory_space=pltpu.VMEM)
HBM = pl.BlockSpec(memory_space=pltpu.HBM)
ANY = pl.BlockSpec(memory_space=pl.ANY)
F32 = jnp.float32
BF16 = jnp.bfloat16


def call(kernel, outs, ins, specs, scratch=(), flops=1, vmem=32, moved=None):
    if moved is None:
        moved = sum(a.size * a.dtype.itemsize for a in ins)
    ins = [
        pltpu.with_memory_space_constraint(a, pltpu.HBM) if spec is HBM else a
        for a, spec in zip(ins, specs)
    ]
    return pl.pallas_call(
        kernel,
        out_shape=tuple(jax.ShapeDtypeStruct(shape, dtype) for shape, dtype in outs),
        in_specs=specs,
        out_specs=tuple(VMEM for _ in outs),
        scratch_shapes=scratch,
        compiler_params=pltpu.CompilerParams(vmem_limit_bytes=vmem * MIB),
        cost_estimate=pl.CostEstimate(flops=flops, bytes_accessed=moved, transcendentals=0),
    )(*ins)


def iota(shape, dim):
    return lax.broadcasted_iota(jnp.int32, shape, dim)


def dot(a, b, contract=(1, 0)):
    dims = (((contract[0],), (contract[1],)), ((), ()))
    return lax.dot_general(a, b, dims, preferred_element_type=F32)


def places_of(routes, cap):
    toks = routes[0].shape[0]
    lane = iota((toks, LANES), 1)
    named = jnp.zeros((toks, LANES), F32)
    for route in routes:
        named = named + (lane == route).astype(F32)
    earlier = (iota((toks, toks), 1) < iota((toks, toks), 0)).astype(BF16)
    ahead = dot(earlier, named.astype(BF16))
    places = []
    for k, route in enumerate(routes):
        slot = jnp.sum(jnp.where(lane == route, ahead, 0.0), 1, keepdims=True).astype(jnp.int32)
        for other in routes[:k]:
            slot = slot + (other == route).astype(jnp.int32)
        places.append(route * cap + slot)
    return places


def columns(table, start, batches, tops, batch):
    out = []
    for k in range(tops):
        if isinstance(batch, int):
            col = start + batch * tops + k
            out.append(table[:, col : col + 1].astype(jnp.int32))
            continue
        taken = table[:, start + k : start + k + 1]
        for m in range(1, batches):
            col = start + m * tops + k
            taken = jnp.where(batch == m, table[:, col : col + 1], taken)
        out.append(taken.astype(jnp.int32))
    return out


def prep_kernel(dims, *refs):
    sources, head_hbm, refs = refs[:5], refs[5], refs[6:]
    packed_ref, small_ref, states_ref, early_ref = refs[:4]
    held, sems = refs[4:9], refs[9]
    hidden_ref, gain_ref, router_ref, route_ref, final_ref = held
    copies = [pltpu.make_async_copy(*pair, sems.at[i]) for i, pair in enumerate(zip(sources, held))]
    copy = pltpu.make_async_copy(head_hbm.at[pl.ds(0, early_ref.shape[0])], early_ref, sems.at[5])
    for each in copies + [copy]:
        each.start()
    for each in copies:
        each.wait()
    batches, toks, width, experts, splits, tops, cap = dims
    wide = width // HALVES
    batch = lax.axis_index("section") % batches
    count = packed_ref.shape[0]
    lane = iota((toks, count), 1)
    lane_place = lane // (splits * batches * cap) * cap + lane % cap
    lane_batch = lane // cap % batches
    picks, normed = [], []
    own = hidden_ref[0]
    eye = (iota((toks, toks), 0) == iota((toks, toks), 1)).astype(F32)
    table = jnp.concatenate(
        [dot(eye, route_ref[m].astype(F32), (1, 1)) for m in range(batches)]
        + [jnp.zeros((toks, LANES - batches * tops), F32)],
        1,
    )
    for m in range(batches):
        hidden = hidden_ref[m]
        values = hidden.astype(F32)
        factor = lax.rsqrt(jnp.mean(values * values, -1, keepdims=True) + 1e-06)
        normed.append((values * factor * gain_ref[...]).astype(BF16))
        hit = jnp.zeros((toks, count), F32)
        for place in places_of(columns(table, 0, batches, tops, m), cap):
            hit = hit + ((lane_place == place) & (lane_batch == m)).astype(F32)
        picks.append(hit.astype(BF16))
        if m:
            own = jnp.where(batch == m, hidden, own)
    packed = dot(jnp.concatenate(picks, 0), jnp.concatenate(normed, 0), (0, 0))
    packed_ref[...] = packed.astype(BF16)
    small_ref[...] = jnp.zeros_like(small_ref)
    small_ref[0:1, 0:width] = gain_ref[...]
    small_ref[1 : 1 + experts, 0:width] = router_ref[...].astype(F32)
    small_ref[1 + experts : 2 + experts, 0:width] = final_ref[...][None, :]
    small_ref[0:toks, width:] = table
    for half in range(HALVES):
        states_ref[half * toks : (half + 1) * toks, :] = own[:, half * wide : (half + 1) * wide]
    copy.wait()


def prep(dims, table_rows, early, hidden_in, layer_gain, router, routing, final_gain, head):
    batches, toks, width, experts, splits, _, cap = dims
    arrays = (
        hidden_in,
        layer_gain,
        router[0].T,
        routing[0].transpose(0, 2, 1),
        final_gain,
    )
    return call(
        lambda *refs: prep_kernel(dims, *refs),
        [
            ((experts * splits * batches * cap, width), BF16),
            ((table_rows, width + LANES), F32),
            ((HALVES * toks, width // HALVES), BF16),
            ((early, width), BF16),
        ],
        (*arrays, head),
        [HBM] * 6,
        [pltpu.VMEM(a.shape, a.dtype) for a in arrays] + [pltpu.SemaphoreType.DMA((6,))],
    )


def plan(dims, layer, states, shifted, sections):
    batches, toks, width, experts, splits, tops, cap = dims
    wide = width // HALVES
    section = lax.axis_index("section")
    table = pick_layer(shifted, section, layer, sections)
    routes = columns(table[:toks, width:], 0, batches, tops, section % batches)
    places = places_of(routes, cap)
    values = [states[h * toks : (h + 1) * toks].astype(F32) for h in range(HALVES)]
    square = sum(jnp.sum(v * v, -1, keepdims=True) for v in values)
    factor = lax.rsqrt(square / width + 1e-06)
    logits = 0.0
    for half in range(HALVES):
        cols = slice(half * wide, (half + 1) * wide)
        normed = (values[half] * factor * table[0:1, cols]).astype(BF16)
        logits = logits + dot(normed, table[:, cols].astype(BF16), (1, 1))
    lane = iota(logits.shape, 1)
    scores = [
        jax.nn.sigmoid(jnp.sum(jnp.where(lane == route + 1, logits, 0.0), 1, keepdims=True))
        for route in routes
    ]
    whole = sum(scores)
    count = experts * splits * HALVES * cap
    row = iota((toks, count), 1)
    row_place = row // (splits * HALVES * cap) * cap + row % cap
    row_half = row // cap % HALVES
    mix = jnp.zeros((toks, count), F32)
    for score, place in zip(scores, places):
        mix = mix + jnp.where(row_place == place, 2.5 * (score / whole), 0.0)
    return [jnp.where(row_half == half, mix, 0.0) for half in range(HALVES)]


def pick_layer(shifted, section, layer, sections):
    shift = (section - layer + sections) % sections
    table = shifted[0]
    for k in range(1, sections):
        table = jnp.where(shift == k, shifted[k], table)
    return table


def next_pack(dims, layer, shifted, sections, pack_ref, gain_ref):
    batches, toks, width, experts, splits, tops, cap = dims
    wide = width // HALVES
    section = lax.axis_index("section")
    table = pick_layer(shifted, section, layer, sections)
    routes = columns(table[:toks, width:], 0, batches, tops, section % batches)
    count = pack_ref.shape[1]
    row = iota((toks, count), 1)
    row_place = row // (splits * HALVES * cap) % experts * cap + row % cap
    row_half = row // cap % HALVES
    hit = jnp.zeros((toks, count), F32)
    for place in places_of(routes, cap):
        hit = hit + (row_place == place).astype(F32)
    for half in range(HALVES):
        flags = jnp.where(row_half == half, hit, 0.0)
        pack_ref[half * toks : (half + 1) * toks, :] = flags.astype(BF16)
        gain_ref[half : half + 1, :] = table[0:1, half * wide : (half + 1) * wide]


def ffn_kernel(dims, layer, sections, chunks, *refs):
    batches, toks, width, experts, _, _, cap = dims
    last = layer == sections - 1
    near_ref, far_ref, gate_hbm, up_hbm, down_hbm, head_hbm, states_ref = refs[:7]
    shifted_refs, refs = refs[7 : 7 + sections], refs[7 + sections :]
    keep_ref, send_ref, mix_ref = refs[:3]
    refs = refs[3:]
    gain_ref, extra_ref, refs = refs[0], refs[1], refs[2:]
    gate_ref, up_ref, down_ref, sems = refs
    split = layer > 0
    count, wide = keep_ref.shape
    rows = count // HALVES
    groups = rows // (batches * cap)
    depth = width // chunks

    copies = []
    for c in range(chunks):
        part = pl.ds(c * depth, depth)
        copies.append(pltpu.make_async_copy(gate_hbm.at[part], gate_ref.at[part], sems.at[2 * c]))
        copies.append(pltpu.make_async_copy(up_hbm.at[part], up_ref.at[part], sems.at[2 * c + 1]))
    for half in range(HALVES):
        part = pl.ds(half * wide, wide)
        copies.append(
            pltpu.make_async_copy(down_hbm.at[:, part], down_ref.at[:, part], sems.at[2 * chunks + half])
        )
    if last:
        late = extra_ref.shape[0]
        rest = pl.ds(head_hbm.shape[0] - late, late)
        copies.append(pltpu.make_async_copy(head_hbm.at[rest], extra_ref, sems.at[2 * chunks + HALVES]))
    for copy in copies:
        copy.start()

    shifted = [ref[...] for ref in shifted_refs]
    for half, mix in enumerate(plan(dims, layer, states_ref[...], shifted, sections)):
        high = mix.astype(BF16)
        mix_ref[half * toks : (half + 1) * toks, :] = high
        low = (mix - high.astype(F32)).astype(BF16)
        mix_ref[(HALVES + half) * toks : (HALVES + half + 1) * toks, :] = low
    if last:
        for half in range(HALVES):
            cols = slice(half * wide, (half + 1) * wide)
            gain_ref[half : half + 1, :] = shifted[0][1 + experts : 2 + experts, cols]
    else:
        next_pack(dims, layer + 1, shifted, sections, extra_ref, gain_ref)

    def whole(ref):
        if not split:
            return ref[...]
        row, col = iota((rows, count), 0), iota((rows, count), 1)
        parts = []
        for half in range(HALVES):
            pick = row // cap * (HALVES * cap) + half * cap + row % cap == col
            parts.append(dot(pick.astype(BF16), ref[...]).astype(BF16))
        return jnp.concatenate(parts, 1)

    row, col = iota((count, rows), 0), iota((count, rows), 1)
    slot, block, side = row % cap, row // (HALVES * cap), row // cap % HALVES
    if split:
        source = block * cap + slot
    else:
        source = (block % groups * batches + block // groups) * cap + slot

    data = jnp.concatenate([whole(near_ref), whole(far_ref)], 0)
    gate_val = up_val = 0.0
    for c in range(chunks):
        copies[2 * c].wait()
        copies[2 * c + 1].wait()
        part = slice(c * depth, (c + 1) * depth)
        gate_val = gate_val + dot(data[:, part], gate_ref[part, :])
        up_val = up_val + dot(data[:, part], up_ref[part, :])
    inner = (gate_val / (1.0 + jnp.exp(-gate_val)) * up_val).astype(BF16)
    keep = send = 0.0
    for half in range(HALVES):
        copies[2 * chunks + half].wait()
        part = dot(inner, down_ref[:, half * wide : (half + 1) * wide]).astype(BF16)
        pick = ((source == col) & (side == half)).astype(BF16)
        send = send + dot(pick, part[rows:])
        keep = keep + dot(pick, part[:rows])
    send_ref[...] = send.astype(BF16)
    keep_ref[...] = keep.astype(BF16)
    for copy in copies[2 * chunks + HALVES :]:
        copy.wait()


def ffn(dims, layer, sections, near, far, gate, up, down, head, early, states, shifted):
    batches, toks, width, experts, splits, _, cap = dims
    hidden = gate.shape[1]
    wide = width // HALVES
    back = experts * splits * HALVES * cap
    count = batches * back
    chunks = 4
    outs = [((count, wide), BF16), ((count, wide), BF16), ((2 * HALVES * toks, back), BF16)]
    outs.append(((HALVES, wide), F32))
    if layer < sections - 1:
        outs.append(((HALVES * toks, sections * back), BF16))
    else:
        outs.append(((head.shape[0] - early, width), BF16))
    ins = (near, far, gate, up, down, head, states, *shifted)
    specs = [VMEM, VMEM, HBM, HBM, HBM, HBM] + [VMEM] * (1 + sections)
    scratch = [
        pltpu.VMEM((width, hidden), BF16),
        pltpu.VMEM((width, hidden), BF16),
        pltpu.VMEM((hidden, width), BF16),
        pltpu.SemaphoreType.DMA((2 * chunks + HALVES + 1,)),
    ]
    return call(
        lambda *refs: ffn_kernel(dims, layer, sections, chunks, *refs),
        outs,
        ins,
        specs,
        scratch,
        flops=6 * count * width * hidden,
    )


def head_kernel(batches, early, near_ref, far_ref, target_ref, *refs):
    others = batches - 1
    sources, refs = refs[: 1 + 2 * others], refs[1 + 2 * others :]
    out_ref, table_ref, sems = refs
    vocab = sources[0].shape[0]
    section, member = lax.axis_index("section"), lax.axis_index("expert")
    members = lax.axis_size("expert")
    batch = section % batches
    copies, spot = [], 0
    for i, source in enumerate(sources):
        size = source.shape[0]
        copies.append(pltpu.make_async_copy(source, table_ref.at[pl.ds(spot, size)], sems.at[i]))
        spot += size
    for copy in copies:
        copy.start()

    toks = near_ref.shape[0] + far_ref.shape[0]
    each = toks // members
    col = iota((toks, toks), 1)
    core = (col // (toks // PAIR) + member) % PAIR
    moved = iota((toks, toks), 0) == (col // each % (members // PAIR) * PAIR + core) * each + col % each
    moved = moved.astype(F32)
    ids = target_ref[...].astype(F32)
    target = ids[0:1]
    for m in range(1, batches):
        target = jnp.where(batch == m, ids[m : m + 1], target)
    exact = lax.Precision.HIGHEST
    target = jnp.broadcast_to(target, (8, toks))
    target = jnp.dot(target, moved, precision=exact, preferred_element_type=F32)[0:1].astype(jnp.int32)

    rows = jnp.concatenate([near_ref[...], far_ref[...]], 0)
    for copy in copies[1:]:
        copy.wait()
    after = dot(table_ref[vocab:, :], rows, (1, 1))
    copies[0].wait()
    blocks, spot = [(dot(table_ref[:vocab, :], rows, (1, 1)), (section * members + member) * vocab)], 0
    for i, source in enumerate(sources[1:]):
        size = source.shape[0]
        shift = i % others + 1
        owner = section - batch + (batch - shift + batches) % batches
        start = (owner * members + member) * vocab + (early if i >= others else 0)
        blocks.append((after[spot : spot + size], start))
        spot += size
    peak = blocks[0][0].max(0, keepdims=True)
    for block, _ in blocks[1:]:
        peak = jnp.maximum(peak, block.max(0, keepdims=True))
    total = hit = 0.0
    for block, start in blocks:
        total = total + jnp.sum(jnp.exp(block - peak), 0, keepdims=True)
        hit = hit + jnp.sum(jnp.where(iota(block.shape, 0) + start == target, block, 0.0), 0, keepdims=True)
    both = jnp.concatenate([peak + jnp.log(total), hit, jnp.zeros((6, toks), F32)], 0)
    both = lax.dot_general(
        both, moved, (((1,), (1,)), ((), ())), precision=exact, preferred_element_type=F32
    )
    out = jnp.concatenate([both[0:1], both[1:2]], 1)
    out_ref[...] = jnp.broadcast_to(out[None], out_ref.shape)


def final_kernel(batches, toks, stats_ref, seq_ref, token_ref, mean_ref):
    member = lax.axis_index("expert")
    members = lax.axis_size("expert")
    sections = lax.axis_size("section")
    count = members * toks
    stats = stats_ref[:, 0, :]
    spot = member * toks
    lane = iota((1, count), 1)
    seat = iota((1, SEQS), 1)
    for m in range(batches):
        rows = [stats[s * members : (s + 1) * members] for s in range(m, sections, batches)]
        rows = rows[0] if len(rows) == 1 else jnp.concatenate(rows, 0)
        local, hits = rows[:, :count], rows[:, count:]
        peak = jnp.max(local, 0, keepdims=True)
        lse = peak + jnp.log(jnp.sum(jnp.exp(local - peak), 0, keepdims=True))
        logprob = jnp.sum(hits, 0, keepdims=True) - lse
        ids = seq_ref[m : m + 1, :]
        means = jnp.zeros((1, SEQS), F32)
        for s in range(SEQS):
            inside = ids == s
            summed = jnp.sum(jnp.where(inside, logprob, 0.0), 1, keepdims=True)
            size = jnp.sum(jnp.where(inside, 1.0, 0.0), 1, keepdims=True)
            means = jnp.where(seat == s, summed / size, means)
        mean_ref[m : m + 1, :] = means
        mine = pltpu.roll(logprob, count - spot, 1)
        token_ref[m : m + 1, :] = mine[:, :toks]


def body(
    hidden_in, layer_gain, router, w_gate, w_up, w_down, final_gain, head, routing, targets, seq_ids
):
    batches, toks, width = hidden_in.shape
    experts = router.shape[2]
    tops = routing.shape[3]
    sections = lax.axis_size("section")
    members = lax.axis_size("expert")
    splits = members // experts // PAIR
    groups = members // PAIR
    cap = min(toks, 9 * toks * tops // (8 * experts))
    wide = width // HALVES
    dims = (batches, toks, width, experts, splits, tops, cap)
    same_core = [[g * PAIR + c for g in range(groups)] for c in range(PAIR)]
    same_core_all = [
        [s * members + g * PAIR + c for s in range(sections) for g in range(groups)]
        for c in range(PAIR)
    ]
    partner = [(i, i ^ 1) for i in range(members)]

    def exchange(rows):
        return lax.all_to_all(
            rows, "expert", split_axis=0, concat_axis=0, axis_index_groups=same_core, tiled=True
        )

    def exchange_all(rows):
        return lax.all_to_all(
            rows,
            ("section", "expert"),
            split_axis=0,
            concat_axis=0,
            axis_index_groups=same_core_all,
            tiled=True,
        )

    def swap_core(rows):
        return lax.ppermute(rows, "expert", partner)

    def by_section(array, shift, across):
        return lax.ppermute(
            array,
            "section",
            [(s, s - s % across + (s + shift) % across) for s in range(sections)],
        )

    early = head.shape[0] * 5 // 8 // 16 * 16
    table_rows = max(-(-(2 + experts) // 8) * 8, toks)
    packed, small, states, early_head = prep(
        dims, table_rows, early, hidden_in, layer_gain, router, routing, final_gain, head
    )
    first_parts = []
    for shift in range(1, batches):
        first_parts.append(by_section(early_head, shift, batches))
    near = exchange(packed)

    shifted = [small]
    for shift in range(1, sections):
        shifted.append(by_section(small, shift, sections))

    size = groups * HALVES * cap
    for tick in range(sections):
        far = swap_core(near)
        keep, send, mixes, gain, extra = ffn(
            dims,
            tick,
            sections,
            near,
            far,
            w_gate[0],
            w_up[0],
            w_down[0],
            head,
            early,
            states,
            shifted,
        )
        total = (keep.astype(F32) + swap_core(send).astype(F32)).astype(BF16)
        if sections > batches:
            total = jnp.concatenate([total] * (sections // batches), 0)
        back = exchange_all(total)[tick * size : (tick + 1) * size]
        mixed = dot(mixes, back)
        states = states.astype(F32) + mixed[: HALVES * toks] + mixed[HALVES * toks :]
        states = states.astype(BF16)
        values = states.astype(F32).reshape(HALVES, toks, wide)
        factor = lax.rsqrt(jnp.sum(values * values, (0, 2), keepdims=True) / width + 1e-06)
        if tick == sections - 1:
            break
        normed = (values * factor * gain[:, None, :]).astype(BF16)
        packed = dot(extra, normed.reshape(HALVES * toks, wide), (0, 0)).astype(BF16)
        near = exchange_all(packed)
        if sections > batches:
            base = tick + 1 - (tick + 1) % batches
            near = near[base * size : (base + batches) * size]

    states, late_head = lax.optimization_barrier((states, extra))
    late_parts = []
    for shift in range(1, batches):
        late_parts.append(by_section(late_head, shift, batches))
    final = (values * factor * gain[:, None, :]).astype(BF16)
    final = jnp.concatenate([final[h] for h in range(HALVES)], 1)
    near = exchange(jnp.broadcast_to(final[None], (groups, toks, width)).reshape(groups * toks, width))
    far = swap_core(near)
    world = sections * members
    (stats,) = call(
        lambda *refs: head_kernel(batches, early, *refs),
        [((world, 1, 2 * members * toks), F32)],
        (near, far, targets, head, *first_parts, *late_parts),
        [VMEM] * 3 + [HBM] + [ANY] * (2 * batches - 2),
        [
            pltpu.VMEM((batches * head.shape[0], width), BF16),
            pltpu.SemaphoreType.DMA((2 * batches - 1,)),
        ],
        flops=4 * head.size * members * toks,
    )
    stats = lax.all_to_all(stats, ("section", "expert"), split_axis=0, concat_axis=0, tiled=True)
    return call(
        lambda *refs: final_kernel(batches, toks, *refs),
        [((batches, toks), F32), ((batches, SEQS), F32)],
        (stats, seq_ids),
        [VMEM] * 2,
    )


def solution(mesh):
    return jax.shard_map(
        body,
        mesh=mesh,
        in_specs=(
            P(None, "expert", None),
            P("section", None),
            P("section", None, None),
            P("section", None, "expert"),
            P("section", None, "expert"),
            P("section", "expert", None),
            P(),
            P(("section", "expert"), None),
            P("section", None, "expert", None),
            P(),
            P(),
        ),
        out_specs=(P(None, "expert"), P()),
        check_vma=False,
    )
```

time: 170 us -> 160 us (0.941)
  blocking collectives: 51.7 us -> 84.6 us
  matrix products: 20 us -> 0.65 us
  waiting for transfers between devices: 66.7 us -> 48.1 us
  Pallas kernels: 0 us -> 16.9 us
  starting transfers between devices: 18.8 us -> 7.33 us
  other arithmetic: 6.17 us -> 0.65 us
  local copies, waits for them, and re-layouts: 4.63 us -> 1.08 us
    all_to_all x0 -> x4, blocking collectives: none -> 64.3 us  [the longest x3 52.5 us: exchange_all(): lax.all_to_all(rows, ('section', 'expert'), split_axis=0, concat_axis=0,...]
    all_to_all x3 -> x1, blocking collectives: 51.7 us -> 20.3 us  [exchange(): lax.all_to_all(rows, 'expert', split_axis=0, concat_axis=0, axis_index_gr...]
    dot_general x14 -> x3, matrix products: 20 us -> 0.65 us  [dot(): return lax.dot_general(a, b, dims, preferred_element_type=F32)]
    pallas_call x0 -> x5, Pallas kernels: none -> 16.9 us  [call(): pl.pallas_call(kernel, out_shape=tuple((jax.ShapeDtypeStruct(shape, dtype...]
    all_to_all x2 -> x1, waiting for transfers between devices: 26.4 us -> 10.3 us  [exchange(): lax.all_to_all(rows, 'expert', split_axis=0, concat_axis=0, axis_index_gr...]
    ppermute x3, waiting for transfers between devices: 24.5 us -> 32.5 us  [by_section(): lax.ppermute(array, 'section', [(s, s - s % across + (s + shift) % across...]
    all_to_all x1 -> x0, waiting for transfers between devices: 7.33 us -> none  [body(): lax.all_to_all(jnp.broadcast_to(stats, (world, stats.shape[1])), ('sectio...]
    all_to_all x1 -> x0, starting transfers between devices: 3.88 us -> none  [body(): lax.all_to_all(jnp.broadcast_to(stats, (world, stats.shape[1])), ('sectio...]
  transfers between devices with their start and end apart: 11 -> 9, of which waited for: 11 -> 7; matrix products, arithmetic and copies ran while one was open for 1% -> 0% of each run, Pallas kernels for 0% -> 0%
where the time goes in v2:
time: 160 us
  blocking collectives  84.6 us (53%)
  waiting for transfers between devices  48.1 us (30%)
  Pallas kernels  16.9 us (11%)
  starting transfers between devices  7.33 us (5%)
    all_to_all x3, blocking collectives, exchange_all(): lax.all_to_all(rows, ('section', 'expert'), split_axis=0, concat_axis=0,...  52.5 us
    ppermute x3, waiting for transfers between devices, by_section(): lax.ppermute(array, 'section', [(s, s - s % across + (s + shift) % across...  32.5 us
    all_to_all x1, blocking collectives, exchange(): lax.all_to_all(rows, 'expert', split_axis=0, concat_axis=0, axis_index_gr...  20.3 us
    pallas_call x5, Pallas kernels, call(): pl.pallas_call(kernel, out_shape=tuple((jax.ShapeDtypeStruct(shape, dtype...  16.9 us
    all_to_all x1, blocking collectives, body(): lax.all_to_all(stats, ('section', 'expert'), split_axis=0, concat_axis=0,...  11.9 us
    all_to_all x1, waiting for transfers between devices, exchange(): lax.all_to_all(rows, 'expert', split_axis=0, concat_axis=0, axis_index_gr...  10.3 us
    ppermute x5, waiting for transfers between devices, swap_core(): return lax.ppermute(rows, 'expert', partner)  5.3 us
    ppermute x3, starting transfers between devices, by_section(): lax.ppermute(array, 'section', [(s, s - s % across + (s + shift) % across...  3.58 us
  transfers between devices with their start and end apart: 9, of which 7 were waited for; matrix products, arithmetic and copies ran while one was open for 0% of the time, Pallas kernels for 0%

profile of v2, /device:TPU:0, one launch (start us, length us, event | category | flops | bytes accessed | tf_op | source)
XLA Modules:
  0.0 160.1 jit_solution(16251782543069567890)
XLA Ops:
  0.6 1.9 %shard_map.122 = (bf16[64,3584]{1,0:T(8,128)(2,1)S(1)}, f32[8,3712]{1,0:T(8,128)S(1)}, bf16[16,1792]{1,0:T(8,128)(2,1)S(1)}, bf16[160,3584]{1,0:T(8,128)(2,1)S(1)}) custom-call(bf16[2,8,3584]{2,1,0:T(8,128)(2,1)} %refs_0_.1, f32[1,3584]{1,0:T(1,128)} %refs_1_.2, bf16[4,3584]{1,0:T(4,128)(2,1)} %bitcast.56, s32[2,2,8]{2,1,0:T(2,128)} %bitcast.57, ...), custom_call_target="tpu_custom_call" | custom-call | flops 1 | bytes 2007168 | tf_op jit(solution)/shard_map/pallas_call | solution.py:28
  2.5 20.3 %all_to_all.53 = bf16[8,8,3584]{2,1,0:T(8,128)(2,1)S(1)} all-to-all(bf16[8,8,3584]{2,1,0:T(8,128)(2,1)S(1)} %bitcast.49), channel_id=1, replica_groups={{0,2,4,6,8,10,12,14},{1,3,5,7,9,11,13,15},{16,18,20,22,24,26,28,30},{17..., dimensions={0} | all-to-all | bytes 917504 | tf_op jit(solution)/shard_map/all_to_all | solution.py:432
  22.8 0.0 collective-permute-start
  22.8 1.5 collective-permute-start.1
  24.3 4.2 %collective-permute-done.1.refs_8_ = f32[8,3712]{1,0:T(8,128)S(1)} collective-permute-done((f32[8,3712]{1,0:T(8,128)S(1)}, f32[8,3712]{1,0:T(8,128)S(1)}, u32[]{:S(2)}, u32[]{:S(2)}) %collective-permute-start.1) | collective-permute-done | bytes 118816 | tf_op jit(solution)/shard_map/ppermute | solution.py:450
  28.5 0.0 collective-permute-done.refs_1_
  28.5 5.4 %shard_map.123 = (bf16[128,1792]{1,0:T(8,128)(2,1)S(1)}, bf16[128,1792]{1,0:T(8,128)(2,1)S(1)}, bf16[32,64]{1,0:T(8,128)(2,1)S(1)}, f32[2,1792]{1,0:T(2,128)S(1)}, bf16[16,128]{1,0:T(8,128)(2,1)S(1)}) custom-call(bf16[64,3584]{1,0:T(8,128)(2,1)S(1)} %bitcast.46, bf16[64,3584]{1,0:T(8,128)(2,1)S(1)} %collective-permute-done.refs_1_, ...), custom_call_target="tpu_custom_call" | custom-call | flops 1409286144 | bytes 14057472 | tf_op jit(solution)/shard_map/pallas_call | solution.py:28
  33.8 0.1 collective-permute-start.2
  33.9 1.8 %collective-permute-done.2 = bf16[128,1792]{1,0:T(8,128)(2,1)S(1)} collective-permute-done((bf16[128,1792]{1,0:T(8,128)(2,1)S(1)}, bf16[128,1792]{1,0:T(8,128)(2,1)S(1)}, u32[]{:S(2)}, u32[]{:S(2)}) %collective-permute-start.2) | collective-permute-done | bytes 458784 | tf_op jit(solution)/shard_map/ppermute | solution.py:447
  35.7 0.1 fusion.1
  35.8 18.5 %all_to_all.54 = bf16[16,8,1792]{2,1,0:T(8,128)(2,1)S(1)} all-to-all(bf16[16,8,1792]{2,1,0:T(8,128)(2,1)S(1)} %fusion.1), channel_id=1, replica_groups={{0,2,4,6,8,10,12,14,16,18,20,22,24,26,28,30},{1,3,5,7,9,11,13,15,17,19,..., dimensions={0} | all-to-all | bytes 917504 | tf_op jit(solution)/shard_map/all_to_all | solution.py:437
  54.4 0.2 fusion.4
  54.5 0.1 fusion.9
  54.7 0.1 reduce_sum.24
  54.8 0.1 mul.50
  54.9 0.3 fusion
  55.2 16.5 %all_to_all.55 = bf16[16,8,1792]{2,1,0:T(8,128)(2,1)S(1)} all-to-all(bf16[16,8,1792]{2,1,0:T(8,128)(2,1)S(1)} %fusion), channel_id=1, replica_groups={{0,2,4,6,8,10,12,14,16,18,20,22,24,26,28,30},{1,3,5,7,9,11,13,15,17,19,..., dimensions={0} | all-to-all | bytes 917504 | tf_op jit(solution)/shard_map/all_to_all | solution.py:437
  71.7 0.0 collective-permute-start.3
  71.7 1.8 %collective-permute-done.3.refs_1_ = bf16[128,1792]{1,0:T(8,128)(2,1)S(1)} collective-permute-done((bf16[128,1792]{1,0:T(8,128)(2,1)S(1)}, bf16[128,1792]{1,0:T(8,128)(2,1)S(1)}, u32[]{:S(2)}, u32[]{:S(2)}) %collective-permute-start.3) | collective-permute-done | bytes 458784 | tf_op jit(solution)/shard_map/ppermute | solution.py:447
  73.5 5.8 %shard_map.124 = (bf16[128,1792]{1,0:T(8,128)(2,1)S(1)}, bf16[128,1792]{1,0:T(8,128)(2,1)S(1)}, bf16[32,64]{1,0:T(8,128)(2,1)S(1)}, f32[2,1792]{1,0:T(2,128)S(1)}, bf16[96,3584]{1,0:T(8,128)(2,1)S(1)}) custom-call(bf16[128,1792]{1,0:T(8,128)(2,1)S(1)} %bitcast.48, bf16[128,1792]{1,0:T(8,128)(2,1)S(1)} %collective-permute-done.3.refs_1_, ...), custom_call_target="tpu_custom_call" | custom-call | flops 1409286144 | bytes 14057472 | tf_op jit(solution)/shard_map/pallas_call | solution.py:28
  79.3 0.0 copy-start.2
  79.3 0.0 copy-start
  79.3 0.2 collective-permute-start.4
  79.5 1.7 %collective-permute-done.4 = bf16[128,1792]{1,0:T(8,128)(2,1)S(1)} collective-permute-done((bf16[128,1792]{1,0:T(8,128)(2,1)S(1)}, bf16[128,1792]{1,0:T(8,128)(2,1)S(1)}, u32[]{:S(2)}, u32[]{:S(2)}) %collective-permute-start.4) | collective-permute-done | bytes 458784 | tf_op jit(solution)/shard_map/ppermute | solution.py:447
  81.2 0.1 fusion.2
  81.3 17.4 %all_to_all.56 = bf16[16,8,1792]{2,1,0:T(8,128)(2,1)S(1)} all-to-all(bf16[16,8,1792]{2,1,0:T(8,128)(2,1)S(1)} %fusion.2), channel_id=1, replica_groups={{0,2,4,6,8,10,12,14,16,18,20,22,24,26,28,30},{1,3,5,7,9,11,13,15,17,19,..., dimensions={0} | all-to-all | bytes 917504 | tf_op jit(solution)/shard_map/all_to_all | solution.py:437
  98.7 0.0 copy-start.1
  98.7 0.2 fusion.3
  98.9 0.1 fusion.8
  99.0 0.0 copy-done.2
  99.0 0.1 reduce_sum.36
  99.1 0.1 fusion.7
  99.3 0.8 broadcast_in_dim.2
  100.1 3.5 %all-to-all-start.4 = ((bf16[8,8,3584]{2,1,0:T(8,128)(2,1)}), bf16[8,8,3584]{2,1,0:T(8,128)(2,1)S(1)}, u32[]{:S(2)}, u32[]{:S(2)}) async-start(bf16[8,8,3584]{2,1,0:T(8,128)(2,1)} %broadcast_in_dim.2), calls=%async_computation.4 | async-start | bytes 917504 | tf_op jit(solution)/shard_map/all_to_all | solution.py:432
  103.6 1.2 collective-permute-start.6
  104.8 0.9 collective-permute-start.7
  105.6 10.3 %all-to-all-done.4 = bf16[8,8,3584]{2,1,0:T(8,128)(2,1)S(1)} async-done(((bf16[8,8,3584]{2,1,0:T(8,128)(2,1)}), bf16[8,8,3584]{2,1,0:T(8,128)(2,1)S(1)}, u32[]{:S(2)}, u32[]{:S(2)}) %all-to-all-start.4) | async-done | bytes 458784 | tf_op jit(solution)/shard_map/all_to_all | solution.py:432
  115.9 0.0 collective-permute-start.5
  115.9 15.9 %collective-permute-done.6.refs_4_ = bf16[160,3584]{1,0:T(8,128)(2,1)S(1)} collective-permute-done((bf16[160,3584]{1,0:T(8,128)(2,1)S(1)}, bf16[160,3584]{1,0:T(8,128)(2,1)S(1)}, u32[]{:S(2)}, u32[]{:S(2)}) %collective-permute-start.6) | collective-permute-done | bytes 1146912 | tf_op jit(solution)/shard_map/ppermute | solution.py:450
  131.8 12.5 %collective-permute-done.7.refs_5_ = bf16[96,3584]{1,0:T(8,128)(2,1)S(1)} collective-permute-done((bf16[96,3584]{1,0:T(8,128)(2,1)}, bf16[96,3584]{1,0:T(8,128)(2,1)S(1)}, u32[]{:S(2)}, u32[]{:S(2)}) %collective-permute-start.7) | collective-permute-done | bytes 688160 | tf_op jit(solution)/shard_map/ppermute | solution.py:450
  144.2 0.0 collective-permute-done.5.refs_1_
  144.3 0.0 copy-done
  144.3 3.2 %shard_map.125 = f32[32,1,256]{2,1,0:T(1,128)S(1)} custom-call(bf16[64,3584]{1,0:T(8,128)(2,1)S(1)} %bitcast.44, bf16[64,3584]{1,0:T(8,128)(2,1)S(1)} %collective-permute-done.5.refs_1_, s32[2,128]{1,0:T(2,128)S(1)} %copy-done, bf16[256,3584]{1,0:T(8,128)(2,1)} %refs_3_.1, bf16[160,3584]{1,0:T(8,128)(2,1)S(1)} %collective-permute-done.6.refs_4_, ...), custom_call_target="tpu_custom_call" | custom-call | flops 469762048 | bytes 4588544 | tf_op jit(solution)/shard_map/pallas_call | solution.py:28
  147.5 11.9 %all_to_all.57.refs_0_ = f32[32,1,256]{2,1,0:T(1,128)S(1)} all-to-all(f32[32,1,256]{2,1,0:T(1,128)S(1)} %shard_map.125), channel_id=1, replica_groups=mesh['section'=2,'expert'=16] {'section','expert'}, dimensions={0} | all-to-all | bytes 65536 | tf_op jit(solution)/shard_map/all_to_all | solution.py:525
  159.4 0.0 copy-done.1
  159.4 0.7 shard_map.126
  (7 shorter events, 0.1 us)
Async XLA Ops:
  22.8 5.7 %collective-permute-start = (bf16[64,3584]{1,0:T(8,128)(2,1)S(1)}, bf16[64,3584]{1,0:T(8,128)(2,1)S(1)}, u32[]{:S(2)}, u32[]{:S(2)}) collective-permute-start(bf16[64,3584]{1,0:T(8,128)(2,1)S(1)} %bitcast.45), channel_id=1, source_target_pairs={{0,1},{1,0},{2,3},{3,2},{4,5},{5,4},{6,7},{7,6},{8,9},{9,8},{10,11... | collective-permute-start | bytes 1376264 | tf_op jit(solution)/shard_map/ppermute | solution.py:447
  22.8 5.6 %collective-permute-start.1 = (f32[8,3712]{1,0:T(8,128)S(1)}, f32[8,3712]{1,0:T(8,128)S(1)}, u32[]{:S(2)}, u32[]{:S(2)}) collective-permute-start(f32[8,3712]{1,0:T(8,128)S(1)} %get-tuple-element.19.refs_7_), channel_id=1, source_target_pairs={{0,16},{16,0},{1,17},{17,1},{2,18},{18,2},{3,19},{19,3},{4,20},{20... | collective-permute-start | bytes 356360 | tf_op jit(solution)/shard_map/ppermute | solution.py:450
  33.8 1.9 %collective-permute-start.2 = (bf16[128,1792]{1,0:T(8,128)(2,1)S(1)}, bf16[128,1792]{1,0:T(8,128)(2,1)S(1)}, u32[]{:S(2)}, u32[]{:S(2)}) collective-permute-start(bf16[128,1792]{1,0:T(8,128)(2,1)S(1)} %get-tuple-element.22), channel_id=1, source_target_pairs={{0,1},{1,0},{2,3},{3,2},{4,5},{5,4},{6,7},{7,6},{8,9},{9,8},{10,11... | collective-permute-start | bytes 1376264 | tf_op jit(solution)/shard_map/ppermute | solution.py:447
  71.7 1.8 %collective-permute-start.3 = (bf16[128,1792]{1,0:T(8,128)(2,1)S(1)}, bf16[128,1792]{1,0:T(8,128)(2,1)S(1)}, u32[]{:S(2)}, u32[]{:S(2)}) collective-permute-start(bf16[128,1792]{1,0:T(8,128)(2,1)S(1)} %bitcast.47), channel_id=1, source_target_pairs={{0,1},{1,0},{2,3},{3,2},{4,5},{5,4},{6,7},{7,6},{8,9},{9,8},{10,11... | collective-permute-start | bytes 1376264 | tf_op jit(solution)/shard_map/ppermute | solution.py:447
  79.3 19.7 %copy-start.2 = (bf16[96,3584]{1,0:T(8,128)(2,1)}, bf16[96,3584]{1,0:T(8,128)(2,1)S(1)}, u32[]{:S(2)}) copy-start(bf16[96,3584]{1,0:T(8,128)(2,1)S(1)} %get-tuple-element.31) | copy-start | bytes 2064388
  79.3 65.0 %copy-start = (s32[2,128]{1,0:T(2,128)S(1)}, s32[2,128]{1,0:T(2,128)}, u32[]{:S(2)}) copy-start(s32[2,128]{1,0:T(2,128)} %refs_2_.1) | copy-start | bytes 3076
  79.3 1.9 %collective-permute-start.4 = (bf16[128,1792]{1,0:T(8,128)(2,1)S(1)}, bf16[128,1792]{1,0:T(8,128)(2,1)S(1)}, u32[]{:S(2)}, u32[]{:S(2)}) collective-permute-start(bf16[128,1792]{1,0:T(8,128)(2,1)S(1)} %get-tuple-element.27), channel_id=1, source_target_pairs={{0,1},{1,0},{2,3},{3,2},{4,5},{5,4},{6,7},{7,6},{8,9},{9,8},{10,11... | collective-permute-start | bytes 1376264 | tf_op jit(solution)/shard_map/ppermute | solution.py:447
  98.7 60.6 %copy-start.1 = (s32[2,128]{1,0:T(2,128)S(1)}, s32[2,128]{1,0:T(2,128)}, u32[]{:S(2)}) copy-start(s32[2,128]{1,0:T(2,128)} %refs_1_.3) | copy-start | bytes 3076
  100.1 15.8 %all-to-all-start.4 = ((bf16[8,8,3584]{2,1,0:T(8,128)(2,1)}), bf16[8,8,3584]{2,1,0:T(8,128)(2,1)S(1)}, u32[]{:S(2)}, u32[]{:S(2)}) async-start(bf16[8,8,3584]{2,1,0:T(8,128)(2,1)} %broadcast_in_dim.2), calls=%async_computation.4 | async-start | bytes 917504 | tf_op jit(solution)/shard_map/all_to_all | solution.py:432
  103.6 28.2 %collective-permute-start.6 = (bf16[160,3584]{1,0:T(8,128)(2,1)S(1)}, bf16[160,3584]{1,0:T(8,128)(2,1)S(1)}, u32[]{:S(2)}, u32[]{:S(2)}) collective-permute-start(bf16[160,3584]{1,0:T(8,128)(2,1)S(1)} %get-tuple-element.29), channel_id=1, source_target_pairs={{0,16},{16,0},{1,17},{17,1},{2,18},{18,2},{3,19},{19,3},{4,20},{20... | collective-permute-start | bytes 3440648 | tf_op jit(solution)/shard_map/ppermute | solution.py:450
  104.8 39.5 %collective-permute-start.7 = (bf16[96,3584]{1,0:T(8,128)(2,1)}, bf16[96,3584]{1,0:T(8,128)(2,1)S(1)}, u32[]{:S(2)}, u32[]{:S(2)}) collective-permute-start(bf16[96,3584]{1,0:T(8,128)(2,1)} %copy-done.2), channel_id=1, source_target_pairs={{0,16},{16,0},{1,17},{17,1},{2,18},{18,2},{3,19},{19,3},{4,20},{20... | collective-permute-start | bytes 2064392 | tf_op jit(solution)/shard_map/ppermute | solution.py:450
  115.9 28.4 %collective-permute-start.5 = (bf16[64,3584]{1,0:T(8,128)(2,1)S(1)}, bf16[64,3584]{1,0:T(8,128)(2,1)S(1)}, u32[]{:S(2)}, u32[]{:S(2)}) collective-permute-start(bf16[64,3584]{1,0:T(8,128)(2,1)S(1)} %bitcast.43), channel_id=1, source_target_pairs={{0,1},{1,0},{2,3},{3,2},{4,5},{5,4},{6,7},{7,6},{8,9},{9,8},{10,11... | collective-permute-start | bytes 1376264 | tf_op jit(solution)/shard_map/ppermute | solution.py:447

commit v3 on v2

--- a/solution.py
+++ b/solution.py
@@ -27,7 +27,9 @@
     ]
     return pl.pallas_call(
         kernel,
-        out_shape=tuple(jax.ShapeDtypeStruct(shape, dtype) for shape, dtype in outs),
+        out_shape=tuple(
+            pltpu.VMEM(*out[:2]) if out[2:] else jax.ShapeDtypeStruct(*out) for out in outs
+        ),
         in_specs=specs,
         out_specs=tuple(VMEM for _ in outs),
         scratch_shapes=scratch,
@@ -88,12 +90,12 @@
         each.start()
     for each in copies:
         each.wait()
-    batches, toks, width, experts, splits, tops, cap = dims
+    batches, toks, width, experts, _, tops, cap = dims
     wide = width // HALVES
     batch = lax.axis_index("section") % batches
     count = packed_ref.shape[0]
     lane = iota((toks, count), 1)
-    lane_place = lane // (splits * batches * cap) * cap + lane % cap
+    lane_place = lane // (batches * cap) * cap + lane % cap
     lane_batch = lane // cap % batches
     picks, normed = [], []
     own = hidden_ref[0]
@@ -127,7 +129,7 @@
 
 
 def prep(dims, table_rows, early, hidden_in, layer_gain, router, routing, final_gain, head):
-    batches, toks, width, experts, splits, _, cap = dims
+    batches, toks, width, experts, _, _, cap = dims
     arrays = (
         hidden_in,
         layer_gain,
@@ -138,7 +140,7 @@
     return call(
         lambda *refs: prep_kernel(dims, *refs),
         [
-            ((experts * splits * batches * cap, width), BF16),
+            ((experts * batches * cap, width), BF16),
             ((table_rows, width + LANES), F32),
             ((HALVES * toks, width // HALVES), BF16),
             ((early, width), BF16),
@@ -189,14 +191,14 @@
 
 
 def next_pack(dims, layer, shifted, sections, pack_ref, gain_ref):
-    batches, toks, width, experts, splits, tops, cap = dims
+    batches, toks, width, experts, _, tops, cap = dims
     wide = width // HALVES
     section = lax.axis_index("section")
     table = pick_layer(shifted, section, layer, sections)
     routes = columns(table[:toks, width:], 0, batches, tops, section % batches)
     count = pack_ref.shape[1]
     row = iota((toks, count), 1)
-    row_place = row // (splits * HALVES * cap) % experts * cap + row % cap
+    row_place = row // (HALVES * cap) % experts * cap + row % cap
     row_half = row // cap % HALVES
     hit = jnp.zeros((toks, count), F32)
     for place in places_of(routes, cap):
@@ -207,35 +209,21 @@
         gain_ref[half : half + 1, :] = table[0:1, half * wide : (half + 1) * wide]
 
 
-def ffn_kernel(dims, layer, sections, chunks, *refs):
-    batches, toks, width, experts, _, _, cap = dims
+def ready_kernel(dims, layer, sections, *refs):
+    _, toks, width, experts, _, _, _ = dims
     last = layer == sections - 1
-    near_ref, far_ref, gate_hbm, up_hbm, down_hbm, head_hbm, states_ref = refs[:7]
-    shifted_refs, refs = refs[7 : 7 + sections], refs[7 + sections :]
-    keep_ref, send_ref, mix_ref = refs[:3]
-    refs = refs[3:]
-    gain_ref, extra_ref, refs = refs[0], refs[1], refs[2:]
-    gate_ref, up_ref, down_ref, sems = refs
-    split = layer > 0
-    count, wide = keep_ref.shape
-    rows = count // HALVES
-    groups = rows // (batches * cap)
-    depth = width // chunks
-
-    copies = []
-    for c in range(chunks):
-        part = pl.ds(c * depth, depth)
-        copies.append(pltpu.make_async_copy(gate_hbm.at[part], gate_ref.at[part], sems.at[2 * c]))
-        copies.append(pltpu.make_async_copy(up_hbm.at[part], up_ref.at[part], sems.at[2 * c + 1]))
-    for half in range(HALVES):
-        part = pl.ds(half * wide, wide)
-        copies.append(
-            pltpu.make_async_copy(down_hbm.at[:, part], down_ref.at[:, part], sems.at[2 * chunks + half])
-        )
-    if last:
-        late = extra_ref.shape[0]
+    wide = width // HALVES
+    weights, head_hbm, states_ref = refs[:3], refs[3], refs[4]
+    shifted_refs, refs = refs[5 : 5 + sections], refs[5 + sections :]
+    mix_ref, gain_ref, refs = refs[0], refs[1], refs[2:]
+    if not last:
+        pack_ref, refs = refs[0], refs[1:]
+    held, sems = refs[:3], refs[-1]
+    copies = [pltpu.make_async_copy(*pair, sems.at[i]) for i, pair in enumerate(zip(weights, held))]
+    if layer == 0:
+        late = refs[3].shape[0]
         rest = pl.ds(head_hbm.shape[0] - late, late)
-        copies.append(pltpu.make_async_copy(head_hbm.at[rest], extra_ref, sems.at[2 * chunks + HALVES]))
+        copies.append(pltpu.make_async_copy(head_hbm.at[rest], refs[3], sems.at[len(weights)]))
     for copy in copies:
         copy.start()
 
@@ -250,12 +238,44 @@
             cols = slice(half * wide, (half + 1) * wide)
             gain_ref[half : half + 1, :] = shifted[0][1 + experts : 2 + experts, cols]
     else:
-        next_pack(dims, layer + 1, shifted, sections, extra_ref, gain_ref)
+        next_pack(dims, layer + 1, shifted, sections, pack_ref, gain_ref)
+
+    for copy in copies:
+        copy.wait()
+
+
+def ready(dims, layer, sections, weights, head, early, states, shifted):
+    _, toks, width, experts, splits, _, cap = dims
+    back = experts * splits * HALVES * cap
+    outs = [((2 * HALVES * toks, back), BF16), ((HALVES, width // HALVES), F32)]
+    if layer < sections - 1:
+        outs.append(((HALVES * toks, sections * experts * HALVES * cap), BF16))
+    outs += [(weight.shape, BF16, True) for weight in weights]
+    if layer == 0:
+        outs.append(((head.shape[0] - early, width), BF16))
+    return call(
+        lambda *refs: ready_kernel(dims, layer, sections, *refs),
+        outs,
+        (*weights, head, states, *shifted),
+        [HBM] * 4 + [VMEM] * (1 + sections),
+        [pltpu.SemaphoreType.DMA((4,))],
+    )
+
+
+def expert_kernel(dims, split, *refs):
+    batches, _, _, experts, splits, _, cap = dims
+    sources, refs = refs[: PAIR * splits], refs[PAIR * splits :]
+    gate_ref, up_ref, down_ref, keep_ref, send_ref = refs
+    count, wide = keep_ref.shape
+    rows = count // HALVES
+    each = rows // splits
+    place = lax.axis_index("expert") // PAIR % splits
 
     def whole(ref):
         if not split:
             return ref[...]
-        row, col = iota((rows, count), 0), iota((rows, count), 1)
+        shape = (each, HALVES * each)
+        row, col = iota(shape, 0), iota(shape, 1)
         parts = []
         for half in range(HALVES):
             pick = row // cap * (HALVES * cap) + half * cap + row % cap == col
@@ -263,73 +283,77 @@
         return jnp.concatenate(parts, 1)
 
     row, col = iota((count, rows), 0), iota((count, rows), 1)
-    slot, block, side = row % cap, row // (HALVES * cap), row // cap % HALVES
-    if split:
-        source = block * cap + slot
-    else:
-        source = (block % groups * batches + block // groups) * cap + slot
-
-    data = jnp.concatenate([whole(near_ref), whole(far_ref)], 0)
-    gate_val = up_val = 0.0
-    for c in range(chunks):
-        copies[2 * c].wait()
-        copies[2 * c + 1].wait()
-        part = slice(c * depth, (c + 1) * depth)
-        gate_val = gate_val + dot(data[:, part], gate_ref[part, :])
-        up_val = up_val + dot(data[:, part], up_ref[part, :])
+    slot, side = row % cap, row // cap % HALVES
+    shift = (place - row // (HALVES * cap) % splits + splits) % splits
+    block = row // (HALVES * cap * splits)
+    if not split:
+        block = block % experts * batches + block // experts
+    source = shift * each + block * cap + slot
+    data = jnp.concatenate([whole(ref) for ref in sources], 0)
+    gate_val, up_val = dot(data, gate_ref[...]), dot(data, up_ref[...])
     inner = (gate_val / (1.0 + jnp.exp(-gate_val)) * up_val).astype(BF16)
     keep = send = 0.0
     for half in range(HALVES):
-        copies[2 * chunks + half].wait()
         part = dot(inner, down_ref[:, half * wide : (half + 1) * wide]).astype(BF16)
         pick = ((source == col) & (side == half)).astype(BF16)
         send = send + dot(pick, part[rows:])
         keep = keep + dot(pick, part[:rows])
     send_ref[...] = send.astype(BF16)
     keep_ref[...] = keep.astype(BF16)
-    for copy in copies[2 * chunks + HALVES :]:
-        copy.wait()
-
-
-def ffn(dims, layer, sections, near, far, gate, up, down, head, early, states, shifted):
-    batches, toks, width, experts, splits, _, cap = dims
-    hidden = gate.shape[1]
+
+
+def expert_rows(dims, layer, sources, weights):
+    batches, _, width, experts, splits, _, cap = dims
+    count = batches * experts * splits * HALVES * cap
+    return call(
+        lambda *refs: expert_kernel(dims, layer > 0, *refs),
+        [((count, width // HALVES), BF16)] * 2,
+        (*sources, *weights),
+        [VMEM] * (len(sources) + 3),
+        flops=6 * count * width * weights[0].shape[1],
+    )
+
+
+def advance_kernel(dims, layer, last, back_ref, mix_ref, states_ref, gain_ref, *refs):
+    _, toks, width, _, _, _, _ = dims
     wide = width // HALVES
-    back = experts * splits * HALVES * cap
-    count = batches * back
-    chunks = 4
-    outs = [((count, wide), BF16), ((count, wide), BF16), ((2 * HALVES * toks, back), BF16)]
-    outs.append(((HALVES, wide), F32))
-    if layer < sections - 1:
-        outs.append(((HALVES * toks, sections * back), BF16))
+    size = mix_ref.shape[1]
+    mixed = dot(mix_ref[...], back_ref[layer * size : (layer + 1) * size, :])
+    states = states_ref[...].astype(F32) + mixed[: HALVES * toks] + mixed[HALVES * toks :]
+    states = states.astype(BF16)
+    values = states.astype(F32)
+    square = jnp.sum(values * values, -1, keepdims=True)
+    factor = lax.rsqrt(sum(square[h * toks : (h + 1) * toks] for h in range(HALVES)) / width + 1e-06)
+    normed = [
+        (values[h * toks : (h + 1) * toks] * factor * gain_ref[h : h + 1, :]).astype(BF16)
+        for h in range(HALVES)
+    ]
+    if last:
+        out_ref = refs[0]
+        for h in range(HALVES):
+            for copy in range(out_ref.shape[0] // toks):
+                out_ref[copy * toks : (copy + 1) * toks, h * wide : (h + 1) * wide] = normed[h]
+        return
+    pack_ref, out_ref, packed_ref = refs
+    out_ref[...] = states
+    packed_ref[...] = dot(pack_ref[...], jnp.concatenate(normed, 0), (0, 0)).astype(BF16)
+
+
+def advance(dims, layer, back, mixes, states, gain, pack):
+    _, toks, width, experts, splits, _, _ = dims
+    last = pack is None
+    if last:
+        outs = [((experts * splits * toks, width), BF16)]
     else:
-        outs.append(((head.shape[0] - early, width), BF16))
-    ins = (near, far, gate, up, down, head, states, *shifted)
-    specs = [VMEM, VMEM, HBM, HBM, HBM, HBM] + [VMEM] * (1 + sections)
-    scratch = [
-        pltpu.VMEM((width, hidden), BF16),
-        pltpu.VMEM((width, hidden), BF16),
-        pltpu.VMEM((hidden, width), BF16),
-        pltpu.SemaphoreType.DMA((2 * chunks + HALVES + 1,)),
-    ]
+        outs = [(states.shape, BF16), ((pack.shape[1], width // HALVES), BF16)]
+    ins = (back, mixes, states, gain) + (() if last else (pack,))
     return call(
-        lambda *refs: ffn_kernel(dims, layer, sections, chunks, *refs),
-        outs,
-        ins,
-        specs,
-        scratch,
-        flops=6 * count * width * hidden,
-    )
-
-
-def head_kernel(batches, early, near_ref, far_ref, target_ref, *refs):
-    others = batches - 1
-    sources, refs = refs[: 1 + 2 * others], refs[1 + 2 * others :]
-    out_ref, table_ref, sems = refs
-    vocab = sources[0].shape[0]
-    section, member = lax.axis_index("section"), lax.axis_index("expert")
-    members = lax.axis_size("expert")
-    batch = section % batches
+        lambda *refs: advance_kernel(dims, layer, last, *refs), outs, ins, [VMEM] * len(ins)
+    )
+
+
+def table_kernel(*refs):
+    sources, table_ref, sems = refs[:-2], refs[-2], refs[-1]
     copies, spot = [], 0
     for i, source in enumerate(sources):
         size = source.shape[0]
@@ -337,7 +361,16 @@
         spot += size
     for copy in copies:
         copy.start()
-
+    for copy in copies:
+        copy.wait()
+
+
+def head_kernel(batches, early, near_ref, far_ref, target_ref, table_ref, out_ref):
+    others = batches - 1
+    vocab = table_ref.shape[0] // batches
+    section, member = lax.axis_index("section"), lax.axis_index("expert")
+    members = lax.axis_size("expert")
+    batch = section % batches
     toks = near_ref.shape[0] + far_ref.shape[0]
     each = toks // members
     col = iota((toks, toks), 1)
@@ -353,17 +386,13 @@
     target = jnp.dot(target, moved, precision=exact, preferred_element_type=F32)[0:1].astype(jnp.int32)
 
     rows = jnp.concatenate([near_ref[...], far_ref[...]], 0)
-    for copy in copies[1:]:
-        copy.wait()
-    after = dot(table_ref[vocab:, :], rows, (1, 1))
-    copies[0].wait()
-    blocks, spot = [(dot(table_ref[:vocab, :], rows, (1, 1)), (section * members + member) * vocab)], 0
-    for i, source in enumerate(sources[1:]):
-        size = source.shape[0]
-        shift = i % others + 1
-        owner = section - batch + (batch - shift + batches) % batches
+    logits = dot(table_ref[...], rows, (1, 1))
+    blocks, spot = [(logits[:vocab], (section * members + member) * vocab)], vocab
+    for i in range(2 * others):
+        size = early if i < others else vocab - early
+        owner = section - batch + (batch - i % others - 1 + batches) % batches
         start = (owner * members + member) * vocab + (early if i >= others else 0)
-        blocks.append((after[spot : spot + size], start))
+        blocks.append((logits[spot : spot + size], start))
         spot += size
     peak = blocks[0][0].max(0, keepdims=True)
     for block, _ in blocks[1:]:
@@ -419,7 +448,6 @@
     splits = members // experts // PAIR
     groups = members // PAIR
     cap = min(toks, 9 * toks * tops // (8 * experts))
-    wide = width // HALVES
     dims = (batches, toks, width, experts, splits, tops, cap)
     same_core = [[g * PAIR + c for g in range(groups)] for c in range(PAIR)]
     same_core_all = [
@@ -427,21 +455,39 @@
         for c in range(PAIR)
     ]
     partner = [(i, i ^ 1) for i in range(members)]
+    split = splits * PAIR
+    same_place = [[e * split + r for e in range(experts)] for r in range(split)]
+    same_place_all = [
+        [s * members + e * split + r for s in range(sections) for e in range(experts)]
+        for r in range(split)
+    ]
 
     def exchange(rows):
         return lax.all_to_all(
             rows, "expert", split_axis=0, concat_axis=0, axis_index_groups=same_core, tiled=True
         )
 
-    def exchange_all(rows):
+    def exchange_all(rows, over):
         return lax.all_to_all(
             rows,
             ("section", "expert"),
             split_axis=0,
             concat_axis=0,
-            axis_index_groups=same_core_all,
+            axis_index_groups=over,
             tiled=True,
         )
+
+    def dispatch_first(rows):
+        return lax.all_to_all(
+            rows, "expert", split_axis=0, concat_axis=0, axis_index_groups=same_place, tiled=True
+        )
+
+    def to_split(rows, shift):
+        pairs = []
+        for i in range(members):
+            place = i // PAIR % splits
+            pairs.append((i, i + ((place + shift) % splits - place) * PAIR))
+        return lax.ppermute(rows, "expert", pairs)
 
     def swap_core(rows):
         return lax.ppermute(rows, "expert", partner)
@@ -461,65 +507,60 @@
     first_parts = []
     for shift in range(1, batches):
         first_parts.append(by_section(early_head, shift, batches))
-    near = exchange(packed)
+    near = dispatch_first(packed)
 
     shifted = [small]
     for shift in range(1, sections):
         shifted.append(by_section(small, shift, sections))
 
-    size = groups * HALVES * cap
+    inner_size = experts * HALVES * cap
     for tick in range(sections):
-        far = swap_core(near)
-        keep, send, mixes, gain, extra = ffn(
-            dims,
-            tick,
-            sections,
-            near,
-            far,
-            w_gate[0],
-            w_up[0],
-            w_down[0],
-            head,
-            early,
-            states,
-            shifted,
+        crossing = []
+        for shift in range(1, splits):
+            crossing.append(to_split(near, shift))
+        mixes, gain, *got = ready(
+            dims, tick, sections, (w_gate[0], w_up[0], w_down[0]), head, early, states, shifted
         )
+        pack = got.pop(0) if tick < sections - 1 else None
+        weights = got[:3]
+        if tick == 0:
+            late_head = got[3]
+        mine = [near, *crossing]
+        sources = mine + [swap_core(rows) for rows in mine]
+        keep, send = expert_rows(dims, tick, sources, weights)
         total = (keep.astype(F32) + swap_core(send).astype(F32)).astype(BF16)
         if sections > batches:
             total = jnp.concatenate([total] * (sections // batches), 0)
-        back = exchange_all(total)[tick * size : (tick + 1) * size]
-        mixed = dot(mixes, back)
-        states = states.astype(F32) + mixed[: HALVES * toks] + mixed[HALVES * toks :]
-        states = states.astype(BF16)
-        values = states.astype(F32).reshape(HALVES, toks, wide)
-        factor = lax.rsqrt(jnp.sum(values * values, (0, 2), keepdims=True) / width + 1e-06)
+        back = exchange_all(total, same_core_all)
         if tick == sections - 1:
             break
-        normed = (values * factor * gain[:, None, :]).astype(BF16)
-        packed = dot(extra, normed.reshape(HALVES * toks, wide), (0, 0)).astype(BF16)
-        near = exchange_all(packed)
+        states, packed = advance(dims, tick, back, mixes, states, gain, pack)
+        near = exchange_all(packed, same_place_all)
         if sections > batches:
             base = tick + 1 - (tick + 1) % batches
-            near = near[base * size : (base + batches) * size]
-
-    states, late_head = lax.optimization_barrier((states, extra))
-    late_parts = []
-    for shift in range(1, batches):
-        late_parts.append(by_section(late_head, shift, batches))
-    final = (values * factor * gain[:, None, :]).astype(BF16)
-    final = jnp.concatenate([final[h] for h in range(HALVES)], 1)
-    near = exchange(jnp.broadcast_to(final[None], (groups, toks, width)).reshape(groups * toks, width))
+            near = near[base * inner_size : (base + batches) * inner_size]
+        if tick == 0:
+            near, late_head = lax.optimization_barrier((near, late_head))
+            late_parts = []
+            for shift in range(1, batches):
+                late_parts.append(by_section(late_head, shift, batches))
+
+    (last_rows,) = advance(dims, tick, back, mixes, states, gain, None)
+    near = exchange(last_rows)
     far = swap_core(near)
     world = sections * members
+    (table,) = call(
+        table_kernel,
+        [((batches * head.shape[0], width), BF16, True)],
+        (head, *first_parts, *late_parts),
+        [HBM] + [ANY] * (2 * batches - 2),
+        [pltpu.SemaphoreType.DMA((2 * batches - 1,))],
+    )
     (stats,) = call(
         lambda *refs: head_kernel(batches, early, *refs),
         [((world, 1, 2 * members * toks), F32)],
-        (near, far, targets, head, *first_parts, *late_parts),
-        [VMEM] * 3 + [HBM] + [ANY] * (2 * batches - 2),
-        [
-            pltpu.VMEM((batches * head.shape[0], width), BF16),
-            pltpu.SemaphoreType.DMA((2 * batches - 1,)),
-        ],
+        (near, far, targets, table),
+        [VMEM] * 4,
         flops=4 * head.size * members * toks,
     )
     stats = lax.all_to_all(stats, ("section", "expert"), split_axis=0, concat_axis=0, tiled=True)

time: 160 us -> 164 us (1.025)
  blocking collectives: 84.6 us -> 75.2 us
  waiting for transfers between devices: 48.1 us -> 56.7 us
  Pallas kernels: 16.9 us -> 20.6 us
  starting transfers between devices: 7.33 us -> 9.81 us
    ppermute x0 -> x2, waiting for transfers between devices: none -> 9.95 us  [to_split(): return lax.ppermute(rows, 'expert', pairs)]
    all_to_all x1, blocking collectives: 20.3 us -> 14.3 us  [dispatch_first(): lax.all_to_all(rows, 'expert', split_axis=0, concat_axis=0, axis_index_gr...]
    all_to_all x3, blocking collectives: 52.5 us -> 48.6 us  [exchange_all(): lax.all_to_all(rows, ('section', 'expert'), split_axis=0, concat_axis=0,...]
    pallas_call x5 -> x10, Pallas kernels: 16.9 us -> 20.6 us  [call(): pl.pallas_call(kernel, out_shape=tuple((pltpu.VMEM(*out[:2]) if out[2:] e...]
    ppermute x0 -> x2, starting transfers between devices: none -> 2.08 us  [to_split(): return lax.ppermute(rows, 'expert', pairs)]
    ppermute x5 -> x7, waiting for transfers between devices: 5.3 us -> 3.26 us  [swap_core(): return lax.ppermute(rows, 'expert', partner)]
  transfers between devices with their start and end apart: 9 -> 13, of which waited for: 7 -> 8; matrix products, arithmetic and copies ran while one was open for 0% -> 0% of each run, Pallas kernels for 0% -> 6%
where the time goes in v3:
time: 164 us; the launch traced here: 163 us
  blocking collectives  75.2 us (46%)
  waiting for transfers between devices  56.7 us (35%)
  Pallas kernels  20.6 us (13%)
  starting transfers between devices  9.81 us (6%)
    all_to_all x3, blocking collectives, exchange_all(): lax.all_to_all(rows, ('section', 'expert'), split_axis=0, concat_axis=0,...  48.6 us
    ppermute x3, waiting for transfers between devices, by_section(): lax.ppermute(array, 'section', [(s, s - s % across + (s + shift) % across...  32.5 us
    pallas_call x10, Pallas kernels, call(): pl.pallas_call(kernel, out_shape=tuple((pltpu.VMEM(*out[:2]) if out[2:] e...  20.6 us
    all_to_all x1, blocking collectives, dispatch_first(): lax.all_to_all(rows, 'expert', split_axis=0, concat_axis=0, axis_index_gr...  14.3 us
    all_to_all x1, blocking collectives, body(): lax.all_to_all(stats, ('section', 'expert'), split_axis=0, concat_axis=0,...  12.2 us
    all_to_all x1, waiting for transfers between devices, exchange(): lax.all_to_all(rows, 'expert', split_axis=0, concat_axis=0, axis_index_gr...  10.9 us
    ppermute x2, waiting for transfers between devices, to_split(): return lax.ppermute(rows, 'expert', pairs)  9.95 us
    ppermute x3, starting transfers between devices, by_section(): lax.ppermute(array, 'section', [(s, s - s % across + (s + shift) % across...  3.58 us
  transfers between devices with their start and end apart: 13, of which 8 were waited for; matrix products, arithmetic and copies ran while one was open for 0% of the time, Pallas kernels for 6%

profile of v3, /device:TPU:0, one launch (start us, length us, event | category | flops | bytes accessed | tf_op | source)
XLA Modules:
  0.0 163.3 jit_solution(9641982387308225121)
XLA Ops:
  0.6 1.8 %shard_map.122 = (bf16[32,3584]{1,0:T(8,128)(2,1)S(1)}, f32[8,3712]{1,0:T(8,128)S(1)}, bf16[16,1792]{1,0:T(8,128)(2,1)S(1)}, bf16[160,3584]{1,0:T(8,128)(2,1)S(1)}) custom-call(bf16[2,8,3584]{2,1,0:T(8,128)(2,1)} %refs_0_.2, f32[1,3584]{1,0:T(1,128)} %refs_1_.2, bf16[4,3584]{1,0:T(4,128)(2,1)} %bitcast.39, s32[2,2,8]{2,1,0:T(2,128)} %bitcast.40, ...), custom_call_target="tpu_custom_call" | custom-call | flops 1 | bytes 2007168 | tf_op jit(solution)/shard_map/pallas_call | solution.py:28
  2.4 14.3 %all_to_all.61 = bf16[4,8,3584]{2,1,0:T(8,128)(2,1)S(1)} all-to-all(bf16[4,8,3584]{2,1,0:T(8,128)(2,1)S(1)} %bitcast.32), channel_id=1, replica_groups={{0,4,8,12},{1,5,9,13},{2,6,10,14},{3,7,11,15},{16,20,24,28},{17,21,25,2..., dimensions={0} | all-to-all | bytes 458752 | tf_op jit(solution)/shard_map/all_to_all | solution.py:481
  16.8 1.5 collective-permute-start
  18.3 0.0 collective-permute-start.1
  18.3 4.5 %collective-permute-done.refs_1_ = bf16[32,3584]{1,0:T(8,128)(2,1)S(1)} collective-permute-done((bf16[32,3584]{1,0:T(8,128)(2,1)S(1)}, bf16[32,3584]{1,0:T(8,128)(2,1)S(1)}, u32[]{:S(2)}, u32[]{:S(2)}) %collective-permute-start) | collective-permute-done | bytes 229408 | tf_op jit(solution)/shard_map/ppermute | solution.py:490
  22.8 0.0 collective-permute-start.2
  22.8 1.5 collective-permute-start.3
  24.3 4.2 %collective-permute-done.3.refs_6_ = f32[8,3712]{1,0:T(8,128)S(1)} collective-permute-done((f32[8,3712]{1,0:T(8,128)S(1)}, f32[8,3712]{1,0:T(8,128)S(1)}, u32[]{:S(2)}, u32[]{:S(2)}) %collective-permute-start.3) | collective-permute-done | bytes 118816 | tf_op jit(solution)/shard_map/ppermute | solution.py:496
  28.4 4.4 %shard_map.123 = (bf16[32,64]{1,0:T(8,128)(2,1)S(1)}, f32[2,1792]{1,0:T(2,128)S(1)}, bf16[16,64]{1,0:T(8,128)(2,1)S(1)}, bf16[3584,512]{1,0:T(8,128)(2,1)S(1)}, ...) custom-call(bf16[3584,512]{1,0:T(8,128)(2,1)} %bitcast.33, ...), custom_call_target="tpu_custom_call" | custom-call | flops 1 | bytes 13139968 | tf_op jit(solution)/shard_map/pallas_call | solution.py:28
  32.8 0.0 copy-start.2
  32.8 0.0 collective-permute-done.1.refs_2_
  32.8 0.0 collective-permute-done.2.refs_3_
  32.8 2.3 %shard_map.124 = (bf16[128,1792]{1,0:T(8,128)(2,1)S(1)}, bf16[128,1792]{1,0:T(8,128)(2,1)S(1)}) custom-call(bf16[32,3584]{1,0:T(8,128)(2,1)S(1)} %bitcast.27, bf16[32,3584]{1,0:T(8,128)(2,1)S(1)} %collective-permute-done.refs_1_, bf16[32,3584]{1,0:T(8,128)(2,1)S(1)} %collective-permute-done.1.refs_2_, bf16[32,3584]{1,0:T(8,128)(2,1)S(1)} %collective-permute-done.2.refs_3_, ...), custom_call_target="tpu_custom_call" | custom-call | flops 1409286144 | bytes 11927552 | tf_op jit(solution)/shard_map/pallas_call | solution.py:28
  35.1 0.1 collective-permute-start.4
  35.2 1.8 %collective-permute-done.4 = bf16[128,1792]{1,0:T(8,128)(2,1)S(1)} collective-permute-done((bf16[128,1792]{1,0:T(8,128)(2,1)S(1)}, bf16[128,1792]{1,0:T(8,128)(2,1)S(1)}, u32[]{:S(2)}, u32[]{:S(2)}) %collective-permute-start.4) | collective-permute-done | bytes 458784 | tf_op jit(solution)/shard_map/ppermute | solution.py:493
  37.0 0.1 fusion
  37.1 19.7 %all_to_all.62 = bf16[16,8,1792]{2,1,0:T(8,128)(2,1)S(1)} all-to-all(bf16[16,8,1792]{2,1,0:T(8,128)(2,1)S(1)} %fusion), channel_id=1, replica_groups={{0,2,4,6,8,10,12,14,16,18,20,22,24,26,28,30},{1,3,5,7,9,11,13,15,17,19,..., dimensions={0} | all-to-all | bytes 917504 | tf_op jit(solution)/shard_map/all_to_all | solution.py:471
  56.8 0.5 shard_map.125
  57.3 11.9 %all_to_all.63 = bf16[8,8,1792]{2,1,0:T(8,128)(2,1)S(1)} all-to-all(bf16[8,8,1792]{2,1,0:T(8,128)(2,1)S(1)} %bitcast.31), channel_id=1, replica_groups={{0,4,8,12,16,20,24,28},{1,5,9,13,17,21,25,29},{2,6,10,14,18,22,26,30},{..., dimensions={0} | all-to-all | bytes 458752 | tf_op jit(solution)/shard_map/all_to_all | solution.py:471
  69.1 0.6 collective-permute-start.5
  69.7 0.0 collective-permute-start.6
  69.7 0.0 copy-done.2
  69.7 5.5 %collective-permute-done.5.refs_1_ = bf16[64,1792]{1,0:T(8,128)(2,1)S(1)} collective-permute-done((bf16[64,1792]{1,0:T(8,128)(2,1)S(1)}, bf16[64,1792]{1,0:T(8,128)(2,1)S(1)}, u32[]{:S(2)}, u32[]{:S(2)}) %collective-permute-start.5) | collective-permute-done | bytes 229408 | tf_op jit(solution)/shard_map/ppermute | solution.py:490
  75.1 0.0 collective-permute-start.7
  75.1 4.2 %shard_map.126 = (bf16[32,64]{1,0:T(8,128)(2,1)S(1)}, f32[2,1792]{1,0:T(2,128)S(1)}, bf16[3584,512]{1,0:T(8,128)(2,1)S(1)}, bf16[3584,512]{1,0:T(8,128)(2,1)S(1)}, bf16[512,3584]{1,0:T(8,128)(2,1)S(1)}) custom-call(bf16[3584,512]{1,0:T(8,128)(2,1)} %bitcast.34, bf16[3584,512]{1,0:T(8,128)(2,1)} %bitcast.36, bf16[512,3584]{1,0:T(8,128)(2,1)} %bitcast.38, ...), custom_call_target="tpu_custom_call" | custom-call | flops 1 | bytes 13139968 | tf_op jit(solution)/shard_map/pallas_call | solution.py:28
  79.4 0.0 collective-permute-done.6.refs_2_
  79.4 0.0 collective-permute-done.7.refs_3_
  79.4 2.5 %shard_map.127 = (bf16[128,1792]{1,0:T(8,128)(2,1)S(1)}, bf16[128,1792]{1,0:T(8,128)(2,1)S(1)}) custom-call(bf16[64,1792]{1,0:T(8,128)(2,1)S(1)} %bitcast.30, bf16[64,1792]{1,0:T(8,128)(2,1)S(1)} %collective-permute-done.5.refs_1_, bf16[64,1792]{1,0:T(8,128)(2,1)S(1)} %collective-permute-done.6.refs_2_, bf16[64,1792]{1,0:T(8,128)(2,1)S(1)} %collective-permute-done.7.refs_3_, ...), custom_call_target="tpu_custom_call" | custom-call | flops 1409286144 | bytes 11927552 | tf_op jit(solution)/shard_map/pallas_call | solution.py:28
  81.9 0.6 collective-permute-start.8
  82.5 1.4 collective-permute-done.8
  84.0 0.1 fusion.1
  84.1 17.1 %all_to_all.64 = bf16[16,8,1792]{2,1,0:T(8,128)(2,1)S(1)} all-to-all(bf16[16,8,1792]{2,1,0:T(8,128)(2,1)S(1)} %fusion.1), channel_id=1, replica_groups={{0,2,4,6,8,10,12,14,16,18,20,22,24,26,28,30},{1,3,5,7,9,11,13,15,17,19,..., dimensions={0} | all-to-all | bytes 917504 | tf_op jit(solution)/shard_map/all_to_all | solution.py:471
  101.2 1.1 shard_map.128
  102.3 3.5 %all-to-all-start.4 = ((bf16[8,8,3584]{2,1,0:T(8,128)(2,1)}), bf16[8,8,3584]{2,1,0:T(8,128)(2,1)S(1)}, u32[]{:S(2)}, u32[]{:S(2)}) async-start(bf16[8,8,3584]{2,1,0:T(8,128)(2,1)} %bitcast.15), calls=%async_computation.4 | async-start | bytes 917504 | tf_op jit(solution)/shard_map/all_to_all | solution.py:466
  105.8 1.4 collective-permute-start.10
  107.2 0.7 collective-permute-start.11
  107.9 10.9 %all-to-all-done.4 = bf16[8,8,3584]{2,1,0:T(8,128)(2,1)S(1)} async-done(((bf16[8,8,3584]{2,1,0:T(8,128)(2,1)}), bf16[8,8,3584]{2,1,0:T(8,128)(2,1)S(1)}, u32[]{:S(2)}, u32[]{:S(2)}) %all-to-all-start.4) | async-done | bytes 458784 | tf_op jit(solution)/shard_map/all_to_all | solution.py:466
  118.8 0.0 collective-permute-start.9
  118.8 15.2 %collective-permute-done.10.refs_1_ = bf16[160,3584]{1,0:T(8,128)(2,1)S(1)} collective-permute-done((bf16[160,3584]{1,0:T(8,128)(2,1)S(1)}, bf16[160,3584]{1,0:T(8,128)(2,1)S(1)}, u32[]{:S(2)}, u32[]{:S(2)}) %collective-permute-start.10) | collective-permute-done | bytes 1146912 | tf_op jit(solution)/shard_map/ppermute | solution.py:496
  134.0 13.2 %collective-permute-done.11.refs_2_ = bf16[96,3584]{1,0:T(8,128)(2,1)S(1)} collective-permute-done((bf16[96,3584]{1,0:T(8,128)(2,1)}, bf16[96,3584]{1,0:T(8,128)(2,1)S(1)}, u32[]{:S(2)}, u32[]{:S(2)}) %collective-permute-start.11) | collective-permute-done | bytes 688160 | tf_op jit(solution)/shard_map/ppermute | solution.py:496
  147.2 1.5 shard_map.129.refs_3_
  148.7 0.0 copy-start.1
  148.7 0.0 collective-permute-done.9.refs_1_
  148.7 0.0 copy-done
  148.8 1.6 shard_map.130
  150.4 12.2 %all_to_all.65.refs_0_ = f32[32,1,256]{2,1,0:T(1,128)S(1)} all-to-all(f32[32,1,256]{2,1,0:T(1,128)S(1)} %shard_map.130), channel_id=1, replica_groups=mesh['section'=2,'expert'=16] {'section','expert'}, dimensions={0} | all-to-all | bytes 65536 | tf_op jit(solution)/shard_map/all_to_all | solution.py:566
  162.6 0.0 copy-done.1
  162.6 0.7 shard_map.131
  (1 shorter events, 0.0 us)
Async XLA Ops:
  16.8 6.0 %collective-permute-start = (bf16[32,3584]{1,0:T(8,128)(2,1)S(1)}, bf16[32,3584]{1,0:T(8,128)(2,1)S(1)}, u32[]{:S(2)}, u32[]{:S(2)}) collective-permute-start(bf16[32,3584]{1,0:T(8,128)(2,1)S(1)} %bitcast.25), channel_id=1, source_target_pairs={{0,2},{1,3},{2,0},{3,1},{4,6},{5,7},{6,4},{7,5},{8,10},{9,11},{10,... | collective-permute-start | bytes 688136 | tf_op jit(solution)/shard_map/ppermute | solution.py:490
  18.3 14.5 %collective-permute-start.1 = (bf16[32,3584]{1,0:T(8,128)(2,1)S(1)}, bf16[32,3584]{1,0:T(8,128)(2,1)S(1)}, u32[]{:S(2)}, u32[]{:S(2)}) collective-permute-start(bf16[32,3584]{1,0:T(8,128)(2,1)S(1)} %bitcast.26), channel_id=1, source_target_pairs={{0,1},{1,0},{2,3},{3,2},{4,5},{5,4},{6,7},{7,6},{8,9},{9,8},{10,11... | collective-permute-start | bytes 688136 | tf_op jit(solution)/shard_map/ppermute | solution.py:493
  22.8 10.0 %collective-permute-start.2 = (bf16[32,3584]{1,0:T(8,128)(2,1)S(1)}, bf16[32,3584]{1,0:T(8,128)(2,1)S(1)}, u32[]{:S(2)}, u32[]{:S(2)}) collective-permute-start(bf16[32,3584]{1,0:T(8,128)(2,1)S(1)} %collective-permute-done.refs_1_), channel_id=1, source_target_pairs={{0,1},{1,0},{2,3},{3,2},{4,5},{5,4},{6,7},{7,6},{8,9},{9,8},{10,11... | collective-permute-start | bytes 688136 | tf_op jit(solution)/shard_map/ppermute | solution.py:493
  22.8 5.6 %collective-permute-start.3 = (f32[8,3712]{1,0:T(8,128)S(1)}, f32[8,3712]{1,0:T(8,128)S(1)}, u32[]{:S(2)}, u32[]{:S(2)}) collective-permute-start(f32[8,3712]{1,0:T(8,128)S(1)} %get-tuple-element.28.refs_5_), channel_id=1, source_target_pairs={{0,16},{16,0},{1,17},{17,1},{2,18},{18,2},{3,19},{19,3},{4,20},{20... | collective-permute-start | bytes 356360 | tf_op jit(solution)/shard_map/ppermute | solution.py:496
  32.8 36.9 %copy-start.2 = (bf16[96,3584]{1,0:T(8,128)(2,1)}, bf16[96,3584]{1,0:T(8,128)(2,1)S(1)}, u32[]{:S(2)}) copy-start(bf16[96,3584]{1,0:T(8,128)(2,1)S(1)} %get-tuple-element.49) | copy-start | bytes 2064388
  35.1 1.9 %collective-permute-start.4 = (bf16[128,1792]{1,0:T(8,128)(2,1)S(1)}, bf16[128,1792]{1,0:T(8,128)(2,1)S(1)}, u32[]{:S(2)}, u32[]{:S(2)}) collective-permute-start(bf16[128,1792]{1,0:T(8,128)(2,1)S(1)} %get-tuple-element.33), channel_id=1, source_target_pairs={{0,1},{1,0},{2,3},{3,2},{4,5},{5,4},{6,7},{7,6},{8,9},{9,8},{10,11... | collective-permute-start | bytes 1376264 | tf_op jit(solution)/shard_map/ppermute | solution.py:493
  69.1 6.0 %collective-permute-start.5 = (bf16[64,1792]{1,0:T(8,128)(2,1)S(1)}, bf16[64,1792]{1,0:T(8,128)(2,1)S(1)}, u32[]{:S(2)}, u32[]{:S(2)}) collective-permute-start(bf16[64,1792]{1,0:T(8,128)(2,1)S(1)} %bitcast.28), channel_id=1, source_target_pairs={{0,2},{1,3},{2,0},{3,1},{4,6},{5,7},{6,4},{7,5},{8,10},{9,11},{10,... | collective-permute-start | bytes 688136 | tf_op jit(solution)/shard_map/ppermute | solution.py:490
  69.7 9.7 %collective-permute-start.6 = (bf16[64,1792]{1,0:T(8,128)(2,1)S(1)}, bf16[64,1792]{1,0:T(8,128)(2,1)S(1)}, u32[]{:S(2)}, u32[]{:S(2)}) collective-permute-start(bf16[64,1792]{1,0:T(8,128)(2,1)S(1)} %bitcast.29), channel_id=1, source_target_pairs={{0,1},{1,0},{2,3},{3,2},{4,5},{5,4},{6,7},{7,6},{8,9},{9,8},{10,11... | collective-permute-start | bytes 688136 | tf_op jit(solution)/shard_map/ppermute | solution.py:493
  75.1 4.3 %collective-permute-start.7 = (bf16[64,1792]{1,0:T(8,128)(2,1)S(1)}, bf16[64,1792]{1,0:T(8,128)(2,1)S(1)}, u32[]{:S(2)}, u32[]{:S(2)}) collective-permute-start(bf16[64,1792]{1,0:T(8,128)(2,1)S(1)} %collective-permute-done.5.refs_1_), channel_id=1, source_target_pairs={{0,1},{1,0},{2,3},{3,2},{4,5},{5,4},{6,7},{7,6},{8,9},{9,8},{10,11... | collective-permute-start | bytes 688136 | tf_op jit(solution)/shard_map/ppermute | solution.py:493
  81.9 2.0 %collective-permute-start.8 = (bf16[128,1792]{1,0:T(8,128)(2,1)S(1)}, bf16[128,1792]{1,0:T(8,128)(2,1)S(1)}, u32[]{:S(2)}, u32[]{:S(2)}) collective-permute-start(bf16[128,1792]{1,0:T(8,128)(2,1)S(1)} %get-tuple-element.45), channel_id=1, source_target_pairs={{0,1},{1,0},{2,3},{3,2},{4,5},{5,4},{6,7},{7,6},{8,9},{9,8},{10,11... | collective-permute-start | bytes 1376264 | tf_op jit(solution)/shard_map/ppermute | solution.py:493
  102.3 16.5 %all-to-all-start.4 = ((bf16[8,8,3584]{2,1,0:T(8,128)(2,1)}), bf16[8,8,3584]{2,1,0:T(8,128)(2,1)S(1)}, u32[]{:S(2)}, u32[]{:S(2)}) async-start(bf16[8,8,3584]{2,1,0:T(8,128)(2,1)} %bitcast.15), calls=%async_computation.4 | async-start | bytes 917504 | tf_op jit(solution)/shard_map/all_to_all | solution.py:466
  105.8 28.2 %collective-permute-start.10 = (bf16[160,3584]{1,0:T(8,128)(2,1)S(1)}, bf16[160,3584]{1,0:T(8,128)(2,1)S(1)}, u32[]{:S(2)}, u32[]{:S(2)}) collective-permute-start(bf16[160,3584]{1,0:T(8,128)(2,1)S(1)} %get-tuple-element.48), channel_id=1, source_target_pairs={{0,16},{16,0},{1,17},{17,1},{2,18},{18,2},{3,19},{19,3},{4,20},{20... | collective-permute-start | bytes 3440648 | tf_op jit(solution)/shard_map/ppermute | solution.py:496
  107.2 40.0 %collective-permute-start.11 = (bf16[96,3584]{1,0:T(8,128)(2,1)}, bf16[96,3584]{1,0:T(8,128)(2,1)S(1)}, u32[]{:S(2)}, u32[]{:S(2)}) collective-permute-start(bf16[96,3584]{1,0:T(8,128)(2,1)} %copy-done.2), channel_id=1, source_target_pairs={{0,16},{16,0},{1,17},{17,1},{2,18},{18,2},{3,19},{19,3},{4,20},{20... | collective-permute-start | bytes 2064392 | tf_op jit(solution)/shard_map/ppermute | solution.py:496
  118.8 30.0 %copy-start = (s32[2,128]{1,0:T(2,128)S(1)}, s32[2,128]{1,0:T(2,128)}, u32[]{:S(2)}) copy-start(s32[2,128]{1,0:T(2,128)} %refs_2_.1) | copy-start | bytes 3076
  118.8 29.9 %collective-permute-start.9 = (bf16[64,3584]{1,0:T(8,128)(2,1)S(1)}, bf16[64,3584]{1,0:T(8,128)(2,1)S(1)}, u32[]{:S(2)}, u32[]{:S(2)}) collective-permute-start(bf16[64,3584]{1,0:T(8,128)(2,1)S(1)} %bitcast.21), channel_id=1, source_target_pairs={{0,1},{1,0},{2,3},{3,2},{4,5},{5,4},{6,7},{7,6},{8,9},{9,8},{10,11... | collective-permute-start | bytes 1376264 | tf_op jit(solution)/shard_map/ppermute | solution.py:493
  148.7 13.9 %copy-start.1 = (s32[2,128]{1,0:T(2,128)S(1)}, s32[2,128]{1,0:T(2,128)}, u32[]{:S(2)}) copy-start(s32[2,128]{1,0:T(2,128)} %refs_1_.3) | copy-start | bytes 3076

commit v4 on v3

--- a/solution.py
+++ b/solution.py
@@ -271,9 +271,23 @@
     each = rows // splits
     place = lax.axis_index("expert") // PAIR % splits
 
+    fast = HALVES * cap == 8 and experts % 2 == 0 and (split or batches * cap == 8)
+    turn = HALVES * cap // 2
+
+    def low(shape):
+        return iota(shape, 1) < turn
+
     def whole(ref):
         if not split:
             return ref[...]
+        if fast:
+            blocks = ref[...].astype(F32).reshape(each // 8, 2, 8, wide)
+            first, second = blocks[:, 0], blocks[:, 1]
+            low_half = low(first.shape)
+            left = jnp.where(low_half, first, pltpu.roll(second, turn, 1))
+            right = jnp.where(low_half, pltpu.roll(first, turn, 1), second)
+            parts = [left.reshape(each, wide).astype(BF16), right.reshape(each, wide).astype(BF16)]
+            return jnp.concatenate(parts, 1)
         shape = (each, HALVES * each)
         row, col = iota(shape, 0), iota(shape, 1)
         parts = []
@@ -292,6 +306,28 @@
     data = jnp.concatenate([whole(ref) for ref in sources], 0)
     gate_val, up_val = dot(data, gate_ref[...]), dot(data, up_ref[...])
     inner = (gate_val / (1.0 + jnp.exp(-gate_val)) * up_val).astype(BF16)
+    if fast:
+        left, right = (dot(inner, down_ref[:, h * wide : (h + 1) * wide]) for h in range(HALVES))
+        for core, ref in ((1, send_ref), (0, keep_ref)):
+            moved = []
+            for k in range(splits):
+                part = slice(core * rows + k * each, core * rows + (k + 1) * each)
+                a = left[part].reshape(each // 8, 8, wide)
+                b = right[part].reshape(each // 8, 8, wide)
+                low_half = low(a.shape)
+                first = jnp.where(low_half, a, pltpu.roll(b, turn, 1))
+                moved.append((first, jnp.where(low_half, pltpu.roll(a, turn, 1), b)))
+            for index in range(batches * experts):
+                if split:
+                    which, at = index % 2, index // 2
+                else:
+                    which, at = index // experts, index % experts
+                for h in range(splits):
+                    taken = moved[0][which][at]
+                    for k in range(1, splits):
+                        taken = jnp.where((place - h + splits) % splits == k, moved[k][which][at], taken)
+                    ref[(index * splits + h) * 8 : (index * splits + h + 1) * 8, :] = taken.astype(BF16)
+        return
     keep = send = 0.0
     for half in range(HALVES):
         part = dot(inner, down_ref[:, half * wide : (half + 1) * wide]).astype(BF16)

time: 164 us -> 162 us (0.988)
  no operation moved by 1% of the time
where the time goes in v4:
time: 162 us
  blocking collectives  75.2 us (46%)
  waiting for transfers between devices  56.7 us (35%)
  Pallas kernels  19.4 us (12%)
  starting transfers between devices  9.81 us (6%)
    all_to_all x3, blocking collectives, exchange_all(): lax.all_to_all(rows, ('section', 'expert'), split_axis=0, concat_axis=0,...  48.7 us
    ppermute x3, waiting for transfers between devices, by_section(): lax.ppermute(array, 'section', [(s, s - s % across + (s + shift) % across...  32.5 us
    pallas_call x10, Pallas kernels, call(): pl.pallas_call(kernel, out_shape=tuple((pltpu.VMEM(*out[:2]) if out[2:] e...  19.4 us
    all_to_all x1, blocking collectives, dispatch_first(): lax.all_to_all(rows, 'expert', split_axis=0, concat_axis=0, axis_index_gr...  14.3 us
    all_to_all x1, blocking collectives, body(): lax.all_to_all(stats, ('section', 'expert'), split_axis=0, concat_axis=0,...  12.2 us
    all_to_all x1, waiting for transfers between devices, exchange(): lax.all_to_all(rows, 'expert', split_axis=0, concat_axis=0, axis_index_gr...  11 us
    ppermute x2, waiting for transfers between devices, to_split(): return lax.ppermute(rows, 'expert', pairs)  9.95 us
    ppermute x3, starting transfers between devices, by_section(): lax.ppermute(array, 'section', [(s, s - s % across + (s + shift) % across...  3.58 us
  transfers between devices with their start and end apart: 13, of which 8 were waited for; matrix products, arithmetic and copies ran while one was open for 0% of the time, Pallas kernels for 6%

profile of v4, /device:TPU:0, one launch (start us, length us, event | category | flops | bytes accessed | tf_op | source)
XLA Modules:
  0.0 162.1 jit_solution(13212107078787816552)
XLA Ops:
  0.6 1.8 %shard_map.122 = (bf16[32,3584]{1,0:T(8,128)(2,1)S(1)}, f32[8,3712]{1,0:T(8,128)S(1)}, bf16[16,1792]{1,0:T(8,128)(2,1)S(1)}, bf16[160,3584]{1,0:T(8,128)(2,1)S(1)}) custom-call(bf16[2,8,3584]{2,1,0:T(8,128)(2,1)} %refs_0_.2, f32[1,3584]{1,0:T(1,128)} %refs_1_.2, bf16[4,3584]{1,0:T(4,128)(2,1)} %bitcast.39, s32[2,2,8]{2,1,0:T(2,128)} %bitcast.40, ...), custom_call_target="tpu_custom_call" | custom-call | flops 1 | bytes 2007168 | tf_op jit(solution)/shard_map/pallas_call | solution.py:28
  2.4 14.3 %all_to_all.61 = bf16[4,8,3584]{2,1,0:T(8,128)(2,1)S(1)} all-to-all(bf16[4,8,3584]{2,1,0:T(8,128)(2,1)S(1)} %bitcast.32), channel_id=1, replica_groups={{0,4,8,12},{1,5,9,13},{2,6,10,14},{3,7,11,15},{16,20,24,28},{17,21,25,2..., dimensions={0} | all-to-all | bytes 458752 | tf_op jit(solution)/shard_map/all_to_all | solution.py:517
  16.8 1.5 collective-permute-start
  18.3 0.0 collective-permute-start.1
  18.3 4.5 %collective-permute-done.refs_1_ = bf16[32,3584]{1,0:T(8,128)(2,1)S(1)} collective-permute-done((bf16[32,3584]{1,0:T(8,128)(2,1)S(1)}, bf16[32,3584]{1,0:T(8,128)(2,1)S(1)}, u32[]{:S(2)}, u32[]{:S(2)}) %collective-permute-start) | collective-permute-done | bytes 229408 | tf_op jit(solution)/shard_map/ppermute | solution.py:526
  22.8 0.0 collective-permute-start.2
  22.8 1.5 collective-permute-start.3
  24.3 4.2 %collective-permute-done.3.refs_6_ = f32[8,3712]{1,0:T(8,128)S(1)} collective-permute-done((f32[8,3712]{1,0:T(8,128)S(1)}, f32[8,3712]{1,0:T(8,128)S(1)}, u32[]{:S(2)}, u32[]{:S(2)}) %collective-permute-start.3) | collective-permute-done | bytes 118816 | tf_op jit(solution)/shard_map/ppermute | solution.py:532
  28.4 4.4 %shard_map.123 = (bf16[32,64]{1,0:T(8,128)(2,1)S(1)}, f32[2,1792]{1,0:T(2,128)S(1)}, bf16[16,64]{1,0:T(8,128)(2,1)S(1)}, bf16[3584,512]{1,0:T(8,128)(2,1)S(1)}, ...) custom-call(bf16[3584,512]{1,0:T(8,128)(2,1)} %bitcast.33, ...), custom_call_target="tpu_custom_call" | custom-call | flops 1 | bytes 13139968 | tf_op jit(solution)/shard_map/pallas_call | solution.py:28
  32.8 0.0 copy-start.2
  32.8 0.0 collective-permute-done.1.refs_2_
  32.8 0.0 collective-permute-done.2.refs_3_
  32.8 1.8 %shard_map.124 = (bf16[128,1792]{1,0:T(8,128)(2,1)S(1)}, bf16[128,1792]{1,0:T(8,128)(2,1)S(1)}) custom-call(bf16[32,3584]{1,0:T(8,128)(2,1)S(1)} %bitcast.27, bf16[32,3584]{1,0:T(8,128)(2,1)S(1)} %collective-permute-done.refs_1_, bf16[32,3584]{1,0:T(8,128)(2,1)S(1)} %collective-permute-done.1.refs_2_, bf16[32,3584]{1,0:T(8,128)(2,1)S(1)} %collective-permute-done.2.refs_3_, ...), custom_call_target="tpu_custom_call" | custom-call | flops 1409286144 | bytes 11927552 | tf_op jit(solution)/shard_map/pallas_call | solution.py:28
  34.6 0.1 collective-permute-start.4
  34.7 1.8 %collective-permute-done.4 = bf16[128,1792]{1,0:T(8,128)(2,1)S(1)} collective-permute-done((bf16[128,1792]{1,0:T(8,128)(2,1)S(1)}, bf16[128,1792]{1,0:T(8,128)(2,1)S(1)}, u32[]{:S(2)}, u32[]{:S(2)}) %collective-permute-start.4) | collective-permute-done | bytes 458784 | tf_op jit(solution)/shard_map/ppermute | solution.py:529
  36.5 0.1 fusion
  36.6 19.7 %all_to_all.62 = bf16[16,8,1792]{2,1,0:T(8,128)(2,1)S(1)} all-to-all(bf16[16,8,1792]{2,1,0:T(8,128)(2,1)S(1)} %fusion), channel_id=1, replica_groups={{0,2,4,6,8,10,12,14,16,18,20,22,24,26,28,30},{1,3,5,7,9,11,13,15,17,19,..., dimensions={0} | all-to-all | bytes 917504 | tf_op jit(solution)/shard_map/all_to_all | solution.py:507
  56.3 0.5 shard_map.125
  56.8 11.9 %all_to_all.63 = bf16[8,8,1792]{2,1,0:T(8,128)(2,1)S(1)} all-to-all(bf16[8,8,1792]{2,1,0:T(8,128)(2,1)S(1)} %bitcast.31), channel_id=1, replica_groups={{0,4,8,12,16,20,24,28},{1,5,9,13,17,21,25,29},{2,6,10,14,18,22,26,30},{..., dimensions={0} | all-to-all | bytes 458752 | tf_op jit(solution)/shard_map/all_to_all | solution.py:507
  68.6 0.6 collective-permute-start.5
  69.2 0.0 collective-permute-start.6
  69.2 0.0 copy-done.2
  69.2 5.5 %collective-permute-done.5.refs_1_ = bf16[64,1792]{1,0:T(8,128)(2,1)S(1)} collective-permute-done((bf16[64,1792]{1,0:T(8,128)(2,1)S(1)}, bf16[64,1792]{1,0:T(8,128)(2,1)S(1)}, u32[]{:S(2)}, u32[]{:S(2)}) %collective-permute-start.5) | collective-permute-done | bytes 229408 | tf_op jit(solution)/shard_map/ppermute | solution.py:526
  74.7 0.0 collective-permute-start.7
  74.7 4.2 %shard_map.126 = (bf16[32,64]{1,0:T(8,128)(2,1)S(1)}, f32[2,1792]{1,0:T(2,128)S(1)}, bf16[3584,512]{1,0:T(8,128)(2,1)S(1)}, bf16[3584,512]{1,0:T(8,128)(2,1)S(1)}, bf16[512,3584]{1,0:T(8,128)(2,1)S(1)}) custom-call(bf16[3584,512]{1,0:T(8,128)(2,1)} %bitcast.34, bf16[3584,512]{1,0:T(8,128)(2,1)} %bitcast.36, bf16[512,3584]{1,0:T(8,128)(2,1)} %bitcast.38, ...), custom_call_target="tpu_custom_call" | custom-call | flops 1 | bytes 13139968 | tf_op jit(solution)/shard_map/pallas_call | solution.py:28
  78.9 0.0 collective-permute-done.6.refs_2_
  78.9 0.0 collective-permute-done.7.refs_3_
  78.9 1.8 %shard_map.127 = (bf16[128,1792]{1,0:T(8,128)(2,1)S(1)}, bf16[128,1792]{1,0:T(8,128)(2,1)S(1)}) custom-call(bf16[64,1792]{1,0:T(8,128)(2,1)S(1)} %bitcast.30, bf16[64,1792]{1,0:T(8,128)(2,1)S(1)} %collective-permute-done.5.refs_1_, bf16[64,1792]{1,0:T(8,128)(2,1)S(1)} %collective-permute-done.6.refs_2_, bf16[64,1792]{1,0:T(8,128)(2,1)S(1)} %collective-permute-done.7.refs_3_, ...), custom_call_target="tpu_custom_call" | custom-call | flops 1409286144 | bytes 11927552 | tf_op jit(solution)/shard_map/pallas_call | solution.py:28
  80.7 0.6 collective-permute-start.8
  81.3 1.4 collective-permute-done.8
  82.8 0.1 fusion.1
  82.9 17.1 %all_to_all.64 = bf16[16,8,1792]{2,1,0:T(8,128)(2,1)S(1)} all-to-all(bf16[16,8,1792]{2,1,0:T(8,128)(2,1)S(1)} %fusion.1), channel_id=1, replica_groups={{0,2,4,6,8,10,12,14,16,18,20,22,24,26,28,30},{1,3,5,7,9,11,13,15,17,19,..., dimensions={0} | all-to-all | bytes 917504 | tf_op jit(solution)/shard_map/all_to_all | solution.py:507
  100.0 1.1 shard_map.128
  101.1 3.5 %all-to-all-start.4 = ((bf16[8,8,3584]{2,1,0:T(8,128)(2,1)}), bf16[8,8,3584]{2,1,0:T(8,128)(2,1)S(1)}, u32[]{:S(2)}, u32[]{:S(2)}) async-start(bf16[8,8,3584]{2,1,0:T(8,128)(2,1)} %bitcast.15), calls=%async_computation.4 | async-start | bytes 917504 | tf_op jit(solution)/shard_map/all_to_all | solution.py:502
  104.5 1.4 collective-permute-start.10
  106.0 0.7 collective-permute-start.11
  106.6 11.0 %all-to-all-done.4 = bf16[8,8,3584]{2,1,0:T(8,128)(2,1)S(1)} async-done(((bf16[8,8,3584]{2,1,0:T(8,128)(2,1)}), bf16[8,8,3584]{2,1,0:T(8,128)(2,1)S(1)}, u32[]{:S(2)}, u32[]{:S(2)}) %all-to-all-start.4) | async-done | bytes 458784 | tf_op jit(solution)/shard_map/all_to_all | solution.py:502
  117.6 0.0 collective-permute-start.9
  117.6 15.2 %collective-permute-done.10.refs_1_ = bf16[160,3584]{1,0:T(8,128)(2,1)S(1)} collective-permute-done((bf16[160,3584]{1,0:T(8,128)(2,1)S(1)}, bf16[160,3584]{1,0:T(8,128)(2,1)S(1)}, u32[]{:S(2)}, u32[]{:S(2)}) %collective-permute-start.10) | collective-permute-done | bytes 1146912 | tf_op jit(solution)/shard_map/ppermute | solution.py:532
  132.7 13.2 %collective-permute-done.11.refs_2_ = bf16[96,3584]{1,0:T(8,128)(2,1)S(1)} collective-permute-done((bf16[96,3584]{1,0:T(8,128)(2,1)}, bf16[96,3584]{1,0:T(8,128)(2,1)S(1)}, u32[]{:S(2)}, u32[]{:S(2)}) %collective-permute-start.11) | collective-permute-done | bytes 688160 | tf_op jit(solution)/shard_map/ppermute | solution.py:532
  146.0 1.5 shard_map.129.refs_3_
  147.5 0.0 copy-start.1
  147.5 0.0 collective-permute-done.9.refs_1_
  147.5 0.0 copy-done
  147.5 1.6 shard_map.130
  149.2 12.2 %all_to_all.65.refs_0_ = f32[32,1,256]{2,1,0:T(1,128)S(1)} all-to-all(f32[32,1,256]{2,1,0:T(1,128)S(1)} %shard_map.130), channel_id=1, replica_groups=mesh['section'=2,'expert'=16] {'section','expert'}, dimensions={0} | all-to-all | bytes 65536 | tf_op jit(solution)/shard_map/all_to_all | solution.py:602
  161.4 0.0 copy-done.1
  161.4 0.7 shard_map.131
  (1 shorter events, 0.0 us)
Async XLA Ops:
  16.8 6.0 %collective-permute-start = (bf16[32,3584]{1,0:T(8,128)(2,1)S(1)}, bf16[32,3584]{1,0:T(8,128)(2,1)S(1)}, u32[]{:S(2)}, u32[]{:S(2)}) collective-permute-start(bf16[32,3584]{1,0:T(8,128)(2,1)S(1)} %bitcast.25), channel_id=1, source_target_pairs={{0,2},{1,3},{2,0},{3,1},{4,6},{5,7},{6,4},{7,5},{8,10},{9,11},{10,... | collective-permute-start | bytes 688136 | tf_op jit(solution)/shard_map/ppermute | solution.py:526
  18.3 14.5 %collective-permute-start.1 = (bf16[32,3584]{1,0:T(8,128)(2,1)S(1)}, bf16[32,3584]{1,0:T(8,128)(2,1)S(1)}, u32[]{:S(2)}, u32[]{:S(2)}) collective-permute-start(bf16[32,3584]{1,0:T(8,128)(2,1)S(1)} %bitcast.26), channel_id=1, source_target_pairs={{0,1},{1,0},{2,3},{3,2},{4,5},{5,4},{6,7},{7,6},{8,9},{9,8},{10,11... | collective-permute-start | bytes 688136 | tf_op jit(solution)/shard_map/ppermute | solution.py:529
  22.8 10.0 %collective-permute-start.2 = (bf16[32,3584]{1,0:T(8,128)(2,1)S(1)}, bf16[32,3584]{1,0:T(8,128)(2,1)S(1)}, u32[]{:S(2)}, u32[]{:S(2)}) collective-permute-start(bf16[32,3584]{1,0:T(8,128)(2,1)S(1)} %collective-permute-done.refs_1_), channel_id=1, source_target_pairs={{0,1},{1,0},{2,3},{3,2},{4,5},{5,4},{6,7},{7,6},{8,9},{9,8},{10,11... | collective-permute-start | bytes 688136 | tf_op jit(solution)/shard_map/ppermute | solution.py:529
  22.8 5.6 %collective-permute-start.3 = (f32[8,3712]{1,0:T(8,128)S(1)}, f32[8,3712]{1,0:T(8,128)S(1)}, u32[]{:S(2)}, u32[]{:S(2)}) collective-permute-start(f32[8,3712]{1,0:T(8,128)S(1)} %get-tuple-element.28.refs_5_), channel_id=1, source_target_pairs={{0,16},{16,0},{1,17},{17,1},{2,18},{18,2},{3,19},{19,3},{4,20},{20... | collective-permute-start | bytes 356360 | tf_op jit(solution)/shard_map/ppermute | solution.py:532
  32.8 36.4 %copy-start.2 = (bf16[96,3584]{1,0:T(8,128)(2,1)}, bf16[96,3584]{1,0:T(8,128)(2,1)S(1)}, u32[]{:S(2)}) copy-start(bf16[96,3584]{1,0:T(8,128)(2,1)S(1)} %get-tuple-element.49) | copy-start | bytes 2064388
  34.6 1.9 %collective-permute-start.4 = (bf16[128,1792]{1,0:T(8,128)(2,1)S(1)}, bf16[128,1792]{1,0:T(8,128)(2,1)S(1)}, u32[]{:S(2)}, u32[]{:S(2)}) collective-permute-start(bf16[128,1792]{1,0:T(8,128)(2,1)S(1)} %get-tuple-element.33), channel_id=1, source_target_pairs={{0,1},{1,0},{2,3},{3,2},{4,5},{5,4},{6,7},{7,6},{8,9},{9,8},{10,11... | collective-permute-start | bytes 1376264 | tf_op jit(solution)/shard_map/ppermute | solution.py:529
  68.6 6.0 %collective-permute-start.5 = (bf16[64,1792]{1,0:T(8,128)(2,1)S(1)}, bf16[64,1792]{1,0:T(8,128)(2,1)S(1)}, u32[]{:S(2)}, u32[]{:S(2)}) collective-permute-start(bf16[64,1792]{1,0:T(8,128)(2,1)S(1)} %bitcast.28), channel_id=1, source_target_pairs={{0,2},{1,3},{2,0},{3,1},{4,6},{5,7},{6,4},{7,5},{8,10},{9,11},{10,... | collective-permute-start | bytes 688136 | tf_op jit(solution)/shard_map/ppermute | solution.py:526
  69.2 9.7 %collective-permute-start.6 = (bf16[64,1792]{1,0:T(8,128)(2,1)S(1)}, bf16[64,1792]{1,0:T(8,128)(2,1)S(1)}, u32[]{:S(2)}, u32[]{:S(2)}) collective-permute-start(bf16[64,1792]{1,0:T(8,128)(2,1)S(1)} %bitcast.29), channel_id=1, source_target_pairs={{0,1},{1,0},{2,3},{3,2},{4,5},{5,4},{6,7},{7,6},{8,9},{9,8},{10,11... | collective-permute-start | bytes 688136 | tf_op jit(solution)/shard_map/ppermute | solution.py:529
  74.7 4.3 %collective-permute-start.7 = (bf16[64,1792]{1,0:T(8,128)(2,1)S(1)}, bf16[64,1792]{1,0:T(8,128)(2,1)S(1)}, u32[]{:S(2)}, u32[]{:S(2)}) collective-permute-start(bf16[64,1792]{1,0:T(8,128)(2,1)S(1)} %collective-permute-done.5.refs_1_), channel_id=1, source_target_pairs={{0,1},{1,0},{2,3},{3,2},{4,5},{5,4},{6,7},{7,6},{8,9},{9,8},{10,11... | collective-permute-start | bytes 688136 | tf_op jit(solution)/shard_map/ppermute | solution.py:529
  80.7 2.0 %collective-permute-start.8 = (bf16[128,1792]{1,0:T(8,128)(2,1)S(1)}, bf16[128,1792]{1,0:T(8,128)(2,1)S(1)}, u32[]{:S(2)}, u32[]{:S(2)}) collective-permute-start(bf16[128,1792]{1,0:T(8,128)(2,1)S(1)} %get-tuple-element.45), channel_id=1, source_target_pairs={{0,1},{1,0},{2,3},{3,2},{4,5},{5,4},{6,7},{7,6},{8,9},{9,8},{10,11... | collective-permute-start | bytes 1376264 | tf_op jit(solution)/shard_map/ppermute | solution.py:529
  101.1 16.5 %all-to-all-start.4 = ((bf16[8,8,3584]{2,1,0:T(8,128)(2,1)}), bf16[8,8,3584]{2,1,0:T(8,128)(2,1)S(1)}, u32[]{:S(2)}, u32[]{:S(2)}) async-start(bf16[8,8,3584]{2,1,0:T(8,128)(2,1)} %bitcast.15), calls=%async_computation.4 | async-start | bytes 917504 | tf_op jit(solution)/shard_map/all_to_all | solution.py:502
  104.5 28.2 %collective-permute-start.10 = (bf16[160,3584]{1,0:T(8,128)(2,1)S(1)}, bf16[160,3584]{1,0:T(8,128)(2,1)S(1)}, u32[]{:S(2)}, u32[]{:S(2)}) collective-permute-start(bf16[160,3584]{1,0:T(8,128)(2,1)S(1)} %get-tuple-element.48), channel_id=1, source_target_pairs={{0,16},{16,0},{1,17},{17,1},{2,18},{18,2},{3,19},{19,3},{4,20},{20... | collective-permute-start | bytes 3440648 | tf_op jit(solution)/shard_map/ppermute | solution.py:532
  106.0 40.0 %collective-permute-start.11 = (bf16[96,3584]{1,0:T(8,128)(2,1)}, bf16[96,3584]{1,0:T(8,128)(2,1)S(1)}, u32[]{:S(2)}, u32[]{:S(2)}) collective-permute-start(bf16[96,3584]{1,0:T(8,128)(2,1)} %copy-done.2), channel_id=1, source_target_pairs={{0,16},{16,0},{1,17},{17,1},{2,18},{18,2},{3,19},{19,3},{4,20},{20... | collective-permute-start | bytes 2064392 | tf_op jit(solution)/shard_map/ppermute | solution.py:532
  117.6 30.0 %copy-start = (s32[2,128]{1,0:T(2,128)S(1)}, s32[2,128]{1,0:T(2,128)}, u32[]{:S(2)}) copy-start(s32[2,128]{1,0:T(2,128)} %refs_2_.1) | copy-start | bytes 3076
  117.6 29.9 %collective-permute-start.9 = (bf16[64,3584]{1,0:T(8,128)(2,1)S(1)}, bf16[64,3584]{1,0:T(8,128)(2,1)S(1)}, u32[]{:S(2)}, u32[]{:S(2)}) collective-permute-start(bf16[64,3584]{1,0:T(8,128)(2,1)S(1)} %bitcast.21), channel_id=1, source_target_pairs={{0,1},{1,0},{2,3},{3,2},{4,5},{5,4},{6,7},{7,6},{8,9},{9,8},{10,11... | collective-permute-start | bytes 1376264 | tf_op jit(solution)/shard_map/ppermute | solution.py:529
  147.5 13.9 %copy-start.1 = (s32[2,128]{1,0:T(2,128)S(1)}, s32[2,128]{1,0:T(2,128)}, u32[]{:S(2)}) copy-start(s32[2,128]{1,0:T(2,128)} %refs_1_.3) | copy-start | bytes 3076

commit v5 on v4

--- a/solution.py
+++ b/solution.py
@@ -383,13 +383,11 @@
     else:
         outs = [(states.shape, BF16), ((pack.shape[1], width // HALVES), BF16)]
     ins = (back, mixes, states, gain) + (() if last else (pack,))
-    return call(
-        lambda *refs: advance_kernel(dims, layer, last, *refs), outs, ins, [VMEM] * len(ins)
-    )
-
-
-def table_kernel(*refs):
-    sources, table_ref, sems = refs[:-2], refs[-2], refs[-1]
+    return call(lambda *refs: advance_kernel(dims, layer, last, *refs), outs, ins, [VMEM] * len(ins))
+
+
+def table_kernel(batches, toks, target_ref, *refs):
+    sources, table_ref, moved_ref, wanted_ref, sems = refs[:-4], *refs[-4:]
     copies, spot = [], 0
     for i, source in enumerate(sources):
         size = source.shape[0]
@@ -397,30 +395,36 @@
         spot += size
     for copy in copies:
         copy.start()
+
+    member = lax.axis_index("expert")
+    members = lax.axis_size("expert")
+    batch = lax.axis_index("section") % batches
+    each = toks // members
+    col = iota((toks, toks), 1)
+    core = (col // (toks // PAIR) + member) % PAIR
+    moved = iota((toks, toks), 0) == (col // each % (members // PAIR) * PAIR + core) * each + col % each
+    moved = moved.astype(F32).astype(BF16)
+    moved_ref[...] = moved
+    ids = target_ref[...]
+    target = ids[0:1]
+    for m in range(1, batches):
+        target = jnp.where(batch == m, ids[m : m + 1], target)
+    high, low = target // 256, target % 256
+    digits = jnp.concatenate([high, low, jnp.zeros((6, toks), jnp.int32)], 0).astype(F32).astype(BF16)
+    placed = dot(digits, moved)
+    wanted_ref[...] = (placed[0:1] * 256.0 + placed[1:2]).astype(jnp.int32)
     for copy in copies:
         copy.wait()
 
 
-def head_kernel(batches, early, near_ref, far_ref, target_ref, table_ref, out_ref):
+def head_kernel(batches, early, near_ref, far_ref, table_ref, moved_ref, wanted_ref, out_ref):
     others = batches - 1
     vocab = table_ref.shape[0] // batches
     section, member = lax.axis_index("section"), lax.axis_index("expert")
     members = lax.axis_size("expert")
     batch = section % batches
     toks = near_ref.shape[0] + far_ref.shape[0]
-    each = toks // members
-    col = iota((toks, toks), 1)
-    core = (col // (toks // PAIR) + member) % PAIR
-    moved = iota((toks, toks), 0) == (col // each % (members // PAIR) * PAIR + core) * each + col % each
-    moved = moved.astype(F32)
-    ids = target_ref[...].astype(F32)
-    target = ids[0:1]
-    for m in range(1, batches):
-        target = jnp.where(batch == m, ids[m : m + 1], target)
-    exact = lax.Precision.HIGHEST
-    target = jnp.broadcast_to(target, (8, toks))
-    target = jnp.dot(target, moved, precision=exact, preferred_element_type=F32)[0:1].astype(jnp.int32)
-
+    moved, target = moved_ref[...], wanted_ref[...]
     rows = jnp.concatenate([near_ref[...], far_ref[...]], 0)
     logits = dot(table_ref[...], rows, (1, 1))
     blocks, spot = [(logits[:vocab], (section * members + member) * vocab)], vocab
@@ -437,10 +441,13 @@
     for block, start in blocks:
         total = total + jnp.sum(jnp.exp(block - peak), 0, keepdims=True)
         hit = hit + jnp.sum(jnp.where(iota(block.shape, 0) + start == target, block, 0.0), 0, keepdims=True)
-    both = jnp.concatenate([peak + jnp.log(total), hit, jnp.zeros((6, toks), F32)], 0)
-    both = lax.dot_general(
-        both, moved, (((1,), (1,)), ((), ())), precision=exact, preferred_element_type=F32
-    )
+    rest = jnp.concatenate([peak + jnp.log(total), hit], 0)
+    pieces = []
+    for _ in range(3):
+        pieces.append(rest.astype(BF16))
+        rest = rest - pieces[-1].astype(F32)
+    whole = dot(jnp.concatenate(pieces + [jnp.zeros((2, toks), BF16)], 0), moved, (1, 1))
+    both = whole[0:2] + whole[2:4] + whole[4:6]
     out = jnp.concatenate([both[0:1], both[1:2]], 1)
     out_ref[...] = jnp.broadcast_to(out[None], out_ref.shape)
 
@@ -554,9 +561,7 @@
         crossing = []
         for shift in range(1, splits):
             crossing.append(to_split(near, shift))
-        mixes, gain, *got = ready(
-            dims, tick, sections, (w_gate[0], w_up[0], w_down[0]), head, early, states, shifted
-        )
+        mixes, gain, *got = ready(dims, tick, sections, (w_gate[0], w_up[0], w_down[0]), head, early, states, shifted)
         pack = got.pop(0) if tick < sections - 1 else None
         weights = got[:3]
         if tick == 0:
@@ -585,18 +590,22 @@
     near = exchange(last_rows)
     far = swap_core(near)
     world = sections * members
-    (table,) = call(
-        table_kernel,
-        [((batches * head.shape[0], width), BF16, True)],
-        (head, *first_parts, *late_parts),
-        [HBM] + [ANY] * (2 * batches - 2),
+    table = call(
+        lambda *refs: table_kernel(batches, members * toks, *refs),
+        [
+            ((batches * head.shape[0], width), BF16, True),
+            ((members * toks, members * toks), BF16),
+            ((1, members * toks), jnp.int32),
+        ],
+        (targets, head, *first_parts, *late_parts),
+        [VMEM, HBM] + [ANY] * (2 * batches - 2),
         [pltpu.SemaphoreType.DMA((2 * batches - 1,))],
     )
     (stats,) = call(
         lambda *refs: head_kernel(batches, early, *refs),
         [((world, 1, 2 * members * toks), F32)],
-        (near, far, targets, table),
-        [VMEM] * 4,
+        (near, far, *table),
+        [VMEM] * 5,
         flops=4 * head.size * members * toks,
     )
     stats = lax.all_to_all(stats, ("section", "expert"), split_axis=0, concat_axis=0, tiled=True)

time: 162 us -> 163 us (level)
  no operation moved by 1% of the time
where the time goes in v5:
time: 163 us
  blocking collectives  75.2 us (46%)
  waiting for transfers between devices  56.7 us (35%)
  Pallas kernels  19.1 us (12%)
  starting transfers between devices  9.8 us (6%)
    all_to_all x3, blocking collectives, exchange_all(): lax.all_to_all(rows, ('section', 'expert'), split_axis=0, concat_axis=0,...  48.6 us
    ppermute x3, waiting for transfers between devices, by_section(): lax.ppermute(array, 'section', [(s, s - s % across + (s + shift) % across...  32.5 us
    pallas_call x10, Pallas kernels, call(): pl.pallas_call(kernel, out_shape=tuple((pltpu.VMEM(*out[:2]) if out[2:] e...  19.1 us
    all_to_all x1, blocking collectives, dispatch_first(): lax.all_to_all(rows, 'expert', split_axis=0, concat_axis=0, axis_index_gr...  14.3 us
    all_to_all x1, blocking collectives, body(): lax.all_to_all(stats, ('section', 'expert'), split_axis=0, concat_axis=0,...  12.2 us
    all_to_all x1, waiting for transfers between devices, exchange(): lax.all_to_all(rows, 'expert', split_axis=0, concat_axis=0, axis_index_gr...  10.9 us
    ppermute x2, waiting for transfers between devices, to_split(): return lax.ppermute(rows, 'expert', pairs)  9.95 us
    ppermute x3, starting transfers between devices, by_section(): lax.ppermute(array, 'section', [(s, s - s % across + (s + shift) % across...  3.58 us
  transfers between devices with their start and end apart: 13, of which 8 were waited for; matrix products, arithmetic and copies ran while one was open for 0% of the time, Pallas kernels for 6%

profile of v5, /device:TPU:0, one launch (start us, length us, event | category | flops | bytes accessed | tf_op | source)
XLA Modules:
  0.0 162.6 jit_solution(4904777329492918141)
XLA Ops:
  0.6 1.8 %shard_map.122 = (bf16[32,3584]{1,0:T(8,128)(2,1)S(1)}, f32[8,3712]{1,0:T(8,128)S(1)}, bf16[16,1792]{1,0:T(8,128)(2,1)S(1)}, bf16[160,3584]{1,0:T(8,128)(2,1)S(1)}) custom-call(bf16[2,8,3584]{2,1,0:T(8,128)(2,1)} %refs_0_.2, f32[1,3584]{1,0:T(1,128)} %refs_1_.3, bf16[4,3584]{1,0:T(4,128)(2,1)} %bitcast.39, s32[2,2,8]{2,1,0:T(2,128)} %bitcast.40, ...), custom_call_target="tpu_custom_call" | custom-call | flops 1 | bytes 2007168 | tf_op jit(solution)/shard_map/pallas_call | solution.py:28
  2.4 14.3 %all_to_all.61 = bf16[4,8,3584]{2,1,0:T(8,128)(2,1)S(1)} all-to-all(bf16[4,8,3584]{2,1,0:T(8,128)(2,1)S(1)} %bitcast.32), channel_id=1, replica_groups={{0,4,8,12},{1,5,9,13},{2,6,10,14},{3,7,11,15},{16,20,24,28},{17,21,25,2..., dimensions={0} | all-to-all | bytes 458752 | tf_op jit(solution)/shard_map/all_to_all | solution.py:524
  16.8 1.5 collective-permute-start
  18.3 0.0 collective-permute-start.1
  18.3 4.5 %collective-permute-done.refs_1_ = bf16[32,3584]{1,0:T(8,128)(2,1)S(1)} collective-permute-done((bf16[32,3584]{1,0:T(8,128)(2,1)S(1)}, bf16[32,3584]{1,0:T(8,128)(2,1)S(1)}, u32[]{:S(2)}, u32[]{:S(2)}) %collective-permute-start) | collective-permute-done | bytes 229408 | tf_op jit(solution)/shard_map/ppermute | solution.py:533
  22.8 0.0 collective-permute-start.2
  22.8 1.5 collective-permute-start.3
  24.3 4.2 %collective-permute-done.3.refs_6_ = f32[8,3712]{1,0:T(8,128)S(1)} collective-permute-done((f32[8,3712]{1,0:T(8,128)S(1)}, f32[8,3712]{1,0:T(8,128)S(1)}, u32[]{:S(2)}, u32[]{:S(2)}) %collective-permute-start.3) | collective-permute-done | bytes 118816 | tf_op jit(solution)/shard_map/ppermute | solution.py:539
  28.4 4.4 %shard_map.123 = (bf16[32,64]{1,0:T(8,128)(2,1)S(1)}, f32[2,1792]{1,0:T(2,128)S(1)}, bf16[16,64]{1,0:T(8,128)(2,1)S(1)}, bf16[3584,512]{1,0:T(8,128)(2,1)S(1)}, ...) custom-call(bf16[3584,512]{1,0:T(8,128)(2,1)} %bitcast.33, ...), custom_call_target="tpu_custom_call" | custom-call | flops 1 | bytes 13139968 | tf_op jit(solution)/shard_map/pallas_call | solution.py:28
  32.8 0.0 copy-start.2
  32.8 0.9 copy-done.2
  33.7 0.0 collective-permute-done.1.refs_2_
  33.7 0.0 collective-permute-done.2.refs_3_
  33.7 1.8 %shard_map.124 = (bf16[128,1792]{1,0:T(8,128)(2,1)S(1)}, bf16[128,1792]{1,0:T(8,128)(2,1)S(1)}) custom-call(bf16[32,3584]{1,0:T(8,128)(2,1)S(1)} %bitcast.27, bf16[32,3584]{1,0:T(8,128)(2,1)S(1)} %collective-permute-done.refs_1_, bf16[32,3584]{1,0:T(8,128)(2,1)S(1)} %collective-permute-done.1.refs_2_, bf16[32,3584]{1,0:T(8,128)(2,1)S(1)} %collective-permute-done.2.refs_3_, ...), custom_call_target="tpu_custom_call" | custom-call | flops 1409286144 | bytes 11927552 | tf_op jit(solution)/shard_map/pallas_call | solution.py:28
  35.5 0.1 collective-permute-start.4
  35.6 1.8 %collective-permute-done.4 = bf16[128,1792]{1,0:T(8,128)(2,1)S(1)} collective-permute-done((bf16[128,1792]{1,0:T(8,128)(2,1)S(1)}, bf16[128,1792]{1,0:T(8,128)(2,1)S(1)}, u32[]{:S(2)}, u32[]{:S(2)}) %collective-permute-start.4) | collective-permute-done | bytes 458784 | tf_op jit(solution)/shard_map/ppermute | solution.py:536
  37.4 0.1 fusion
  37.5 19.7 %all_to_all.62 = bf16[16,8,1792]{2,1,0:T(8,128)(2,1)S(1)} all-to-all(bf16[16,8,1792]{2,1,0:T(8,128)(2,1)S(1)} %fusion), channel_id=1, replica_groups={{0,2,4,6,8,10,12,14,16,18,20,22,24,26,28,30},{1,3,5,7,9,11,13,15,17,19,..., dimensions={0} | all-to-all | bytes 917504 | tf_op jit(solution)/shard_map/all_to_all | solution.py:514
  57.2 0.5 shard_map.125
  57.6 11.8 %all_to_all.63 = bf16[8,8,1792]{2,1,0:T(8,128)(2,1)S(1)} all-to-all(bf16[8,8,1792]{2,1,0:T(8,128)(2,1)S(1)} %bitcast.31), channel_id=1, replica_groups={{0,4,8,12,16,20,24,28},{1,5,9,13,17,21,25,29},{2,6,10,14,18,22,26,30},{..., dimensions={0} | all-to-all | bytes 458752 | tf_op jit(solution)/shard_map/all_to_all | solution.py:514
  69.5 0.6 collective-permute-start.5
  70.1 0.0 collective-permute-start.6
  70.1 5.4 %collective-permute-done.5.refs_1_ = bf16[64,1792]{1,0:T(8,128)(2,1)S(1)} collective-permute-done((bf16[64,1792]{1,0:T(8,128)(2,1)S(1)}, bf16[64,1792]{1,0:T(8,128)(2,1)S(1)}, u32[]{:S(2)}, u32[]{:S(2)}) %collective-permute-start.5) | collective-permute-done | bytes 229408 | tf_op jit(solution)/shard_map/ppermute | solution.py:533
  75.5 0.0 collective-permute-start.7
  75.5 4.2 %shard_map.126 = (bf16[32,64]{1,0:T(8,128)(2,1)S(1)}, f32[2,1792]{1,0:T(2,128)S(1)}, bf16[3584,512]{1,0:T(8,128)(2,1)S(1)}, bf16[3584,512]{1,0:T(8,128)(2,1)S(1)}, bf16[512,3584]{1,0:T(8,128)(2,1)S(1)}) custom-call(bf16[3584,512]{1,0:T(8,128)(2,1)} %bitcast.34, bf16[3584,512]{1,0:T(8,128)(2,1)} %bitcast.36, bf16[512,3584]{1,0:T(8,128)(2,1)} %bitcast.38, ...), custom_call_target="tpu_custom_call" | custom-call | flops 1 | bytes 13139968 | tf_op jit(solution)/shard_map/pallas_call | solution.py:28
  79.8 0.0 collective-permute-done.6.refs_2_
  79.8 0.0 collective-permute-done.7.refs_3_
  79.8 1.8 %shard_map.127 = (bf16[128,1792]{1,0:T(8,128)(2,1)S(1)}, bf16[128,1792]{1,0:T(8,128)(2,1)S(1)}) custom-call(bf16[64,1792]{1,0:T(8,128)(2,1)S(1)} %bitcast.30, bf16[64,1792]{1,0:T(8,128)(2,1)S(1)} %collective-permute-done.5.refs_1_, bf16[64,1792]{1,0:T(8,128)(2,1)S(1)} %collective-permute-done.6.refs_2_, bf16[64,1792]{1,0:T(8,128)(2,1)S(1)} %collective-permute-done.7.refs_3_, ...), custom_call_target="tpu_custom_call" | custom-call | flops 1409286144 | bytes 11927552 | tf_op jit(solution)/shard_map/pallas_call | solution.py:28
  81.6 0.0 copy-start.1
  81.6 0.6 collective-permute-start.8
  82.1 1.4 collective-permute-done.8
  83.6 0.1 fusion.1
  83.7 17.1 %all_to_all.64 = bf16[16,8,1792]{2,1,0:T(8,128)(2,1)S(1)} all-to-all(bf16[16,8,1792]{2,1,0:T(8,128)(2,1)S(1)} %fusion.1), channel_id=1, replica_groups={{0,2,4,6,8,10,12,14,16,18,20,22,24,26,28,30},{1,3,5,7,9,11,13,15,17,19,..., dimensions={0} | all-to-all | bytes 917504 | tf_op jit(solution)/shard_map/all_to_all | solution.py:514
  100.8 1.1 shard_map.128
  101.9 3.5 %all-to-all-start.4 = ((bf16[8,8,3584]{2,1,0:T(8,128)(2,1)}), bf16[8,8,3584]{2,1,0:T(8,128)(2,1)S(1)}, u32[]{:S(2)}, u32[]{:S(2)}) async-start(bf16[8,8,3584]{2,1,0:T(8,128)(2,1)} %bitcast.15), calls=%async_computation.4 | async-start | bytes 917504 | tf_op jit(solution)/shard_map/all_to_all | solution.py:509
  105.4 1.4 collective-permute-start.10
  106.8 0.7 collective-permute-start.11
  107.5 10.9 %all-to-all-done.4 = bf16[8,8,3584]{2,1,0:T(8,128)(2,1)S(1)} async-done(((bf16[8,8,3584]{2,1,0:T(8,128)(2,1)}), bf16[8,8,3584]{2,1,0:T(8,128)(2,1)S(1)}, u32[]{:S(2)}, u32[]{:S(2)}) %all-to-all-start.4) | async-done | bytes 458784 | tf_op jit(solution)/shard_map/all_to_all | solution.py:509
  118.4 0.0 collective-permute-start.9
  118.4 15.2 %collective-permute-done.10.refs_2_ = bf16[160,3584]{1,0:T(8,128)(2,1)S(1)} collective-permute-done((bf16[160,3584]{1,0:T(8,128)(2,1)S(1)}, bf16[160,3584]{1,0:T(8,128)(2,1)S(1)}, u32[]{:S(2)}, u32[]{:S(2)}) %collective-permute-start.10) | collective-permute-done | bytes 1146912 | tf_op jit(solution)/shard_map/ppermute | solution.py:539
  133.6 13.2 %collective-permute-done.11.refs_3_ = bf16[96,3584]{1,0:T(8,128)(2,1)S(1)} collective-permute-done((bf16[96,3584]{1,0:T(8,128)(2,1)}, bf16[96,3584]{1,0:T(8,128)(2,1)S(1)}, u32[]{:S(2)}, u32[]{:S(2)}) %collective-permute-start.11) | collective-permute-done | bytes 688160 | tf_op jit(solution)/shard_map/ppermute | solution.py:539
  146.8 0.0 copy-done.1
  146.8 1.5 shard_map.129
  148.3 0.0 collective-permute-done.9.refs_1_
  148.4 1.3 shard_map.130
  149.7 12.2 %all_to_all.65.refs_0_ = f32[32,1,256]{2,1,0:T(1,128)S(1)} all-to-all(f32[32,1,256]{2,1,0:T(1,128)S(1)} %shard_map.130), channel_id=1, replica_groups=mesh['section'=2,'expert'=16] {'section','expert'}, dimensions={0} | all-to-all | bytes 65536 | tf_op jit(solution)/shard_map/all_to_all | solution.py:611
  161.9 0.0 copy-done
  161.9 0.7 shard_map.131
  (1 shorter events, 0.0 us)
Async XLA Ops:
  16.8 6.0 %collective-permute-start = (bf16[32,3584]{1,0:T(8,128)(2,1)S(1)}, bf16[32,3584]{1,0:T(8,128)(2,1)S(1)}, u32[]{:S(2)}, u32[]{:S(2)}) collective-permute-start(bf16[32,3584]{1,0:T(8,128)(2,1)S(1)} %bitcast.25), channel_id=1, source_target_pairs={{0,2},{1,3},{2,0},{3,1},{4,6},{5,7},{6,4},{7,5},{8,10},{9,11},{10,... | collective-permute-start | bytes 688136 | tf_op jit(solution)/shard_map/ppermute | solution.py:533
  18.3 15.4 %collective-permute-start.1 = (bf16[32,3584]{1,0:T(8,128)(2,1)S(1)}, bf16[32,3584]{1,0:T(8,128)(2,1)S(1)}, u32[]{:S(2)}, u32[]{:S(2)}) collective-permute-start(bf16[32,3584]{1,0:T(8,128)(2,1)S(1)} %bitcast.26), channel_id=1, source_target_pairs={{0,1},{1,0},{2,3},{3,2},{4,5},{5,4},{6,7},{7,6},{8,9},{9,8},{10,11... | collective-permute-start | bytes 688136 | tf_op jit(solution)/shard_map/ppermute | solution.py:536
  22.8 10.9 %collective-permute-start.2 = (bf16[32,3584]{1,0:T(8,128)(2,1)S(1)}, bf16[32,3584]{1,0:T(8,128)(2,1)S(1)}, u32[]{:S(2)}, u32[]{:S(2)}) collective-permute-start(bf16[32,3584]{1,0:T(8,128)(2,1)S(1)} %collective-permute-done.refs_1_), channel_id=1, source_target_pairs={{0,1},{1,0},{2,3},{3,2},{4,5},{5,4},{6,7},{7,6},{8,9},{9,8},{10,11... | collective-permute-start | bytes 688136 | tf_op jit(solution)/shard_map/ppermute | solution.py:536
  22.8 5.6 %collective-permute-start.3 = (f32[8,3712]{1,0:T(8,128)S(1)}, f32[8,3712]{1,0:T(8,128)S(1)}, u32[]{:S(2)}, u32[]{:S(2)}) collective-permute-start(f32[8,3712]{1,0:T(8,128)S(1)} %get-tuple-element.31.refs_5_), channel_id=1, source_target_pairs={{0,16},{16,0},{1,17},{17,1},{2,18},{18,2},{3,19},{19,3},{4,20},{20... | collective-permute-start | bytes 356360 | tf_op jit(solution)/shard_map/ppermute | solution.py:539
  32.8 0.9 copy-start.2
  35.5 1.9 %collective-permute-start.4 = (bf16[128,1792]{1,0:T(8,128)(2,1)S(1)}, bf16[128,1792]{1,0:T(8,128)(2,1)S(1)}, u32[]{:S(2)}, u32[]{:S(2)}) collective-permute-start(bf16[128,1792]{1,0:T(8,128)(2,1)S(1)} %get-tuple-element.36), channel_id=1, source_target_pairs={{0,1},{1,0},{2,3},{3,2},{4,5},{5,4},{6,7},{7,6},{8,9},{9,8},{10,11... | collective-permute-start | bytes 1376264 | tf_op jit(solution)/shard_map/ppermute | solution.py:536
  69.5 6.0 %collective-permute-start.5 = (bf16[64,1792]{1,0:T(8,128)(2,1)S(1)}, bf16[64,1792]{1,0:T(8,128)(2,1)S(1)}, u32[]{:S(2)}, u32[]{:S(2)}) collective-permute-start(bf16[64,1792]{1,0:T(8,128)(2,1)S(1)} %bitcast.28), channel_id=1, source_target_pairs={{0,2},{1,3},{2,0},{3,1},{4,6},{5,7},{6,4},{7,5},{8,10},{9,11},{10,... | collective-permute-start | bytes 688136 | tf_op jit(solution)/shard_map/ppermute | solution.py:533
  70.1 9.7 %collective-permute-start.6 = (bf16[64,1792]{1,0:T(8,128)(2,1)S(1)}, bf16[64,1792]{1,0:T(8,128)(2,1)S(1)}, u32[]{:S(2)}, u32[]{:S(2)}) collective-permute-start(bf16[64,1792]{1,0:T(8,128)(2,1)S(1)} %bitcast.29), channel_id=1, source_target_pairs={{0,1},{1,0},{2,3},{3,2},{4,5},{5,4},{6,7},{7,6},{8,9},{9,8},{10,11... | collective-permute-start | bytes 688136 | tf_op jit(solution)/shard_map/ppermute | solution.py:536
  75.5 4.3 %collective-permute-start.7 = (bf16[64,1792]{1,0:T(8,128)(2,1)S(1)}, bf16[64,1792]{1,0:T(8,128)(2,1)S(1)}, u32[]{:S(2)}, u32[]{:S(2)}) collective-permute-start(bf16[64,1792]{1,0:T(8,128)(2,1)S(1)} %collective-permute-done.5.refs_1_), channel_id=1, source_target_pairs={{0,1},{1,0},{2,3},{3,2},{4,5},{5,4},{6,7},{7,6},{8,9},{9,8},{10,11... | collective-permute-start | bytes 688136 | tf_op jit(solution)/shard_map/ppermute | solution.py:536
  81.6 65.2 %copy-start.1 = (s32[2,128]{1,0:T(2,128)S(1)}, s32[2,128]{1,0:T(2,128)}, u32[]{:S(2)}) copy-start(s32[2,128]{1,0:T(2,128)} %refs_0_.3) | copy-start | bytes 3076
  81.6 2.0 %collective-permute-start.8 = (bf16[128,1792]{1,0:T(8,128)(2,1)S(1)}, bf16[128,1792]{1,0:T(8,128)(2,1)S(1)}, u32[]{:S(2)}, u32[]{:S(2)}) collective-permute-start(bf16[128,1792]{1,0:T(8,128)(2,1)S(1)} %get-tuple-element.48), channel_id=1, source_target_pairs={{0,1},{1,0},{2,3},{3,2},{4,5},{5,4},{6,7},{7,6},{8,9},{9,8},{10,11... | collective-permute-start | bytes 1376264 | tf_op jit(solution)/shard_map/ppermute | solution.py:536
  101.9 16.5 %all-to-all-start.4 = ((bf16[8,8,3584]{2,1,0:T(8,128)(2,1)}), bf16[8,8,3584]{2,1,0:T(8,128)(2,1)S(1)}, u32[]{:S(2)}, u32[]{:S(2)}) async-start(bf16[8,8,3584]{2,1,0:T(8,128)(2,1)} %bitcast.15), calls=%async_computation.4 | async-start | bytes 917504 | tf_op jit(solution)/shard_map/all_to_all | solution.py:509
  105.4 28.2 %collective-permute-start.10 = (bf16[160,3584]{1,0:T(8,128)(2,1)S(1)}, bf16[160,3584]{1,0:T(8,128)(2,1)S(1)}, u32[]{:S(2)}, u32[]{:S(2)}) collective-permute-start(bf16[160,3584]{1,0:T(8,128)(2,1)S(1)} %get-tuple-element.51), channel_id=1, source_target_pairs={{0,16},{16,0},{1,17},{17,1},{2,18},{18,2},{3,19},{19,3},{4,20},{20... | collective-permute-start | bytes 3440648 | tf_op jit(solution)/shard_map/ppermute | solution.py:539
  106.8 40.0 %collective-permute-start.11 = (bf16[96,3584]{1,0:T(8,128)(2,1)}, bf16[96,3584]{1,0:T(8,128)(2,1)S(1)}, u32[]{:S(2)}, u32[]{:S(2)}) collective-permute-start(bf16[96,3584]{1,0:T(8,128)(2,1)} %copy-done.2), channel_id=1, source_target_pairs={{0,16},{16,0},{1,17},{17,1},{2,18},{18,2},{3,19},{19,3},{4,20},{20... | collective-permute-start | bytes 2064392 | tf_op jit(solution)/shard_map/ppermute | solution.py:539
  118.4 43.5 %copy-start = (s32[2,128]{1,0:T(2,128)S(1)}, s32[2,128]{1,0:T(2,128)}, u32[]{:S(2)}) copy-start(s32[2,128]{1,0:T(2,128)} %refs_1_.5) | copy-start | bytes 3076
  118.4 29.9 %collective-permute-start.9 = (bf16[64,3584]{1,0:T(8,128)(2,1)S(1)}, bf16[64,3584]{1,0:T(8,128)(2,1)S(1)}, u32[]{:S(2)}, u32[]{:S(2)}) collective-permute-start(bf16[64,3584]{1,0:T(8,128)(2,1)S(1)} %bitcast.21), channel_id=1, source_target_pairs={{0,1},{1,0},{2,3},{3,2},{4,5},{5,4},{6,7},{7,6},{8,9},{9,8},{10,11... | collective-permute-start | bytes 1376264 | tf_op jit(solution)/shard_map/ppermute | solution.py:536
